TPU v7x, 256 devices: a whole 4x4x8 slice. The times are simulated.
256 devices in a mesh: rows: 16 (over z_lo, x), cols: 16 (over y, z_hi, core).
Axes of the slice: x: 4, y: 4, z: 8 (z_hi: 2, z_lo: 4; z = z_hi * 4 + z_lo), core: 2. Of those that a mesh axis runs over, the one named last changes fastest.
Arguments:
- kernel_hat: bfloat16 [2, 256, 512, 4096], P(None, 'rows', 'cols'), may hold values from -0.5 to 0.5
- coefficients: float32 [128, 512], P(None, 'cols'), may hold values from -6 to 6
- wave_speed_sq: float32 [4096, 4096], P('rows', 'cols'), may hold values from 1 to 4
- wet_mask: int32 [4096, 4096], P('rows', 'cols'), may hold values 0 or 1
- boundary_cell: int32 [4096], replicated, may hold values from 0 to 4095, each once
- height: float32 [4096, 4096], P('rows', 'cols'), may hold values from -3 to 3
- flux_x: float32 [4096, 4096], P('rows', 'cols'), may hold values from -3 to 3
- flux_y: float32 [4096, 4096], P('rows', 'cols'), may hold values from -3 to 3
Outputs:
- boundary_series: float32 [128, 4096], P('rows', 'cols')
- height_out: float32 [4096, 4096], P('rows', 'cols')
- flux_x_out: float32 [4096, 4096], P('rows', 'cols')
- flux_y_out: float32 [4096, 4096], P('rows', 'cols')
Inputs may be any that keep to these rules, and one draw needn't show every extreme that they name: `boundary_cell`: each of the 4096 boundary points names a different grid column, so each column is named by exactly one point.
All inputs are finite; a program needn't handle non-finite values. No bound on the sum of `wet_mask` on one device may be relied on, other than what follows from the above.
Results may differ from a plain program's by a relative error of at most 0.0029.
Values sent between devices are 32-bit elements; how exact they have to be, the bound alone decides.
No kernel may reach another device: no remote copies, remote signals or barrier semaphores. Data moves between devices by JAX's collectives and lax.ppermute only.
A program may use at most 64 MiB of HBM per device.

v0:
```python
import math

import jax
import jax.numpy as jnp
from jax import lax
from jax.sharding import PartitionSpec as P

STEP_RATIO = 0.25


def split_up(x, dim, length):
    lengths = x.shape
    tiles = x.reshape(*lengths[:dim], length, lengths[dim] // length, *lengths[dim + 1 :])
    return jnp.moveaxis(tiles, dim, 0)


def summed_on_arrival(x, axis, dim):
    length = lax.axis_size(axis)
    tiles = lax.all_to_all(split_up(x, dim, length), axis, 0, 0, tiled=True)
    return jnp.sum(tiles, axis=0)


def copy_for_each(x, axis):
    copies = jnp.broadcast_to(x, (lax.axis_size(axis), *x.shape))
    return lax.all_to_all(copies, axis, split_axis=0, concat_axis=0, tiled=True)


def joined_along(tiles, dim):
    lengths = list(tiles.shape[1:])
    lengths[dim] *= tiles.shape[0]
    return jnp.moveaxis(tiles, 0, dim).reshape(lengths)


def gathered_copies(x, axis, dim):
    tiles = copy_for_each(x, axis)
    return joined_along(tiles, dim)


def with_halo(cells, sides, width):
    for axis, dim in sides:
        count = lax.axis_size(axis)
        ends = count - 1
        head = lax.slice_in_dim(cells, 0, width, axis=dim)
        tail = lax.slice_in_dim(cells, cells.shape[dim] - width, cells.shape[dim], axis=dim)
        cells = jnp.concatenate(
            [
                lax.ppermute(tail, axis, [(i, (i + 1) % count) for i in range(ends)]),
                cells,
                lax.ppermute(head, axis, [((i + 1) % count, i) for i in range(ends)]),
            ],
            axis=dim,
        )
    return cells


def neighbours(values, along_dim):
    if along_dim == 1:
        return (values[1:-1, :-1], values[1:-1, 1:])
    return (values[:-1, 1:-1], values[1:, 1:-1])


def face_fluxes(surface, along, across, speed_sq, celerity, wet, along_dim):
    left_surf, right_surf = neighbours(surface, along_dim)
    left_along, right_along = neighbours(along, along_dim)
    left_across, right_across = neighbours(across, along_dim)
    left_sq, right_sq = neighbours(speed_sq, along_dim)
    left_speed, right_speed = neighbours(celerity, along_dim)
    left_wet, right_wet = neighbours(wet, along_dim)
    opened = left_wet * right_wet
    damping = 0.25 * (left_speed + right_speed)
    mass_flux = opened * (0.5 * (left_along + right_along) - damping * (right_surf - left_surf))
    momentum = opened * (
        0.5 * (left_sq * left_surf + right_sq * right_surf) - damping * (right_along - left_along)
    )
    shear_flux = opened * (-damping * (right_across - left_across))
    return (mass_flux, momentum, shear_flux)


def advance(surface, along_x, along_y, speed_sq, wet):
    celerity = jnp.sqrt(speed_sq)
    mass_x, momentum_x, shear_x = face_fluxes(surface, along_x, along_y, speed_sq, celerity, wet, 1)
    mass_y, momentum_y, shear_y = face_fluxes(surface, along_y, along_x, speed_sq, celerity, wet, 0)
    interior_wet = wet[1:-1, 1:-1]

    def update(values, flux_cols, flux_rows):
        change = flux_cols[:, 1:] - flux_cols[:, :-1] + (flux_rows[1:] - flux_rows[:-1])
        return interior_wet * (values[1:-1, 1:-1] - STEP_RATIO * change)

    return (
        update(surface, mass_x, mass_y),
        update(along_x, momentum_x, shear_y),
        update(along_y, shear_x, momentum_y),
    )


def set_row(values, position, replacement, flag):
    return values.at[position].set(jnp.where(flag, replacement, values[position]))


def on_device(
    kernel_hat, coefficients, wave_speed_sq, wet_mask, boundary_cell, height, flux_x, flux_y
):
    high = lax.Precision.HIGHEST
    freq_dev = kernel_hat.shape[1]
    steps_total = coefficients.shape[0]
    freq_total = freq_dev * lax.axis_size("rows")
    freqs = lax.axis_index("rows") * freq_dev + jnp.arange(freq_dev, dtype=jnp.int32)
    times = jnp.arange(steps_total, dtype=jnp.int32)
    factor = 2.0 * math.pi / freq_total
    forward = (freqs[:, None] * times[None, :] % freq_total).astype(jnp.float32) * factor
    coef_re = jnp.dot(jnp.cos(forward), coefficients, precision=high).astype(jnp.bfloat16)
    coef_im = (-jnp.dot(jnp.sin(forward), coefficients, precision=high)).astype(jnp.bfloat16)
    form = "fso,fs->fo"
    kern_re = kernel_hat[0]
    kern_im = kernel_hat[1]
    spec_re = jnp.einsum(form, kern_re, coef_re, preferred_element_type=jnp.float32) - jnp.einsum(
        form, kern_im, coef_im, preferred_element_type=jnp.float32
    )
    spec_im = jnp.einsum(form, kern_re, coef_im, preferred_element_type=jnp.float32) + jnp.einsum(
        form, kern_im, coef_re, preferred_element_type=jnp.float32
    )
    inverse = (times[:, None] * freqs[None, :] % freq_total).astype(jnp.float32) * factor
    inv_cos = jnp.cos(inverse) / freq_total
    inv_sin = jnp.sin(inverse) / freq_total
    summed = summed_on_arrival(jnp.stack([spec_re, spec_im]), "cols", 2)
    partial_value = jnp.dot(inv_cos, summed[0], precision=high) - jnp.dot(
        inv_sin, summed[1], precision=high
    )
    series = summed_on_arrival(partial_value, "rows", 0)
    latest = gathered_copies(series[-2:], "cols", 1)
    tile_width = height.shape[1]
    columns = lax.axis_index("cols") * tile_width - 2 + jnp.arange(tile_width + 4, dtype=jnp.int32)
    selector = (boundary_cell[:, None] == columns[None, :]).astype(jnp.float32)
    ghost_wide = jnp.dot(latest, selector, precision=high)
    at_edge = lax.axis_index("rows") == lax.axis_size("rows") - 1
    wet = wet_mask.astype(jnp.float32)
    speed_pad, wet_pad = (
        with_halo(wave_speed_sq, (("rows", 0), ("cols", 1)), 2),
        with_halo(wet, (("rows", 0), ("cols", 1)), 2),
    )
    speed_pad = set_row(speed_pad, -2, 1.0, at_edge)
    wet_pad = set_row(wet_pad, -2, 1.0, at_edge)
    surf_pad, pad_x, pad_y = (
        with_halo(height, (("rows", 0), ("cols", 1)), 2),
        with_halo(flux_x, (("rows", 0), ("cols", 1)), 2),
        with_halo(flux_y, (("rows", 0), ("cols", 1)), 2),
    )
    surf_pad = set_row(surf_pad, -2, ghost_wide[0], at_edge)
    surface, along_x, along_y = advance(surf_pad, pad_x, pad_y, speed_pad, wet_pad)
    surface = set_row(surface, -1, ghost_wide[1, 1:-1], at_edge)
    along_x = set_row(along_x, -1, 0.0, at_edge)
    along_y = set_row(along_y, -1, 0.0, at_edge)
    surface, along_x, along_y = advance(
        surface, along_x, along_y, speed_pad[1:-1, 1:-1], wet_pad[1:-1, 1:-1]
    )
    return (series, surface, along_x, along_y)


def solution(mesh):
    return jax.shard_map(
        on_device,
        mesh=mesh,
        in_specs=(
            P(None, "rows", "cols", None),
            P(None, "cols"),
            P("rows", "cols"),
            P("rows", "cols"),
            P(),
            P("rows", "cols"),
            P("rows", "cols"),
            P("rows", "cols"),
        ),
        out_specs=(P("rows", "cols"), P("rows", "cols"), P("rows", "cols"), P("rows", "cols")),
        check_vma=False,
    )
```

profile of v0, /device:TPU:8, one launch (start us, length us, event | category | flops | bytes accessed | tf_op | source)
XLA Modules:
  0.0 171.1 jit_solution(15571838280219336880)
XLA Ops:
  0.7 0.7 copy-done
  1.4 0.2 fusion.19
  1.6 0.3 fusion.18
  1.9 3.0 %fusion.8 = f32[16,1,4096]{2,1,0:T(1,128)S(1)} fusion(bf16[2,16,32,4096]{3,2,1,0:T(8,128)(2,1)} %param.20, bf16[16,32,1]{1,0,2:T(8,128)(2,1)S(1)} %fusion.18), kind=kOutput, calls=%fused_computation.8 | convolution fusion | flops 4194304 | bytes 4457472 | tf_op jit(solution)/shard_map/fso,fs->fo/dot_general | solution.py:116
  4.9 3.4 %fusion.2 = f32[16,1,4096]{2,1,0:T(1,128)S(1)} fusion(bf16[2,16,32,4096]{3,2,1,0:T(8,128)(2,1)} %param.20, bf16[16,32,1]{1,0,2:T(8,128)(2,1)S(1)} %fusion.18), kind=kOutput, calls=%fused_computation.2 | convolution fusion | flops 4194304 | bytes 4457472 | tf_op jit(solution)/shard_map/fso,fs->fo/dot_general | solution.py:119
  8.2 0.7 fusion.4
  9.0 0.7 fusion.6
  9.6 0.3 bitcast_subtract_fusion
  10.0 0.3 bitcast_add_fusion
  10.4 1.1 copy.13
  11.6 11.6 %all-to-all-start = ((f32[16,2,16,256]{3,2,1,0:T(8,128)}), f32[16,2,16,256]{3,2,1,0:T(8,128)S(1)}, u32[]{:S(2)}, u32[]{:S(2)}) async-start(f32[16,2,16,256]{3,2,1,0:T(8,128)} %copy.13), calls=%async_computation | async-start | bytes 1048576 | tf_op jit(solution)/shard_map/all_to_all | solution.py:19
  23.1 3.4 %collective-permute-start.4 = (f32[2,256]{1,0:T(2,128)S(1)}, f32[2,256]{1,0:T(2,128)S(1)}, u32[]{:S(2)}, u32[]{:S(2)}) collective-permute-start(f32[2,256]{1,0:T(2,128)S(1)} %get-tuple-element.108), channel_id=1, source_target_pairs={{0,16},{16,32},{32,48},{48,64},{64,80},{80,96},{96,112},{112,128},... | collective-permute-start | bytes 6152 | tf_op jit(solution)/shard_map/ppermute | solution.py:47
  26.5 1.3 collective-permute-start.5
  27.9 4.5 %collective-permute-start = (f32[2,256]{1,0:T(2,128)S(1)}, f32[2,256]{1,0:T(2,128)S(1)}, u32[]{:S(2)}, u32[]{:S(2)}) collective-permute-start(f32[2,256]{1,0:T(2,128)S(1)} %get-tuple-element.104), channel_id=1, source_target_pairs={{0,16},{16,32},{32,48},{48,64},{64,80},{80,96},{96,112},{112,128},... | collective-permute-start | bytes 6152 | tf_op jit(solution)/shard_map/ppermute | solution.py:47
  32.4 1.3 collective-permute-start.1
  33.8 4.5 %collective-permute-start.12 = (f32[2,256]{1,0:T(2,128)S(1)}, f32[2,256]{1,0:T(2,128)S(1)}, u32[]{:S(2)}, u32[]{:S(2)}) collective-permute-start(f32[2,256]{1,0:T(2,128)S(1)} %get-tuple-element.102), channel_id=1, source_target_pairs={{0,16},{16,32},{32,48},{48,64},{64,80},{80,96},{96,112},{112,128},... | collective-permute-start | bytes 6152 | tf_op jit(solution)/shard_map/ppermute | solution.py:47
  38.4 1.3 collective-permute-start.13
  39.7 4.5 %collective-permute-start.16 = (f32[2,256]{1,0:T(2,128)S(1)}, f32[2,256]{1,0:T(2,128)S(1)}, u32[]{:S(2)}, u32[]{:S(2)}) collective-permute-start(f32[2,256]{1,0:T(2,128)S(1)} %get-tuple-element.106), channel_id=1, source_target_pairs={{0,16},{16,32},{32,48},{48,64},{64,80},{80,96},{96,112},{112,128},... | collective-permute-start | bytes 6152 | tf_op jit(solution)/shard_map/ppermute | solution.py:47
  44.3 0.8 fusion.123
  45.1 1.3 collective-permute-start.17
  46.4 4.5 %collective-permute-start.8 = (f32[2,256]{1,0:T(2,128)S(1)}, f32[2,256]{1,0:T(2,128)S(1)}, u32[]{:S(2)}, u32[]{:S(2)}) collective-permute-start(f32[2,256]{1,0:T(2,128)S(1)} %get-tuple-element.100), channel_id=1, source_target_pairs={{0,16},{16,32},{32,48},{48,64},{64,80},{80,96},{96,112},{112,128},... | collective-permute-start | bytes 6152 | tf_op jit(solution)/shard_map/ppermute | solution.py:47
  51.1 1.3 collective-permute-start.9
  52.4 1.9 %collective-permute-start.6 = (f32[260,2]{1,0:T(8,128)}, f32[260,2]{1,0:T(8,128)}, u32[]{:S(2)}, u32[]{:S(2)}) collective-permute-start(f32[260,2]{1,0:T(8,128)} %get-tuple-element.98), channel_id=1, source_target_pairs={{0,1},{1,2},{2,3},{3,4},{4,5},{5,6},{6,7},{7,8},{8,9},{9,10},{10,1... | collective-permute-start | bytes 6248 | tf_op jit(solution)/shard_map/ppermute | solution.py:47
  54.3 0.1 fusion.120
  54.4 8.4 %collective-permute-start.7 = (f32[260,2]{1,0:T(8,128)}, f32[260,2]{1,0:T(8,128)}, u32[]{:S(2)}, u32[]{:S(2)}) collective-permute-start(f32[260,2]{1,0:T(8,128)} %get-tuple-element.99), channel_id=1, source_target_pairs={{1,0},{2,1},{3,2},{4,3},{5,4},{6,5},{7,6},{8,7},{9,8},{10,9},{11,1... | collective-permute-start | bytes 6248 | tf_op jit(solution)/shard_map/ppermute | solution.py:49
  62.9 1.9 %collective-permute-start.2 = (f32[260,2]{1,0:T(8,128)S(1)}, f32[260,2]{1,0:T(8,128)S(1)}, u32[]{:S(2)}, u32[]{:S(2)}) collective-permute-start(f32[260,2]{1,0:T(8,128)S(1)} %get-tuple-element.94), channel_id=1, source_target_pairs={{0,1},{1,2},{2,3},{3,4},{4,5},{5,6},{6,7},{7,8},{8,9},{9,10},{10,1... | collective-permute-start | bytes 6248 | tf_op jit(solution)/shard_map/ppermute | solution.py:47
  65.0 8.4 %collective-permute-start.3 = (f32[260,2]{1,0:T(8,128)S(1)}, f32[260,2]{1,0:T(8,128)S(1)}, u32[]{:S(2)}, u32[]{:S(2)}) collective-permute-start(f32[260,2]{1,0:T(8,128)S(1)} %get-tuple-element.95), channel_id=1, source_target_pairs={{1,0},{2,1},{3,2},{4,3},{5,4},{6,5},{7,6},{8,7},{9,8},{10,9},{11,1... | collective-permute-start | bytes 6248 | tf_op jit(solution)/shard_map/ppermute | solution.py:49
  73.4 1.9 %collective-permute-start.14 = (f32[260,2]{1,0:T(8,128)S(1)}, f32[260,2]{1,0:T(8,128)S(1)}, u32[]{:S(2)}, u32[]{:S(2)}) collective-permute-start(f32[260,2]{1,0:T(8,128)S(1)} %get-tuple-element.92), channel_id=1, source_target_pairs={{0,1},{1,2},{2,3},{3,4},{4,5},{5,6},{6,7},{7,8},{8,9},{9,10},{10,1... | collective-permute-start | bytes 6248 | tf_op jit(solution)/shard_map/ppermute | solution.py:47
  75.4 0.8 fusion.119
  76.2 8.4 %collective-permute-start.15 = (f32[260,2]{1,0:T(8,128)S(1)}, f32[260,2]{1,0:T(8,128)S(1)}, u32[]{:S(2)}, u32[]{:S(2)}) collective-permute-start(f32[260,2]{1,0:T(8,128)S(1)} %get-tuple-element.93), channel_id=1, source_target_pairs={{1,0},{2,1},{3,2},{4,3},{5,4},{6,5},{7,6},{8,7},{9,8},{10,9},{11,1... | collective-permute-start | bytes 6248 | tf_op jit(solution)/shard_map/ppermute | solution.py:49
  84.6 1.9 %collective-permute-start.18 = (f32[260,2]{1,0:T(8,128)S(1)}, f32[260,2]{1,0:T(8,128)S(1)}, u32[]{:S(2)}, u32[]{:S(2)}) collective-permute-start(f32[260,2]{1,0:T(8,128)S(1)} %get-tuple-element.96), channel_id=1, source_target_pairs={{0,1},{1,2},{2,3},{3,4},{4,5},{5,6},{6,7},{7,8},{8,9},{9,10},{10,1... | collective-permute-start | bytes 6248 | tf_op jit(solution)/shard_map/ppermute | solution.py:47
  86.6 0.2 pad_maximum_fusion
  86.8 8.4 %collective-permute-start.19 = (f32[260,2]{1,0:T(8,128)S(1)}, f32[260,2]{1,0:T(8,128)S(1)}, u32[]{:S(2)}, u32[]{:S(2)}) collective-permute-start(f32[260,2]{1,0:T(8,128)S(1)} %get-tuple-element.97), channel_id=1, source_target_pairs={{1,0},{2,1},{3,2},{4,3},{5,4},{6,5},{7,6},{8,7},{9,8},{10,9},{11,1... | collective-permute-start | bytes 6248 | tf_op jit(solution)/shard_map/ppermute | solution.py:49
  95.3 1.9 %collective-permute-start.10 = (f32[260,2]{1,0:T(8,128)}, f32[260,2]{1,0:T(8,128)}, u32[]{:S(2)}, u32[]{:S(2)}) collective-permute-start(f32[260,2]{1,0:T(8,128)} %get-tuple-element.90), channel_id=1, source_target_pairs={{0,1},{1,2},{2,3},{3,4},{4,5},{5,6},{6,7},{7,8},{8,9},{9,10},{10,1... | collective-permute-start | bytes 6248 | tf_op jit(solution)/shard_map/ppermute | solution.py:47
  97.2 0.2 pad_maximum_fusion.3
  97.4 8.4 %collective-permute-start.11 = (f32[260,2]{1,0:T(8,128)}, f32[260,2]{1,0:T(8,128)}, u32[]{:S(2)}, u32[]{:S(2)}) collective-permute-start(f32[260,2]{1,0:T(8,128)} %get-tuple-element.91), channel_id=1, source_target_pairs={{1,0},{2,1},{3,2},{4,3},{5,4},{6,5},{7,6},{8,7},{9,8},{10,9},{11,1... | collective-permute-start | bytes 6248 | tf_op jit(solution)/shard_map/ppermute | solution.py:49
  105.9 0.2 pad_maximum_fusion.4
  106.3 0.1 sqrt.6
  106.4 0.9 collective-permute-done.10
  107.2 1.6 collective-permute-done.11
  108.8 1.2 pad_maximum_fusion.2
  110.0 1.2 fusion.29
  111.2 0.5 fusion.77
  111.7 1.1 fusion.16
  112.9 15.4 %all-to-all-start.1 = ((f32[16,8,256]{2,1,0:T(8,128)}), f32[16,8,256]{2,1,0:T(8,128)S(1)}, u32[]{:S(2)}, u32[]{:S(2)}) async-start(f32[16,8,256]{2,1,0:T(8,128)} %fusion.16), calls=%async_computation.1 | async-start | bytes 262144 | tf_op jit(solution)/shard_map/all_to_all | solution.py:19
  128.3 1.4 fusion.35
  129.7 0.2 slice_sqrt_fusion
  129.9 8.3 %all-to-all-done.1 = f32[16,8,256]{2,1,0:T(8,128)S(1)} async-done(((f32[16,8,256]{2,1,0:T(8,128)}), f32[16,8,256]{2,1,0:T(8,128)S(1)}, u32[]{:S(2)}, u32[]{:S(2)}) %all-to-all-start.1) | async-done | bytes 131104 | tf_op jit(solution)/shard_map/all_to_all | solution.py:19
  138.2 0.6 broadcast_in_dim.20
  138.8 8.4 %all-to-all-start.2 = ((f32[16,2,256]{2,1,0:T(2,128)}), f32[16,2,256]{2,1,0:T(2,128)S(1)}, u32[]{:S(2)}, u32[]{:S(2)}) async-start(f32[16,2,256]{2,1,0:T(2,128)} %broadcast_in_dim.20), calls=%async_computation.2 | async-start | bytes 65536 | tf_op jit(solution)/shard_map/all_to_all | solution.py:25
  147.3 1.2 pad_maximum_fusion.1
  148.4 7.4 %all-to-all-done.2 = f32[16,2,256]{2,1,0:T(2,128)S(1)} async-done(((f32[16,2,256]{2,1,0:T(2,128)}), f32[16,2,256]{2,1,0:T(2,128)S(1)}, u32[]{:S(2)}, u32[]{:S(2)}) %all-to-all-start.2) | async-done | bytes 32800 | tf_op jit(solution)/shard_map/all_to_all | solution.py:25
  155.9 2.8 %fusion = f32[2,260]{1,0:T(2,128)S(1)} fusion(f32[2,4096]{1,0:T(2,128)S(1)} %bitcast.48, s32[4096]{0:T(1024)} %param.24, s32[260]{0:T(512)S(1)} %iota_add_fusion), kind=kOutput, calls=%fused_computation | convolution fusion | flops 26624000 | bytes 52272 | tf_op jit(solution)/shard_map/dot_general | solution.py:134
  158.6 0.2 scatter.21
  158.9 1.2 fusion.27
  160.1 0.7 fusion.39
  160.8 0.9 fusion.33
  161.9 0.7 copy-done.2
  162.5 1.3 scatter.26
  163.9 1.6 fusion.58
  165.5 2.8 %fusion.51 = (f32[256,257]{1,0:T(8,128)S(1)}, f32[256,257]{1,0:T(8,128)}) fusion(f32[260,260]{1,0:T(8,128)S(1)} %scatter.24, f32[258,258]{1,0:T(8,128)S(1)} %scatter.25, f32[258,258]{1,0:T(8,128)} %scatter.26, f32[260,260]{1,0:T(8,128)S(1)} %scatter.20, f32[258,258]{1,0:T(8,128)S(1)} %slice_sqrt_fusion), kind=kLoop, calls=%fused_computation.81 | loop fusion | flops 1118464 | bytes 3158016 | tf_op jit(solution)/shard_map/mul | solution.py:72
  168.3 0.5 fusion.47
  168.8 0.8 fusion.56
  169.7 1.5 fusion.63
  (73 shorter events, 1.0 us)
Async XLA Ops:
  0.6 0.7 copy-start
  1.9 6.4 %copy-start.1 = (bf16[2,16,32,4096]{3,2,1,0:T(8,128)(2,1)S(1)}, bf16[2,16,32,4096]{3,2,1,0:T(8,128)(2,1)}, u32[]{:S(2)}) copy-start(bf16[2,16,32,4096]{3,2,1,0:T(8,128)(2,1)} %param.20) | copy-start | bytes 25165828
  8.9 14.2 %copy-start.10 = (f32[256,256]{1,0:T(8,128)S(1)}, f32[256,256]{1,0:T(8,128)}, u32[]{:S(2)}) copy-start(f32[256,256]{1,0:T(8,128)} %param.25) | copy-start | bytes 786436
  8.9 18.9 %copy-start.11 = (s32[256,256]{1,0:T(8,128)S(1)}, s32[256,256]{1,0:T(8,128)}, u32[]{:S(2)}) copy-start(s32[256,256]{1,0:T(8,128)} %param.23) | copy-start | bytes 786436
  8.9 24.8 %copy-start.7 = (f32[256,256]{1,0:T(8,128)S(1)}, f32[256,256]{1,0:T(8,128)}, u32[]{:S(2)}) copy-start(f32[256,256]{1,0:T(8,128)} %param.22) | copy-start | bytes 786436
  8.9 29.4 %copy-start.8 = (f32[256,256]{1,0:T(8,128)S(1)}, f32[256,256]{1,0:T(8,128)}, u32[]{:S(2)}) copy-start(f32[256,256]{1,0:T(8,128)} %param.27) | copy-start | bytes 786436
  9.0 29.4 %copy-start.9 = (f32[256,256]{1,0:T(8,128)S(1)}, f32[256,256]{1,0:T(8,128)}, u32[]{:S(2)}) copy-start(f32[256,256]{1,0:T(8,128)} %param.26) | copy-start | bytes 786436
  11.6 99.6 %all-to-all-start = ((f32[16,2,16,256]{3,2,1,0:T(8,128)}), f32[16,2,16,256]{3,2,1,0:T(8,128)S(1)}, u32[]{:S(2)}, u32[]{:S(2)}) async-start(f32[16,2,16,256]{3,2,1,0:T(8,128)} %copy.13), calls=%async_computation | async-start | bytes 1048576 | tf_op jit(solution)/shard_map/all_to_all | solution.py:19
  23.1 15.3 %collective-permute-start.4 = (f32[2,256]{1,0:T(2,128)S(1)}, f32[2,256]{1,0:T(2,128)S(1)}, u32[]{:S(2)}, u32[]{:S(2)}) collective-permute-start(f32[2,256]{1,0:T(2,128)S(1)} %get-tuple-element.108), channel_id=1, source_target_pairs={{0,16},{16,32},{32,48},{48,64},{64,80},{80,96},{96,112},{112,128},... | collective-permute-start | bytes 6152 | tf_op jit(solution)/shard_map/ppermute | solution.py:47
  26.5 13.2 %collective-permute-start.5 = (f32[2,256]{1,0:T(2,128)S(1)}, f32[2,256]{1,0:T(2,128)S(1)}, u32[]{:S(2)}, u32[]{:S(2)}) collective-permute-start(f32[2,256]{1,0:T(2,128)S(1)} %get-tuple-element.109), channel_id=1, source_target_pairs={{16,0},{32,16},{48,32},{64,48},{80,64},{96,80},{112,96},{128,112},... | collective-permute-start | bytes 6152 | tf_op jit(solution)/shard_map/ppermute | solution.py:49
  27.9 17.2 %collective-permute-start = (f32[2,256]{1,0:T(2,128)S(1)}, f32[2,256]{1,0:T(2,128)S(1)}, u32[]{:S(2)}, u32[]{:S(2)}) collective-permute-start(f32[2,256]{1,0:T(2,128)S(1)} %get-tuple-element.104), channel_id=1, source_target_pairs={{0,16},{16,32},{32,48},{48,64},{64,80},{80,96},{96,112},{112,128},... | collective-permute-start | bytes 6152 | tf_op jit(solution)/shard_map/ppermute | solution.py:47
  32.4 13.9 %collective-permute-start.1 = (f32[2,256]{1,0:T(2,128)S(1)}, f32[2,256]{1,0:T(2,128)S(1)}, u32[]{:S(2)}, u32[]{:S(2)}) collective-permute-start(f32[2,256]{1,0:T(2,128)S(1)} %get-tuple-element.105), channel_id=1, source_target_pairs={{16,0},{32,16},{48,32},{64,48},{80,64},{96,80},{112,96},{128,112},... | collective-permute-start | bytes 6152 | tf_op jit(solution)/shard_map/ppermute | solution.py:49
  33.8 17.3 %collective-permute-start.12 = (f32[2,256]{1,0:T(2,128)S(1)}, f32[2,256]{1,0:T(2,128)S(1)}, u32[]{:S(2)}, u32[]{:S(2)}) collective-permute-start(f32[2,256]{1,0:T(2,128)S(1)} %get-tuple-element.102), channel_id=1, source_target_pairs={{0,16},{16,32},{32,48},{48,64},{64,80},{80,96},{96,112},{112,128},... | collective-permute-start | bytes 6152 | tf_op jit(solution)/shard_map/ppermute | solution.py:47
  38.4 14.0 %collective-permute-start.13 = (f32[2,256]{1,0:T(2,128)S(1)}, f32[2,256]{1,0:T(2,128)S(1)}, u32[]{:S(2)}, u32[]{:S(2)}) collective-permute-start(f32[2,256]{1,0:T(2,128)S(1)} %get-tuple-element.103), channel_id=1, source_target_pairs={{16,0},{32,16},{48,32},{64,48},{80,64},{96,80},{112,96},{128,112},... | collective-permute-start | bytes 6152 | tf_op jit(solution)/shard_map/ppermute | solution.py:49
  39.7 14.7 %collective-permute-start.16 = (f32[2,256]{1,0:T(2,128)S(1)}, f32[2,256]{1,0:T(2,128)S(1)}, u32[]{:S(2)}, u32[]{:S(2)}) collective-permute-start(f32[2,256]{1,0:T(2,128)S(1)} %get-tuple-element.106), channel_id=1, source_target_pairs={{0,16},{16,32},{32,48},{48,64},{64,80},{80,96},{96,112},{112,128},... | collective-permute-start | bytes 6152 | tf_op jit(solution)/shard_map/ppermute | solution.py:47
  45.1 17.8 %collective-permute-start.17 = (f32[2,256]{1,0:T(2,128)S(1)}, f32[2,256]{1,0:T(2,128)S(1)}, u32[]{:S(2)}, u32[]{:S(2)}) collective-permute-start(f32[2,256]{1,0:T(2,128)S(1)} %get-tuple-element.107), channel_id=1, source_target_pairs={{16,0},{32,16},{48,32},{64,48},{80,64},{96,80},{112,96},{128,112},... | collective-permute-start | bytes 6152 | tf_op jit(solution)/shard_map/ppermute | solution.py:49
  46.4 18.6 %collective-permute-start.8 = (f32[2,256]{1,0:T(2,128)S(1)}, f32[2,256]{1,0:T(2,128)S(1)}, u32[]{:S(2)}, u32[]{:S(2)}) collective-permute-start(f32[2,256]{1,0:T(2,128)S(1)} %get-tuple-element.100), channel_id=1, source_target_pairs={{0,16},{16,32},{32,48},{48,64},{64,80},{80,96},{96,112},{112,128},... | collective-permute-start | bytes 6152 | tf_op jit(solution)/shard_map/ppermute | solution.py:47
  51.1 22.4 %collective-permute-start.9 = (f32[2,256]{1,0:T(2,128)S(1)}, f32[2,256]{1,0:T(2,128)S(1)}, u32[]{:S(2)}, u32[]{:S(2)}) collective-permute-start(f32[2,256]{1,0:T(2,128)S(1)} %get-tuple-element.101), channel_id=1, source_target_pairs={{16,0},{32,16},{48,32},{64,48},{80,64},{96,80},{112,96},{128,112},... | collective-permute-start | bytes 6152 | tf_op jit(solution)/shard_map/ppermute | solution.py:49
  52.4 94.9 %collective-permute-start.6 = (f32[260,2]{1,0:T(8,128)}, f32[260,2]{1,0:T(8,128)}, u32[]{:S(2)}, u32[]{:S(2)}) collective-permute-start(f32[260,2]{1,0:T(8,128)} %get-tuple-element.98), channel_id=1, source_target_pairs={{0,1},{1,2},{2,3},{3,4},{4,5},{5,6},{6,7},{7,8},{8,9},{9,10},{10,1... | collective-permute-start | bytes 6248 | tf_op jit(solution)/shard_map/ppermute | solution.py:47
  54.4 92.8 %collective-permute-start.7 = (f32[260,2]{1,0:T(8,128)}, f32[260,2]{1,0:T(8,128)}, u32[]{:S(2)}, u32[]{:S(2)}) collective-permute-start(f32[260,2]{1,0:T(8,128)} %get-tuple-element.99), channel_id=1, source_target_pairs={{1,0},{2,1},{3,2},{4,3},{5,4},{6,5},{7,6},{8,7},{9,8},{10,9},{11,1... | collective-permute-start | bytes 6248 | tf_op jit(solution)/shard_map/ppermute | solution.py:49
  62.9 13.3 %collective-permute-start.2 = (f32[260,2]{1,0:T(8,128)S(1)}, f32[260,2]{1,0:T(8,128)S(1)}, u32[]{:S(2)}, u32[]{:S(2)}) collective-permute-start(f32[260,2]{1,0:T(8,128)S(1)} %get-tuple-element.94), channel_id=1, source_target_pairs={{0,1},{1,2},{2,3},{3,4},{4,5},{5,6},{6,7},{7,8},{8,9},{9,10},{10,1... | collective-permute-start | bytes 6248 | tf_op jit(solution)/shard_map/ppermute | solution.py:47
  65.0 19.6 %collective-permute-start.3 = (f32[260,2]{1,0:T(8,128)S(1)}, f32[260,2]{1,0:T(8,128)S(1)}, u32[]{:S(2)}, u32[]{:S(2)}) collective-permute-start(f32[260,2]{1,0:T(8,128)S(1)} %get-tuple-element.95), channel_id=1, source_target_pairs={{1,0},{2,1},{3,2},{4,3},{5,4},{6,5},{7,6},{8,7},{9,8},{10,9},{11,1... | collective-permute-start | bytes 6248 | tf_op jit(solution)/shard_map/ppermute | solution.py:49
  73.4 13.3 %collective-permute-start.14 = (f32[260,2]{1,0:T(8,128)S(1)}, f32[260,2]{1,0:T(8,128)S(1)}, u32[]{:S(2)}, u32[]{:S(2)}) collective-permute-start(f32[260,2]{1,0:T(8,128)S(1)} %get-tuple-element.92), channel_id=1, source_target_pairs={{0,1},{1,2},{2,3},{3,4},{4,5},{5,6},{6,7},{7,8},{8,9},{9,10},{10,1... | collective-permute-start | bytes 6248 | tf_op jit(solution)/shard_map/ppermute | solution.py:47
  76.2 19.1 %collective-permute-start.15 = (f32[260,2]{1,0:T(8,128)S(1)}, f32[260,2]{1,0:T(8,128)S(1)}, u32[]{:S(2)}, u32[]{:S(2)}) collective-permute-start(f32[260,2]{1,0:T(8,128)S(1)} %get-tuple-element.93), channel_id=1, source_target_pairs={{1,0},{2,1},{3,2},{4,3},{5,4},{6,5},{7,6},{8,7},{9,8},{10,9},{11,1... | collective-permute-start | bytes 6248 | tf_op jit(solution)/shard_map/ppermute | solution.py:49
  84.6 12.8 %collective-permute-start.18 = (f32[260,2]{1,0:T(8,128)S(1)}, f32[260,2]{1,0:T(8,128)S(1)}, u32[]{:S(2)}, u32[]{:S(2)}) collective-permute-start(f32[260,2]{1,0:T(8,128)S(1)} %get-tuple-element.96), channel_id=1, source_target_pairs={{0,1},{1,2},{2,3},{3,4},{4,5},{5,6},{6,7},{7,8},{8,9},{9,10},{10,1... | collective-permute-start | bytes 6248 | tf_op jit(solution)/shard_map/ppermute | solution.py:47
  86.8 19.1 %collective-permute-start.19 = (f32[260,2]{1,0:T(8,128)S(1)}, f32[260,2]{1,0:T(8,128)S(1)}, u32[]{:S(2)}, u32[]{:S(2)}) collective-permute-start(f32[260,2]{1,0:T(8,128)S(1)} %get-tuple-element.97), channel_id=1, source_target_pairs={{1,0},{2,1},{3,2},{4,3},{5,4},{6,5},{7,6},{8,7},{9,8},{10,9},{11,1... | collective-permute-start | bytes 6248 | tf_op jit(solution)/shard_map/ppermute | solution.py:49
  95.3 12.0 %collective-permute-start.10 = (f32[260,2]{1,0:T(8,128)}, f32[260,2]{1,0:T(8,128)}, u32[]{:S(2)}, u32[]{:S(2)}) collective-permute-start(f32[260,2]{1,0:T(8,128)} %get-tuple-element.90), channel_id=1, source_target_pairs={{0,1},{1,2},{2,3},{3,4},{4,5},{5,6},{6,7},{7,8},{8,9},{9,10},{10,1... | collective-permute-start | bytes 6248 | tf_op jit(solution)/shard_map/ppermute | solution.py:47
  97.4 11.3 %collective-permute-start.11 = (f32[260,2]{1,0:T(8,128)}, f32[260,2]{1,0:T(8,128)}, u32[]{:S(2)}, u32[]{:S(2)}) collective-permute-start(f32[260,2]{1,0:T(8,128)} %get-tuple-element.91), channel_id=1, source_target_pairs={{1,0},{2,1},{3,2},{4,3},{5,4},{6,5},{7,6},{8,7},{9,8},{10,9},{11,1... | collective-permute-start | bytes 6248 | tf_op jit(solution)/shard_map/ppermute | solution.py:49
  112.9 25.3 %all-to-all-start.1 = ((f32[16,8,256]{2,1,0:T(8,128)}), f32[16,8,256]{2,1,0:T(8,128)S(1)}, u32[]{:S(2)}, u32[]{:S(2)}) async-start(f32[16,8,256]{2,1,0:T(8,128)} %fusion.16), calls=%async_computation.1 | async-start | bytes 262144 | tf_op jit(solution)/shard_map/all_to_all | solution.py:19
  138.2 22.6 %copy-start.12 = (f32[8,256]{1,0:T(8,128)}, f32[8,256]{1,0:T(8,128)S(1)}, u32[]{:S(2)}) copy-start(f32[8,256]{1,0:T(8,128)S(1)} %reduce_sum.19) | copy-start | bytes 24580
  138.8 17.0 %all-to-all-start.2 = ((f32[16,2,256]{2,1,0:T(2,128)}), f32[16,2,256]{2,1,0:T(2,128)S(1)}, u32[]{:S(2)}, u32[]{:S(2)}) async-start(f32[16,2,256]{2,1,0:T(2,128)} %broadcast_in_dim.20), calls=%async_computation.2 | async-start | bytes 65536 | tf_op jit(solution)/shard_map/all_to_all | solution.py:25
  158.9 1.9 %copy-start.4 = (f32[258,259]{1,0:T(8,128)S(1)}, f32[258,259]{1,0:T(8,128)}, u32[]{:S(2)}) copy-start(f32[258,259]{1,0:T(8,128)} %fusion.29) | copy-start | bytes 801868
  158.9 1.9 %copy-start.5 = (f32[259,258]{1,0:T(8,128)S(1)}, f32[259,258]{1,0:T(8,128)}, u32[]{:S(2)}) copy-start(f32[259,258]{1,0:T(8,128)} %fusion.35) | copy-start | bytes 801868
  161.8 0.7 copy-start.2
  165.5 4.1 %copy-start.3 = (f32[258,258]{1,0:T(8,128)S(1)}, f32[258,258]{1,0:T(8,128)}, u32[]{:S(2)}) copy-start(f32[258,258]{1,0:T(8,128)} %scatter.26) | copy-start | bytes 798772
  168.3 1.4 copy-start.6
where the time goes:
time: 174 us; the launch traced here: 171 us
  starting transfers between devices  115 us (66%)
  waiting for transfers between devices  18.2 us (10%)
  other arithmetic  16.6 us (10%)
  matrix products  12.6 us (7%)
  local copies, waits for them, and re-layouts  7.15 us (4%)
    ppermute x10, starting transfers between devices, with_halo(): lax.ppermute(head, axis, [((i + 1) % count, i) for i in range(ends)])  48.7 us
    ppermute x10, starting transfers between devices, with_halo(): lax.ppermute(tail, axis, [(i, (i + 1) % count) for i in range(ends)])  31.2 us
    all_to_all x2, starting transfers between devices, summed_on_arrival(): tiles = lax.all_to_all(split_up(x, dim, length), axis, 0, 0, tiled=True)  27 us
    all_to_all x1, starting transfers between devices, copy_for_each(): return lax.all_to_all(copies, axis, split_axis=0, concat_axis=0, tiled=True)  8.4 us
    all_to_all x2, waiting for transfers between devices, summed_on_arrival(): tiles = lax.all_to_all(split_up(x, dim, length), axis, 0, 0, tiled=True)  8.27 us
    all_to_all x1, waiting for transfers between devices, copy_for_each(): return lax.all_to_all(copies, axis, split_axis=0, concat_axis=0, tiled=True)  7.43 us
    mul x4, other arithmetic, face_fluxes(): opened * (0.5 * (left_sq * left_surf + right_sq * right_surf) - damping *...  5.47 us
    mul x4, other arithmetic, face_fluxes(): shear_flux = opened * (-damping * (right_across - left_across))  4.8 us
  transfers between devices with their start and end apart: 23, of which 4 were waited for; matrix products, arithmetic and copies ran while one was open for 6% of the time, Pallas kernels for 0%

commit v1 on v0

v1 whole, which is shorter than its diff:
```python
import math

import jax
import jax.numpy as jnp
from jax import lax
from jax.sharding import PartitionSpec as P

STEP_RATIO = 0.25
HIGH = lax.Precision.HIGHEST
SIDE = 16
FREQ_DEV = 16
PAIRS = [(i, i ^ 1) for i in range(SIDE)]
ODD_PAIRS = [(i, i + 1) for i in range(1, SIDE - 1, 2)] + [(i + 1, i) for i in range(1, SIDE - 1, 2)]


def swap(x, axis, bits):
    return lax.ppermute(x, axis, [(i, i ^ bits) for i in range(SIDE)])


def pick(x, index):
    return lax.dynamic_index_in_dim(x, index, 0, keepdims=False)


def neighbours(values, along_dim):
    if along_dim == 1:
        return (values[1:-1, :-1], values[1:-1, 1:])
    return (values[:-1, 1:-1], values[1:, 1:-1])


def face_fluxes(surface, along, across, speed_sq, celerity, wet, along_dim):
    left_surf, right_surf = neighbours(surface, along_dim)
    left_along, right_along = neighbours(along, along_dim)
    left_across, right_across = neighbours(across, along_dim)
    left_sq, right_sq = neighbours(speed_sq, along_dim)
    left_speed, right_speed = neighbours(celerity, along_dim)
    left_wet, right_wet = neighbours(wet, along_dim)
    opened = left_wet * right_wet
    damping = 0.25 * (left_speed + right_speed)
    mass_flux = opened * (0.5 * (left_along + right_along) - damping * (right_surf - left_surf))
    momentum = opened * (
        0.5 * (left_sq * left_surf + right_sq * right_surf) - damping * (right_along - left_along)
    )
    shear_flux = opened * (-damping * (right_across - left_across))
    return (mass_flux, momentum, shear_flux)


def advance(surface, along_x, along_y, speed_sq, wet):
    celerity = jnp.sqrt(speed_sq)
    mass_x, momentum_x, shear_x = face_fluxes(surface, along_x, along_y, speed_sq, celerity, wet, 1)
    mass_y, momentum_y, shear_y = face_fluxes(surface, along_y, along_x, speed_sq, celerity, wet, 0)
    interior_wet = wet[1:-1, 1:-1]

    def update(values, flux_cols, flux_rows):
        change = flux_cols[:, 1:] - flux_cols[:, :-1] + (flux_rows[1:] - flux_rows[:-1])
        return interior_wet * (values[1:-1, 1:-1] - STEP_RATIO * change)

    return (
        update(surface, mass_x, mass_y),
        update(along_x, momentum_x, shear_y),
        update(along_y, shear_x, momentum_y),
    )


def spectrum(kernel_hat, coefficients, freqs, times, freq_total):
    factor = 2.0 * math.pi / freq_total
    forward = (freqs[:, None] * times[None, :] % freq_total).astype(jnp.float32) * factor
    coef_re = jnp.dot(jnp.cos(forward), coefficients, precision=HIGH).astype(jnp.bfloat16)
    coef_im = (-jnp.dot(jnp.sin(forward), coefficients, precision=HIGH)).astype(jnp.bfloat16)
    form = "fso,fs->fo"
    kern_re, kern_im = kernel_hat[0], kernel_hat[1]
    spec_re = jnp.einsum(form, kern_re, coef_re, preferred_element_type=jnp.float32) - jnp.einsum(
        form, kern_im, coef_im, preferred_element_type=jnp.float32
    )
    spec_im = jnp.einsum(form, kern_re, coef_im, preferred_element_type=jnp.float32) + jnp.einsum(
        form, kern_im, coef_re, preferred_element_type=jnp.float32
    )
    return jnp.concatenate([spec_re, spec_im], axis=0)


def ghost_tiles(part, table, boundary_cell):
    last = jnp.dot(table[-2:], part, precision=HIGH)
    high_of = boundary_cell // 128
    low_of = boundary_cell % 128
    in_high = (high_of[None, :] == jnp.arange(32, dtype=jnp.int32)[:, None]).astype(jnp.float32)
    in_low = (low_of[None, :] == jnp.arange(128, dtype=jnp.int32)[:, None]).astype(jnp.float32)
    spread = (last[:, None, :] * in_high[None]).reshape(64, -1)
    placed = lax.dot_general(spread, in_low, (((1,), (1,)), ((), ())), precision=HIGH)
    first, second = placed[:32], placed[32:]
    nothing = jnp.zeros((1, 128), jnp.float32)
    before = jnp.concatenate([nothing, first[1:-1:2]], axis=0)
    after = jnp.concatenate([first[2::2], nothing], axis=0)
    return jnp.concatenate(
        [
            first.reshape(SIDE, 2, 128),
            second.reshape(SIDE, 2, 128),
            before[:, None],
            after[:, None],
            jnp.zeros((SIDE, 2, 128), jnp.float32),
        ],
        axis=1,
    )


def halo_rows(fields, index, axis):
    head, tail = fields[:, :2], fields[:, -2:]
    even = index % 2 == 0
    from_pair = lax.ppermute(jnp.where(even, tail, head), axis, PAIRS)
    from_other = lax.ppermute(jnp.where(even, head, tail), axis, ODD_PAIRS)
    return jnp.where(even, from_other, from_pair), jnp.where(even, from_pair, from_other)


def on_device(
    kernel_hat, coefficients, wave_speed_sq, wet_mask, boundary_cell, height, flux_x, flux_y
):
    row = lax.axis_index("rows")
    col = lax.axis_index("cols")
    core, z_hi, y = col % 2, (col // 2) % 2, col // 4
    freq_dev = kernel_hat.shape[1]
    steps_total = coefficients.shape[0]
    freq_total = freq_dev * SIDE
    freqs = row * freq_dev + jnp.arange(freq_dev, dtype=jnp.int32)
    times = jnp.arange(steps_total, dtype=jnp.int32)
    part = spectrum(kernel_hat, coefficients, freqs, times, freq_total)
    inverse = (times[:, None] * freqs[None, :] % freq_total).astype(jnp.float32) * (
        2.0 * math.pi / freq_total
    )
    table = jnp.concatenate([jnp.cos(inverse), -jnp.sin(inverse)], axis=1) / freq_total
    ghosts = ghost_tiles(part, table, boundary_cell)
    slots = part.reshape(32, SIDE, 2, 128).transpose(1, 2, 0, 3).reshape(SIDE, 64, 128)
    slots = jnp.concatenate([slots, ghosts], axis=1).reshape(8, 2, 72, 128)

    fields = jnp.stack([height, flux_x, flux_y, wave_speed_sq, wet_mask.astype(jnp.float32)])
    above, below = halo_rows(fields, row, "rows")
    tall = jnp.concatenate([above, fields, below], axis=1)
    left, right = halo_rows(jnp.swapaxes(jnp.concatenate([tall[:, :, :2], tall[:, :, -2:]], axis=2), 1, 2), col, "cols")
    padded = jnp.concatenate([jnp.swapaxes(left, 1, 2), tall, jnp.swapaxes(right, 1, 2)], axis=2)

    mine = lax.dynamic_index_in_dim(slots, core, 1, keepdims=False)
    other = lax.dynamic_index_in_dim(slots, 1 - core, 1, keepdims=False)
    block = (mine + swap(other, "cols", 1)).reshape(4, 2, 72, 128)
    got = [swap(pick(block, y ^ bits), "cols", 4 * bits) for bits in (1, 3, 2)]
    block = pick(block, y) + got[0] + got[1] + got[2]
    block = pick(block, z_hi) + swap(pick(block, 1 - z_hi), "cols", 2)

    spec = jnp.concatenate([block[:32], block[32:64]], axis=1)
    partial_value = jnp.dot(table, spec, precision=HIGH).reshape(SIDE, 8, 256)
    ghost = jnp.broadcast_to(block[64:][None], (SIDE, 8, 128))
    sent = jnp.concatenate([partial_value, ghost], axis=2)
    arrived = jnp.sum(lax.all_to_all(sent, "rows", 0, 0, tiled=True), axis=0)
    series, ghost = arrived[:, :256], arrived[:, 256:]

    surface, along_x, along_y, speed, wet = padded
    one = advance(surface, along_x, along_y, speed, wet)
    two = advance(*one, speed[1:-1, 1:-1], wet[1:-1, 1:-1])

    at_edge = row == SIDE - 1
    first = jnp.concatenate(
        [jnp.zeros((1, 1)), ghost[4:5, 127:], ghost[0:1], ghost[1:2], ghost[5:6, :1], jnp.zeros((1, 1))], axis=1
    )
    second = jnp.concatenate([ghost[4:5, 127:], ghost[2:3], ghost[3:4], ghost[5:6, :1]], axis=1)
    low = [x[-14:] for x in padded]
    ones = jnp.ones((1, 260), jnp.float32)
    last = jnp.zeros((1, 260), jnp.float32)
    edge = [
        jnp.concatenate([x[:-2], fill, last], axis=0) for x, fill in zip(low, (first, last, last, ones, ones))
    ]
    a, b, c = advance(*edge)
    a = jnp.concatenate([a[:-1], second], axis=0)
    b = jnp.concatenate([b[:-1], last[:, 2:]], axis=0)
    c = jnp.concatenate([c[:-1], last[:, 2:]], axis=0)
    edge = advance(a, b, c, edge[3][1:-1, 1:-1], edge[4][1:-1, 1:-1])
    result = [
        jnp.concatenate([x[:-8], jnp.where(at_edge, e[-8:], x[-8:])], axis=0) for x, e in zip(two, edge)
    ]
    return (series, *result)


def solution(mesh):
    return jax.shard_map(
        on_device,
        mesh=mesh,
        in_specs=(
            P(None, "rows", "cols", None),
            P(None, "cols"),
            P("rows", "cols"),
            P("rows", "cols"),
            P(),
            P("rows", "cols"),
            P("rows", "cols"),
            P("rows", "cols"),
        ),
        out_specs=(P("rows", "cols"), P("rows", "cols"), P("rows", "cols"), P("rows", "cols")),
        check_vma=False,
    )
```

time: 174 us -> 93.2 us (0.54); the launches traced: 171 us -> 92.5 us
  starting transfers between devices: 115 us -> 28.3 us
  local copies, waits for them, and re-layouts: 7.15 us -> 14.3 us
  other arithmetic: 16.6 us -> 23.2 us
  waiting for transfers between devices: 18.2 us -> 15.1 us
  matrix products: 12.6 us -> 10.3 us
    ppermute x20 -> x9, starting transfers between devices: 79.9 us -> 23 us  [the longest x5 8.69 us: swap(): return lax.ppermute(x, axis, [(i, i ^ bits) for i in range(SIDE)])]
    all_to_all x3 -> x1, starting transfers between devices: 35.4 us -> 5.32 us  [on_device(): arrived = jnp.sum(lax.all_to_all(sent, 'rows', 0, 0, tiled=True), axis=0)]
    all_to_all x3 -> x1, waiting for transfers between devices: 15.7 us -> 7.99 us  [on_device(): arrived = jnp.sum(lax.all_to_all(sent, 'rows', 0, 0, tiled=True), axis=0)]
    ppermute x20 -> x9, waiting for transfers between devices: 2.45 us -> 7.08 us  [the longest x5 7.07 us: swap(): return lax.ppermute(x, axis, [(i, i ^ bits) for i in range(SIDE)])]
    unnamed x28 -> x46, local copies, waits for them, and re-layouts: 1.6 us -> 5.39 us
    dot_general x9, matrix products: 12.6 us -> 10.3 us  [the longest x1 3.35 us: spectrum(): jnp.einsum(form, kern_re, coef_im, preferred_element_type=jnp.float32)]
    concatenate x0 -> x6, local copies, waits for them, and re-layouts: none -> 1.75 us  [the longest x1 1.39 us: on_device(): jnp.concatenate([jnp.zeros((1, 1)), ghost[4:5, 127:], ghost[0:1], ghost[1...]
    mul x4 -> x7, other arithmetic: 4.8 us -> 3.77 us  [face_fluxes(): shear_flux = opened * (-damping * (right_across - left_across))]
  transfers between devices with their start and end apart: 23 -> 10, of which waited for: 4 -> 4; matrix products, arithmetic and copies ran while one was open for 6% -> 30% of each run, Pallas kernels for 0% -> 0%
where the time goes in v1:
time: 93.2 us; the launch traced here: 92.5 us
  starting transfers between devices  28.3 us (30%)
  other arithmetic  23.2 us (25%)
  waiting for transfers between devices  15.1 us (16%)
  local copies, waits for them, and re-layouts  14.3 us (15%)
  matrix products  10.3 us (11%)
  between operations  1.38 us (1%)
    ppermute x5, starting transfers between devices, swap(): return lax.ppermute(x, axis, [(i, i ^ bits) for i in range(SIDE)])  8.69 us
    ppermute x2, starting transfers between devices, halo_rows(): from_other = lax.ppermute(jnp.where(even, head, tail), axis, ODD_PAIRS)  8.53 us
    all_to_all x1, waiting for transfers between devices, on_device(): arrived = jnp.sum(lax.all_to_all(sent, 'rows', 0, 0, tiled=True), axis=0)  7.99 us
    ppermute x5, waiting for transfers between devices, swap(): return lax.ppermute(x, axis, [(i, i ^ bits) for i in range(SIDE)])  7.07 us
    mul x8, other arithmetic, face_fluxes(): opened * (0.5 * (left_sq * left_surf + right_sq * right_surf) - damping *...  6.33 us
    ppermute x2, starting transfers between devices, halo_rows(): from_pair = lax.ppermute(jnp.where(even, tail, head), axis, PAIRS)  5.74 us
    unnamed x46, local copies, waits for them, and re-layouts  5.39 us
    all_to_all x1, starting transfers between devices, on_device(): arrived = jnp.sum(lax.all_to_all(sent, 'rows', 0, 0, tiled=True), axis=0)  5.32 us
  transfers between devices with their start and end apart: 10, of which 4 were waited for; matrix products, arithmetic and copies ran while one was open for 30% of the time, Pallas kernels for 0%

profile of v1, /device:TPU:8, one launch (start us, length us, event | category | flops | bytes accessed | tf_op | source)
XLA Modules:
  0.0 92.5 jit_solution(4020049884473788237)
XLA Ops:
  0.7 1.0 %bitcast_dynamic-update-slice_fusion.4 = f32[5,256,256]{2,1,0:T(8,128)S(1)} fusion(f32[256,256]{1,0:T(8,128)} %param.13), kind=kLoop, calls=%fused_computation.135 | loop fusion | bytes 524288
  1.7 1.0 %bitcast_dynamic-update-slice_fusion.3 = f32[5,256,256]{2,1,0:T(8,128)S(1)} fusion(f32[5,256,256]{2,1,0:T(8,128)S(1)} %bitcast_dynamic-update-slice_fusion.4, f32[256,256]{1,0:T(8,128)} %param.14), kind=kLoop, calls=%fused_computation.134 | loop fusion | bytes 524288
  2.7 1.0 %bitcast_dynamic-update-slice_fusion.2 = f32[5,256,256]{2,1,0:T(8,128)S(1)} fusion(f32[5,256,256]{2,1,0:T(8,128)S(1)} %bitcast_dynamic-update-slice_fusion.3, f32[256,256]{1,0:T(8,128)} %param.15), kind=kLoop, calls=%fused_computation.133 | loop fusion | bytes 524288
  3.6 1.0 %bitcast_dynamic-update-slice_fusion.1 = f32[5,256,256]{2,1,0:T(8,128)S(1)} fusion(f32[5,256,256]{2,1,0:T(8,128)S(1)} %bitcast_dynamic-update-slice_fusion.2, f32[256,256]{1,0:T(8,128)} %param.10), kind=kLoop, calls=%fused_computation.132 | loop fusion | bytes 524288
  4.7 0.7 collective-permute-start.5
  5.3 4.3 %collective-permute-start.6 = (f32[5,2,256]{2,1,0:T(2,128)S(1)}, f32[5,2,256]{2,1,0:T(2,128)S(1)}, u32[]{:S(2)}, u32[]{:S(2)}) collective-permute-start(f32[5,2,256]{2,1,0:T(2,128)S(1)} %get-tuple-element.35), channel_id=1, source_target_pairs={{0,16},{16,0},{32,48},{48,32},{64,80},{80,64},{96,112},{112,96},{1... | collective-permute-start | bytes 30728 | tf_op jit(solution)/shard_map/ppermute | solution.py:107
  10.2 3.0 %fusion.2 = f32[16,1,4096]{2,1,0:T(1,128)S(1)} fusion(bf16[2,16,32,4096]{3,2,1,0:T(8,128)(2,1)} %param.8, bf16[16,32,1]{1,0,2:T(8,128)(2,1)S(1)} %fusion.15), kind=kOutput, calls=%fused_computation.2 | convolution fusion | flops 4194304 | bytes 4457472 | tf_op jit(solution)/shard_map/fso,fs->fo/dot_general | solution.py:71
  13.2 3.3 %fusion.4 = f32[16,1,4096]{2,1,0:T(1,128)S(1)} fusion(bf16[2,16,32,4096]{3,2,1,0:T(8,128)(2,1)} %param.8, bf16[16,32,1]{1,0,2:T(8,128)(2,1)S(1)} %fusion.15), kind=kOutput, calls=%fused_computation.4 | convolution fusion | flops 4194304 | bytes 4457472 | tf_op jit(solution)/shard_map/fso,fs->fo/dot_general | solution.py:74
  16.5 0.7 fusion
  17.2 0.7 fusion.6
  18.0 0.6 copy-done.10
  18.6 0.6 bitcast_add_fusion.1
  19.3 0.5 fusion.115
  19.9 1.3 %fusion.12 = f32[64,128]{1,0:T(8,128)S(1)} fusion(f32[64,4096]{1,0:T(8,128)S(1)} %bitcast.100, s32[4096]{0:T(1024)S(1)} %get-tuple-element.79), kind=kOutput, calls=%fused_computation.13 | convolution fusion | flops 403177472 | bytes 1097728 | tf_op jit(solution)/shard_map/dot_general | solution.py:87
  21.3 0.4 reshape.79
  21.8 0.3 copy.45
  23.3 0.3 copy.48
  23.6 7.9 %collective-permute-start.7 = (f32[5,2,260]{2,1,0:T(2,128)S(1)}, f32[5,2,260]{2,1,0:T(2,128)S(1)}, u32[]{:S(2)}, u32[]{:S(2)}) collective-permute-start(f32[5,2,260]{2,1,0:T(2,128)S(1)} %copy.48), channel_id=1, source_target_pairs={{1,2},{3,4},{5,6},{7,8},{9,10},{11,12},{13,14},{2,1},{4,3},{6,5},{... | collective-permute-start | bytes 31208 | tf_op jit(solution)/shard_map/ppermute | solution.py:108
  31.4 0.3 copy.49
  31.8 1.4 %collective-permute-start.8 = (f32[5,2,260]{2,1,0:T(2,128)S(1)}, f32[5,2,260]{2,1,0:T(2,128)S(1)}, u32[]{:S(2)}, u32[]{:S(2)}) collective-permute-start(f32[5,2,260]{2,1,0:T(2,128)S(1)} %copy.49), channel_id=1, source_target_pairs={{0,1},{1,0},{2,3},{3,2},{4,5},{5,4},{6,7},{7,6},{8,9},{9,8},{10,11... | collective-permute-start | bytes 31208 | tf_op jit(solution)/shard_map/ppermute | solution.py:107
  33.2 0.7 dynamic-slice_bitcast_fusion
  34.1 0.6 slice.997
  34.7 0.6 slice.996
  35.6 1.2 %copy.51 = f32[5,2,260]{1,2,0:T(8,128)} copy(f32[5,2,260]{2,1,0:T(2,128)S(1)} %collective-permute-done.8) | data formatting | bytes 20800 | tf_op jit(solution)/shard_map/ppermute | solution.py:107
  36.8 1.2 %select_bitcast_fusion.1 = (f32[5,260,2]{2,1,0:T(8,128)S(1)}, f32[5,260,2]{2,1,0:T(8,128)S(1)}) fusion(f32[5,2,260]{1,2,0:T(8,128)S(1)} %copy.50, f32[5,2,260]{1,2,0:T(8,128)} %copy.51, pred[]{:T(512)S(6)} %eq.56), kind=kLoop, calls=%fused_computation.25 | loop fusion | flops 5200 | bytes 41601 | tf_op jit(solution)/shard_map/transpose | solution.py:136
  38.0 0.8 pad_maximum_fusion
  39.1 0.4 fusion.27
  39.5 1.2 %fusion.25 = (f32[259,258]{1,0:T(8,128)S(1)}, f32[259,258]{1,0:T(8,128)S(1)}) fusion(f32[260,260]{1,0:T(8,128)S(1)} %get-tuple-element.17, f32[260,260]{1,0:T(8,128)S(1)} %get-tuple-element.20, f32[260,260]{1,0:T(8,128)S(1)} %get-tuple-element.18, f32[260,260]{1,0:T(8,128)S(1)} %get-tuple-element.21, f32[260,260]{1,0:T(8,128)S(1)} %fusion.158), kind=kLoop, calls=%fused_computation.41 | loop fusion | flops 1135974 | bytes 3207456 | tf_op jit(solution)/shard_map/mul | solution.py:40
  40.7 0.7 fusion.37
  41.4 0.7 fusion.33
  42.1 1.0 %fusion.31 = (f32[258,258]{1,0:T(8,128)S(1)}, f32[258,258]{1,0:T(8,128)S(1)}, f32[258,258]{1,0:T(8,128)S(1)}, f32[258,258]{1,0:T(8,128)S(1)}) fusion(f32[259,258]{1,0:T(8,128)S(1)} %fusion.33, f32[258,259]{1,0:T(8,128)S(1)} %get-tuple-element.26, f32[260,260]{1,0:T(8,128)S(1)} %get-tuple-element.19, f32[260,260]{1,0:T(8,128)S(1)} %get-tuple-element.21, ...), kind=kLoop, calls=%fused_computation.52 | loop fusion | flops 1198152 | bytes 5591376 | tf_op jit(solution)/shard_map/mul | solution.py:55
  43.1 0.5 fusion.56
  43.7 0.8 fusion.49
  44.5 0.5 fusion.45
  45.0 0.8 fusion.54
  45.8 0.6 fusion.61
  46.4 0.5 copy-done.3
  46.9 1.0 %bitcast_add_fusion = f32[8,72,128]{2,1,0:T(8,128)S(1)} fusion(f32[8,72,128]{2,1,0:T(8,128)} %collective-permute-done, f32[8,2,72,128]{3,2,1,0:T(8,128)S(1)} %copy-done.3, s32[]{:T(128)S(6)} %select_n.135), kind=kLoop, calls=%fused_computation.95 | loop fusion | flops 73728 | bytes 884740 | tf_op jit(solution)/shard_map/add | solution.py:140
  47.9 0.5 collective-permute-start.1
  48.5 2.4 %collective-permute-start.2 = (f32[2,72,128]{2,1,0:T(8,128)S(1)}, f32[2,72,128]{2,1,0:T(8,128)S(1)}, u32[]{:S(2)}, u32[]{:S(2)}) collective-permute-start(f32[2,72,128]{2,1,0:T(8,128)S(1)} %get-tuple-element.46), channel_id=1, source_target_pairs={{0,12},{1,13},{2,14},{3,15},{4,8},{5,9},{6,10},{7,11},{8,4},{9,5},... | collective-permute-start | bytes 221192 | tf_op jit(solution)/shard_map/ppermute | solution.py:17
  50.9 1.2 %collective-permute-start.3 = (f32[2,72,128]{2,1,0:T(8,128)S(1)}, f32[2,72,128]{2,1,0:T(8,128)S(1)}, u32[]{:S(2)}, u32[]{:S(2)}) collective-permute-start(f32[2,72,128]{2,1,0:T(8,128)S(1)} %get-tuple-element.45), channel_id=1, source_target_pairs={{0,8},{1,9},{2,10},{3,11},{4,12},{5,13},{6,14},{7,15},{8,0},{9,1},... | collective-permute-start | bytes 221192 | tf_op jit(solution)/shard_map/ppermute | solution.py:17
  52.1 0.7 maximum_bitcast_fusion.4
  52.9 0.7 collective-permute-done.2
  53.5 3.2 %collective-permute-done.3 = f32[2,72,128]{2,1,0:T(8,128)S(1)} collective-permute-done((f32[2,72,128]{2,1,0:T(8,128)S(1)}, f32[2,72,128]{2,1,0:T(8,128)S(1)}, u32[]{:S(2)}, u32[]{:S(2)}) %collective-permute-start.3) | collective-permute-done | bytes 73760 | tf_op jit(solution)/shard_map/ppermute | solution.py:17
  56.8 4.5 %collective-permute-start.4 = (f32[72,128]{1,0:T(8,128)S(1)}, f32[72,128]{1,0:T(8,128)S(1)}, u32[]{:S(2)}, u32[]{:S(2)}) collective-permute-start(f32[72,128]{1,0:T(8,128)S(1)} %dynamic-slice_bitcast_fusion.4), channel_id=1, source_target_pairs={{0,2},{1,3},{2,0},{3,1},{4,6},{5,7},{6,4},{7,5},{8,10},{9,11},{10,... | collective-permute-start | bytes 110600 | tf_op jit(solution)/shard_map/ppermute | solution.py:17
  61.3 0.7 fusion.160
  62.0 3.2 %collective-permute-done.4 = f32[72,128]{1,0:T(8,128)S(1)} collective-permute-done((f32[72,128]{1,0:T(8,128)S(1)}, f32[72,128]{1,0:T(8,128)S(1)}, u32[]{:S(2)}, u32[]{:S(2)}) %collective-permute-start.4) | collective-permute-done | bytes 36896 | tf_op jit(solution)/shard_map/ppermute | solution.py:17
  65.2 0.3 convolution_bitcast_fusion
  65.5 0.7 pad_maximum_fusion.6
  66.2 5.3 %all-to-all-start = ((f32[16,8,384]{2,1,0:T(8,128)}), f32[16,8,384]{2,1,0:T(8,128)}, u32[]{:S(2)}, u32[]{:S(2)}) async-start(f32[16,8,384]{2,1,0:T(8,128)} %pad_maximum_fusion.6), calls=%async_computation | async-start | bytes 393216 | tf_op jit(solution)/shard_map/all_to_all | solution.py:149
  71.5 0.8 maximum_bitcast_fusion.5
  72.6 0.3 copy-done.6
  73.0 8.0 %all-to-all-done = f32[16,8,384]{2,1,0:T(8,128)} async-done(((f32[16,8,384]{2,1,0:T(8,128)}), f32[16,8,384]{2,1,0:T(8,128)}, u32[]{:S(2)}, u32[]{:S(2)}) %all-to-all-start) | async-done | bytes 196640 | tf_op jit(solution)/shard_map/all_to_all | solution.py:149
  81.0 0.9 %reduce_sum.9 = f32[8,384]{1,0:T(8,128)S(1)} reduce(f32[16,8,384]{2,1,0:T(8,128)} %all-to-all-done, f32[]{:T(128)} %constant.162.clone.1), dimensions={0}, to_apply=%region_0.1 | reduce | flops 46080 | bytes 208900 | tf_op jit(solution)/shard_map/reduce_sum | solution.py:149
  82.0 0.6 fusion.171
  82.6 1.4 %concatenate.114 = f32[1,260]{1,0:T(1,128)S(1)} concatenate(f32[1,1]{1,0:T(1,128)} %constant.170.clone.1, f32[1,1]{1,0:T(1,128)} %get-tuple-element.86, f32[1,128]{1,0:T(1,128)S(1)} %get-tuple-element.84, f32[1,128]{1,0:T(1,128)S(1)} %get-tuple-element.83, f32[1,1]{1,0:T(1,128)} %get-tuple-element.85, f32[1,1]{1,0:T(1,128)} %constant.170.clone.1), dimensions={1} | concatenate | bytes 2080 | tf_op jit(solution)/shard_map/concatenate | solution.py:157
  84.0 1.1 %subtract_multiply_fusion.5 = (f32[12,259]{1,0:T(8,128)S(1)}, f32[12,259]{1,0:T(8,128)S(1)}, f32[12,259]{1,0:T(8,128)S(1)}) fusion(f32[12,260]{1,0:T(8,128)S(1)} %get-tuple-element.14, f32[12,260]{1,0:T(8,128)} %copy-done.6, f32[1,260]{1,0:T(1,128)S(1)} %concatenate.114, f32[12,260]{1,0:T(8,128)} %get-tuple-element.12, f32[12,260]{1,0:T(8,128)S(1)} %get-tuple-element.15, ...), kind=kLoop, calls=%fused_computation.211 | loop fusion | flops 83916 | bytes 125600 | tf_op jit(solution)/shard_map/mul | solution.py:40
  85.3 0.9 fusion.98
  86.4 1.4 %fusion.110 = f32[11,256]{1,0:T(8,128)S(1)} fusion(f32[12,260]{1,0:T(8,128)S(1)} %get-tuple-element.14, f32[12,258]{1,0:T(8,128)S(1)} %get-tuple-element.68, f32[12,258]{1,0:T(8,128)S(1)} %get-tuple-element.67, pred[11]{0:T(512)(128)(4,1)S(1)} %slice.1025, f32[1,1]{1,0:T(1,128)} %get-tuple-element.85, f32[1,128]{1,0:T(1,128)S(1)} %get-tuple-element.82, ...), kind=kLoop, calls=%fused_computation.227 | loop fusion | flops 45056 | bytes 201224 | tf_op jit(solution)/shard_map/mul | solution.py:40
  87.8 1.4 %fusion.113 = (f32[11,256]{1,0:T(8,128)S(1)}, f32[11,256]{1,0:T(8,128)S(1)}) fusion(f32[12,258]{1,0:T(8,128)S(1)} %get-tuple-element.66, pred[11]{0:T(512)(128)(4,1)S(1)} %slice.1025, f32[12,258]{1,0:T(8,128)S(1)} %slice_sqrt_fusion.1, f32[12,260]{1,0:T(8,128)S(1)} %get-tuple-element.15, f32[12,258]{1,0:T(8,128)S(1)} %get-tuple-element.68, ...), kind=kLoop, calls=%fused_computation.232 | loop fusion | flops 56320 | bytes 204296 | tf_op jit(solution)/shard_map/mul | solution.py:43
  89.5 0.6 slice.910
  90.3 0.7 pad_maximum_fusion.5
  91.0 0.7 pad_maximum_fusion.4
  91.8 0.7 pad_maximum_fusion.3
  (103 shorter events, 4.1 us)
Async XLA Ops:
  0.6 9.0 %copy-start = (f32[128,32]{0,1:T(8,128)S(1)}, f32[128,32]{0,1:T(8,128)}, u32[]{:S(2)}) copy-start(f32[128,32]{0,1:T(8,128)} %param.9) | copy-start | bytes 49156
  0.6 4.0 %copy-start.7 = (s32[256,256]{1,0:T(8,128)S(1)}, s32[256,256]{1,0:T(8,128)}, u32[]{:S(2)}) copy-start(s32[256,256]{1,0:T(8,128)} %param.11) | copy-start | bytes 786436
  4.7 17.7 %collective-permute-start.5 = (f32[5,2,256]{2,1,0:T(2,128)S(1)}, f32[5,2,256]{2,1,0:T(2,128)S(1)}, u32[]{:S(2)}, u32[]{:S(2)}) collective-permute-start(f32[5,2,256]{2,1,0:T(2,128)S(1)} %get-tuple-element.34), channel_id=1, source_target_pairs={{16,32},{48,64},{80,96},{112,128},{144,160},{176,192},{208,224},{3... | collective-permute-start | bytes 30728 | tf_op jit(solution)/shard_map/ppermute | solution.py:108
  5.3 17.0 %collective-permute-start.6 = (f32[5,2,256]{2,1,0:T(2,128)S(1)}, f32[5,2,256]{2,1,0:T(2,128)S(1)}, u32[]{:S(2)}, u32[]{:S(2)}) collective-permute-start(f32[5,2,256]{2,1,0:T(2,128)S(1)} %get-tuple-element.35), channel_id=1, source_target_pairs={{0,16},{16,0},{32,48},{48,32},{64,80},{80,64},{96,112},{112,96},{1... | collective-permute-start | bytes 30728 | tf_op jit(solution)/shard_map/ppermute | solution.py:107
  10.2 6.4 %copy-start.1 = (bf16[2,16,32,4096]{3,2,1,0:T(8,128)(2,1)S(1)}, bf16[2,16,32,4096]{3,2,1,0:T(8,128)(2,1)}, u32[]{:S(2)}) copy-start(bf16[2,16,32,4096]{3,2,1,0:T(8,128)(2,1)} %param.8) | copy-start | bytes 25165828
  17.9 1.8 %copy-start.12 = (s32[4096]{0:T(1024)S(1)}, s32[4096]{0:T(1024)}, u32[]{:S(2)}) copy-start(s32[4096]{0:T(1024)} %param.12) | copy-start | bytes 49156
  18.0 0.6 copy-start.10
  22.3 10.9 %copy-start.2 = (f32[8,2,72,128]{3,2,1,0:T(8,128)}, f32[8,2,72,128]{3,2,1,0:T(8,128)S(1)}, u32[]{:S(2)}) copy-start(f32[8,2,72,128]{3,2,1,0:T(8,128)S(1)} %concatenate.107) | copy-start | bytes 1769476
  22.4 29.8 %copy-start.8 = (f32[5,2,256]{2,1,0:T(2,128)}, f32[5,2,256]{2,1,0:T(2,128)S(1)}, u32[]{:S(2)}) copy-start(f32[5,2,256]{2,1,0:T(2,128)S(1)} %get-tuple-element.70) | copy-start | bytes 30724
  23.0 12.3 %copy-start.20 = (pred[12]{0:T(512)(128)(4,1)S(1)}, pred[12]{0:T(512)(128)(4,1)}, u32[]{:S(2)}) copy-start(pred[12]{0:T(512)(128)(4,1)} %constant.171.clone.1) | copy-start | bytes 40
  23.6 11.8 %collective-permute-start.7 = (f32[5,2,260]{2,1,0:T(2,128)S(1)}, f32[5,2,260]{2,1,0:T(2,128)S(1)}, u32[]{:S(2)}, u32[]{:S(2)}) collective-permute-start(f32[5,2,260]{2,1,0:T(2,128)S(1)} %copy.48), channel_id=1, source_target_pairs={{1,2},{3,4},{5,6},{7,8},{9,10},{11,12},{13,14},{2,1},{4,3},{6,5},{... | collective-permute-start | bytes 31208 | tf_op jit(solution)/shard_map/ppermute | solution.py:108
  31.8 3.9 %collective-permute-start.8 = (f32[5,2,260]{2,1,0:T(2,128)S(1)}, f32[5,2,260]{2,1,0:T(2,128)S(1)}, u32[]{:S(2)}, u32[]{:S(2)}) collective-permute-start(f32[5,2,260]{2,1,0:T(2,128)S(1)} %copy.49), channel_id=1, source_target_pairs={{0,1},{1,0},{2,3},{3,2},{4,5},{5,4},{6,7},{7,6},{8,9},{9,8},{10,11... | collective-permute-start | bytes 31208 | tf_op jit(solution)/shard_map/ppermute | solution.py:107
  33.9 12.5 %collective-permute-start = (f32[8,72,128]{2,1,0:T(8,128)}, f32[8,72,128]{2,1,0:T(8,128)}, u32[]{:S(2)}, u32[]{:S(2)}) collective-permute-start(f32[8,72,128]{2,1,0:T(8,128)} %dynamic-slice_bitcast_fusion), channel_id=1, source_target_pairs={{0,1},{1,0},{2,3},{3,2},{4,5},{5,4},{6,7},{7,6},{8,9},{9,8},{10,11... | collective-permute-start | bytes 884744 | tf_op jit(solution)/shard_map/ppermute | solution.py:17
  34.0 4.0 %copy-start.16 = (f32[14]{0:T(128)}, f32[14]{0:T(128)S(1)}, u32[]{:S(2)}) copy-start(f32[14]{0:T(128)S(1)} %pad.32.clone) | copy-start | bytes 172
  34.1 3.9 %copy-start.18 = (f32[14]{0:T(128)}, f32[14]{0:T(128)S(1)}, u32[]{:S(2)}) copy-start(f32[14]{0:T(128)S(1)} %pad.33.clone) | copy-start | bytes 172
  45.8 1.1 %copy-start.3 = (f32[8,2,72,128]{3,2,1,0:T(8,128)S(1)}, f32[8,2,72,128]{3,2,1,0:T(8,128)}, u32[]{:S(2)}) copy-start(f32[8,2,72,128]{3,2,1,0:T(8,128)} %copy-done.2) | copy-start | bytes 1769476
  47.9 13.4 %copy-start.17 = (f32[14]{0:T(128)S(1)}, f32[14]{0:T(128)}, u32[]{:S(2)}) copy-start(f32[14]{0:T(128)} %copy-done.16) | copy-start | bytes 172
  47.9 13.4 %copy-start.19 = (f32[14]{0:T(128)S(1)}, f32[14]{0:T(128)}, u32[]{:S(2)}) copy-start(f32[14]{0:T(128)} %copy-done.18) | copy-start | bytes 172
  47.9 17.2 %copy-start.11 = (f32[128,16]{0,1:T(8,128)S(1)}, f32[128,16]{0,1:T(8,128)}, u32[]{:S(2)}) copy-start(f32[128,16]{0,1:T(8,128)} %copy-done.10) | copy-start | bytes 24580
  47.9 4.9 %collective-permute-start.1 = (f32[2,72,128]{2,1,0:T(8,128)S(1)}, f32[2,72,128]{2,1,0:T(8,128)S(1)}, u32[]{:S(2)}, u32[]{:S(2)}) collective-permute-start(f32[2,72,128]{2,1,0:T(8,128)S(1)} %get-tuple-element.44), channel_id=1, source_target_pairs={{0,4},{1,5},{2,6},{3,7},{4,0},{5,1},{6,2},{7,3},{8,12},{9,13},{10,... | collective-permute-start | bytes 221192 | tf_op jit(solution)/shard_map/ppermute | solution.py:17
  48.5 5.0 %collective-permute-start.2 = (f32[2,72,128]{2,1,0:T(8,128)S(1)}, f32[2,72,128]{2,1,0:T(8,128)S(1)}, u32[]{:S(2)}, u32[]{:S(2)}) collective-permute-start(f32[2,72,128]{2,1,0:T(8,128)S(1)} %get-tuple-element.46), channel_id=1, source_target_pairs={{0,12},{1,13},{2,14},{3,15},{4,8},{5,9},{6,10},{7,11},{8,4},{9,5},... | collective-permute-start | bytes 221192 | tf_op jit(solution)/shard_map/ppermute | solution.py:17
  50.9 5.9 %collective-permute-start.3 = (f32[2,72,128]{2,1,0:T(8,128)S(1)}, f32[2,72,128]{2,1,0:T(8,128)S(1)}, u32[]{:S(2)}, u32[]{:S(2)}) collective-permute-start(f32[2,72,128]{2,1,0:T(8,128)S(1)} %get-tuple-element.45), channel_id=1, source_target_pairs={{0,8},{1,9},{2,10},{3,11},{4,12},{5,13},{6,14},{7,15},{8,0},{9,1},... | collective-permute-start | bytes 221192 | tf_op jit(solution)/shard_map/ppermute | solution.py:17
  56.8 8.3 %collective-permute-start.4 = (f32[72,128]{1,0:T(8,128)S(1)}, f32[72,128]{1,0:T(8,128)S(1)}, u32[]{:S(2)}, u32[]{:S(2)}) collective-permute-start(f32[72,128]{1,0:T(8,128)S(1)} %dynamic-slice_bitcast_fusion.4), channel_id=1, source_target_pairs={{0,2},{1,3},{2,0},{3,1},{4,6},{5,7},{6,4},{7,5},{8,10},{9,11},{10,... | collective-permute-start | bytes 110600 | tf_op jit(solution)/shard_map/ppermute | solution.py:17
  66.2 14.8 %all-to-all-start = ((f32[16,8,384]{2,1,0:T(8,128)}), f32[16,8,384]{2,1,0:T(8,128)}, u32[]{:S(2)}, u32[]{:S(2)}) async-start(f32[16,8,384]{2,1,0:T(8,128)} %pad_maximum_fusion.6), calls=%async_computation | async-start | bytes 393216 | tf_op jit(solution)/shard_map/all_to_all | solution.py:149
  71.5 1.4 %copy-start.13 = (f32[13]{0:T(128)S(1)}, f32[13]{0:T(128)}, u32[]{:S(2)}) copy-start(f32[13]{0:T(128)} %slice.997) | copy-start | bytes 160
  71.5 1.4 %copy-start.15 = (f32[13]{0:T(128)S(1)}, f32[13]{0:T(128)}, u32[]{:S(2)}) copy-start(f32[13]{0:T(128)} %slice.996) | copy-start | bytes 160
  72.3 0.6 copy-start.6
  72.3 12.8 %copy-start.4 = (f32[12,260]{1,0:T(8,128)S(1)}, f32[12,260]{1,0:T(8,128)}, u32[]{:S(2)}) copy-start(f32[12,260]{1,0:T(8,128)} %get-tuple-element.12) | copy-start | bytes 37444
  72.3 12.8 %copy-start.5 = (f32[12,260]{1,0:T(8,128)S(1)}, f32[12,260]{1,0:T(8,128)}, u32[]{:S(2)}) copy-start(f32[12,260]{1,0:T(8,128)} %get-tuple-element.13) | copy-start | bytes 37444
  72.3 12.8 %copy-start.9 = (f32[14,260]{1,0:T(8,128)S(1)}, f32[14,260]{1,0:T(8,128)}, u32[]{:S(2)}) copy-start(f32[14,260]{1,0:T(8,128)} %get-tuple-element.11) | copy-start | bytes 43684
  72.3 12.8 %copy-start.14 = (f32[13]{0:T(128)S(1)}, f32[13]{0:T(128)}, u32[]{:S(2)}) copy-start(f32[13]{0:T(128)} %slice.997) | copy-start | bytes 160

commit v2 on v0

v2 whole, which is shorter than its diff:
```python
import math

import jax
import jax.numpy as jnp
from jax import lax
from jax.experimental import pallas as pl
from jax.experimental.pallas import tpu as pltpu
from jax.sharding import PartitionSpec as P


HIGH = lax.Precision.HIGHEST
SIDE = 16
PAIRS = [(i, i ^ 1) for i in range(SIDE)]
ODD_PAIRS = [(i, i + 1) for i in range(1, SIDE - 1, 2)] + [(i + 1, i) for i in range(1, SIDE - 1, 2)]
PAD = 16
TALL = 256 + 2 * PAD
WIDE = 384
VMEM = pl.BlockSpec(memory_space=pltpu.VMEM)
HBM = pl.BlockSpec(memory_space=pltpu.HBM)
F32 = jnp.float32


def like(*shape, dtype=F32):
    return jax.ShapeDtypeStruct(shape, dtype)


def params(limit=48):
    return pltpu.CompilerParams(vmem_limit_bytes=limit * 1024 * 1024)


def cost(flops, nbytes=1 << 16):
    return pl.CostEstimate(flops=flops, bytes_accessed=nbytes, transcendentals=0)


def swap(x, axis, bits):
    return lax.ppermute(x, axis, [(i, i ^ bits) for i in range(SIDE)])


def row_phase(rows, times, first, quarter):
    freq = first + 4 * (rows // 8) + rows % 4
    return (freq * times + quarter) & 255


def turn(phase):
    return jnp.cos(phase.astype(F32) * (2.0 * math.pi / 256))


def spectrum_kernel(chunks, kern_hbm, coef_ref, cell_ref, mine_ref, other_ref, data, last, low_hot, sems):
    wide = 4096 // chunks
    copies = []
    for n in range(chunks):
        part = pl.ds(n * wide, wide)
        copies.append(pltpu.make_async_copy(kern_hbm.at[:, :, :, part], data.at[n], sems.at[n]))
        copies[-1].start()
    even = lax.axis_index("cols") % 2 == 0
    first = lax.axis_index("rows") * 16

    rows = lax.broadcasted_iota(jnp.int32, (32, 128), 0)
    lanes = lax.broadcasted_iota(jnp.int32, (32, 128), 1)
    part_of = (rows // 4) % 2
    by_re = turn(row_phase(rows, lanes, first, 64 * part_of))
    by_im = turn(row_phase(rows, lanes, first, 64 * part_of - 64))
    coef = jnp.concatenate([coef_ref[...]] * 4, axis=0)
    contract = (((1,), (1,)), ((), ()))
    own = (lanes // 32) == (rows % 4)
    from_re = jnp.where(own, lax.dot_general(by_re, coef, contract, precision=HIGH, preferred_element_type=F32), 0.0)
    from_im = jnp.where(own, lax.dot_general(by_im, coef, contract, precision=HIGH, preferred_element_type=F32), 0.0)
    weights = jnp.concatenate([from_re, from_im], axis=1)
    weights = [weights[8 * g : 8 * g + 8].astype(jnp.bfloat16) for g in range(4)]

    cells = cell_ref[...]
    low_of, high_of = cells & 127, cells >> 7
    low_rows = lax.broadcasted_iota(jnp.int32, (128, 512), 0)
    for n in range(8):
        part = slice(n * 512, n * 512 + 512)
        low_hot[:, part] = jnp.where(low_of[:, part] == low_rows, 1.0, 0.0).astype(jnp.bfloat16)

    at_row = lax.broadcasted_iota(jnp.int32, (32, 1), 0)
    pair = [turn(row_phase(at_row, t, first, 64 * ((at_row // 4) % 2))) * (1.0 / 256) for t in (126, 127)]
    for n in range(chunks):
        copies[n].wait()
        got = []
        for g in range(4):
            rhs = jnp.concatenate(
                [data[n, p, 4 * g : 4 * g + 4].reshape(128, wide) for p in range(2)], axis=0
            )
            got.append(jnp.dot(weights[g], rhs, preferred_element_type=F32))
        value = jnp.concatenate(got, axis=0)
        for k in range(2):
            last[k : k + 1, n * wide : n * wide + wide] = jnp.sum(value * pair[k], axis=0, keepdims=True)
        for m in range(wide // 512):
            k = n * (wide // 512) + m
            for half in range(2):
                at = m * 512 + half * 128
                one, two = value[:, at : at + 128], value[:, at + 256 : at + 384]
                mine_ref[k, half * 32 : half * 32 + 32, :] = jnp.where(even, one, two)
                other_ref[k, half * 32 : half * 32 + 32, :] = jnp.where(even, two, one)

    high_rows = lax.broadcasted_iota(jnp.int32, (32, 512), 0)
    placed = jnp.zeros((128, 128), F32)
    for n in range(8):
        part = slice(n * 512, n * 512 + 512)
        here = high_of[:, part] == high_rows
        spread = []
        for k in range(2):
            value = last[k : k + 1, part]
            coarse = value.astype(jnp.bfloat16).astype(F32)
            for piece in (coarse, value - coarse):
                spread.append(jnp.where(here, piece, 0.0).astype(jnp.bfloat16))
        placed = placed + lax.dot_general(
            jnp.concatenate(spread, axis=0), low_hot[:, part], contract, preferred_element_type=F32
        )
    early = placed[0:32] + placed[32:64]
    late = placed[64:96] + placed[96:128]
    index = lax.broadcasted_iota(jnp.int32, (32, 128), 0)
    before = jnp.where(index == 0, 0.0, pltpu.roll(early, 1, 0))
    after = jnp.where(index == 30, 0.0, pltpu.roll(early, 30, 0))
    zeros = jnp.zeros((2, 128), F32)
    for k in range(8):
        tiles = []
        for c in range(2):
            j = 4 * k + 2 * c
            tiles.append(
                jnp.concatenate(
                    [early[j : j + 2], late[j : j + 2], before[j : j + 1], after[j : j + 1], zeros], axis=0
                )
            )
        mine_ref[k, 64:72, :] = jnp.where(even, tiles[0], tiles[1])
        other_ref[k, 64:72, :] = jnp.where(even, tiles[1], tiles[0])


def spectrum(kernel_hat, coefficients, boundary_cell):
    chunks = 8
    wide = 4096 // chunks

    def kernel(*refs):
        spectrum_kernel(chunks, *refs)

    return pl.pallas_call(
        kernel,
        out_shape=(like(8, 72, 128), like(8, 72, 128)),
        in_specs=[HBM, VMEM, VMEM],
        out_specs=(VMEM, VMEM),
        scratch_shapes=[
            pltpu.VMEM((chunks, 2, 16, 32, wide), jnp.bfloat16),
            pltpu.VMEM((8, 4096), F32),
            pltpu.VMEM((128, 4096), jnp.bfloat16),
            pltpu.SemaphoreType.DMA((chunks,)),
        ],
        compiler_params=params(),
        cost_estimate=cost(1 << 28, 8 << 20),
        name="spectrum",
    )(kernel_hat, coefficients.T, boundary_cell.reshape(1, -1))


def after_core_kernel(mine, got, keep, one, two, three):
    y = lax.axis_index("cols") // 4
    for out, bits in ((keep, 0), (one, 1), (two, 2), (three, 3)):
        at = pl.ds(2 * (y ^ bits), 2)
        out[...] = mine[at] + got[at]


def after_y_kernel(keep, one, two, three, mine, other):
    total = [keep[i] + one[i] + two[i] + three[i] for i in range(2)]
    low = (lax.axis_index("cols") // 2) % 2 == 0
    mine[...] = jnp.where(low, total[0], total[1])
    other[...] = jnp.where(low, total[1], total[0])


def after_z_kernel(mine, got, sent):
    first = lax.axis_index("rows") * 16
    times = lax.broadcasted_iota(jnp.int32, (128, 32), 0)
    at_row = lax.broadcasted_iota(jnp.int32, (128, 32), 1)
    table = turn(row_phase(at_row, times, first, 64 * ((at_row // 4) % 2))) * (1.0 / 256)
    block = mine[...] + got[...]
    spec = jnp.concatenate([block[:32], block[32:64]], axis=1)
    value = jnp.dot(table, spec, precision=HIGH, preferred_element_type=F32)
    for n in range(SIDE):
        sent[n, :, :256] = value[8 * n : 8 * n + 8]
        sent[n, :, 256:] = block[64:]


def whole(kernel, outs, flops, *args, scratch=()):
    return pl.pallas_call(
        kernel,
        out_shape=outs,
        in_specs=[VMEM] * len(args),
        out_specs=jax.tree.map(lambda _: VMEM, outs),
        scratch_shapes=scratch,
        compiler_params=params(),
        cost_estimate=cost(flops),
    )(*args)


def edge_rows_kernel(h, x, y, s, w, pair, other):
    even = lax.axis_index("rows") % 2 == 0
    pair[...] = jnp.zeros_like(pair)
    other[...] = jnp.zeros_like(other)
    for f, ref in enumerate((h, x, y, s, w)):
        head, tail = ref[0:2, :].astype(F32), ref[254:256, :].astype(F32)
        pair[2 * f : 2 * f + 2, :] = jnp.where(even, tail, head)
        other[2 * f : 2 * f + 2, :] = jnp.where(even, head, tail)


def sides(axis, pair, other):
    even = lax.axis_index(axis) % 2 == 0
    return jnp.where(even, other, pair), jnp.where(even, pair, other)


def edge_cols_kernel(h, x, y, s, w, row_pair, row_other, pair, other, mat):
    above, below = sides("rows", row_pair[...], row_other[...])
    mat[...] = jnp.zeros_like(mat)

    def place(rows, take):
        left_mix, lane = None, None
        for f in range(5):
            value = take(f)
            left = pltpu.roll(value[:, :128], 2 * f, 1) if f else value[:, :128]
            right = pltpu.roll(value[:, 128:], 18 + 2 * f, 1)
            if lane is None:
                lane = lax.broadcasted_iota(jnp.int32, left.shape, 1)
                left_mix = jnp.zeros(left.shape, F32)
            left_mix = jnp.where((lane // 2) == f, left, left_mix)
            left_mix = jnp.where((lane // 2) == 8 + f, right, left_mix)
        mat[rows, :] = left_mix

    for n in range(4):
        part = slice(64 * n, 64 * n + 64)
        place(slice(PAD + 64 * n, PAD + 64 * n + 64), lambda f: (h, x, y, s, w)[f][part, :].astype(F32))
    place(slice(PAD - 2, PAD), lambda f: above[2 * f : 2 * f + 2])
    place(slice(PAD + 256, PAD + 258), lambda f: below[2 * f : 2 * f + 2])
    even = lax.axis_index("cols") % 2 == 0
    for n in range(3):
        part = slice(128 * n, 128 * n + 128)
        flat = mat[part, :].T
        pair[:, part] = jnp.where(even, flat[16:32], flat[:16])
        other[:, part] = jnp.where(even, flat[:16], flat[16:32])


def right_of(v):
    return pltpu.roll(v, WIDE - 1, 1)


def left_of(v):
    return pltpu.roll(v, 1, 1)


def below_of(v):
    return pltpu.roll(v, v.shape[0] - 1, 0)


def above_of(v):
    return pltpu.roll(v, 1, 0)


def fluxes(after, h, q, p, e, c, w):
    opened = 0.5 * (w * after(w))
    damping = 0.5 * opened * (c + after(c))
    mass = opened * (q + after(q)) - damping * (after(h) - h)
    momentum = opened * (e + after(e)) - damping * (after(q) - q)
    shear = -damping * (after(p) - p)
    return mass, momentum, shear


def advance(h, x, y, s, c, w, top, rows):
    e = s * h
    mass_y, momentum_y, shear_y = fluxes(below_of, h, y, x, e, c, w)
    cut = lambda v: v[top : top + rows]
    rise = lambda v: cut(v - above_of(v))
    h, x, y, e, c, w = (cut(v) for v in (h, x, y, e, c, w))
    mass_x, momentum_x, shear_x = fluxes(right_of, h, x, y, e, c, w)
    step = lambda v, a, b: w * (v - 0.25 * ((a - left_of(a)) + rise(b)))
    return step(h, mass_x, mass_y), step(x, momentum_x, shear_y), step(y, shear_x, momentum_y)


def stencil_kernel(h, x, y, s, w, row_pair, row_other, col_pair, col_other, h_out, x_out, y_out, edge, fields, state):
    above, below = sides("rows", row_pair[...], row_other[...])
    left, right = sides("cols", col_pair[...], col_other[...])
    lane = lax.broadcasted_iota(jnp.int32, (WIDE, 128), 1)
    zeros = jnp.zeros((96, 128), F32)
    turned = jnp.concatenate(
        [
            jnp.concatenate([right[:, part], left[:, part], zeros], axis=0).T
            for part in (slice(0, 128), slice(128, 256), slice(256, 384))
        ],
        axis=0,
    )
    none = jnp.zeros((PAD, 256), F32)
    for f, ref in enumerate((h, x, y, s, w)):
        outer = pltpu.roll(turned, (128 - 2 * f) % 128, 1)
        inner = pltpu.roll(turned, 110 - 2 * f, 1)
        strip = jnp.where(lane < 2, outer, jnp.where(lane >= 126, inner, 0.0))[:TALL]
        fields[f, :, 256:] = strip
        fields[f, 0:PAD, :256] = none
        fields[f, PAD + 256 :, :256] = none
        fields[f, PAD - 2 : PAD, :256] = above[2 * f : 2 * f + 2]
        fields[f, PAD + 256 : PAD + 258, :256] = below[2 * f : 2 * f + 2]
        fields[f, PAD : PAD + 256, :256] = ref[...].astype(F32)
    for n in range(3):
        part = slice(96 * n, 96 * n + 96)
        fields[5, part, :] = jnp.sqrt(fields[3, part, :])

    size = 16
    for at in range(8, TALL - 8, size):
        part = slice(at - 8, at + size + 8)
        got = advance(*(fields[f, part, :] for f in (0, 1, 2, 3, 5, 4)), 8, size)
        for f in range(3):
            state[f, at : at + size, :] = got[f]
    for at in range(PAD, PAD + 256, size):
        part = slice(at - 8, at + size + 8)
        got = advance(*(state[f, part, :] for f in range(3)), *(fields[f, part, :] for f in (3, 5, 4)), 8, size)
        for f, out in enumerate((h_out, x_out, y_out)):
            out[at - PAD : at - PAD + size, :] = got[f][:, :256]
            if at == PAD + 256 - size:
                edge[6 + f, 0:8, :] = got[f][8:]
                edge[6 + f, 8:16, :] = jnp.zeros((8, WIDE), F32)
    for n, f in enumerate((0, 1, 2, 3, 5, 4)):
        edge[n] = fields[f, PAD + 248 : PAD + 264, :]


def last_kernel(arrived, edge, h_in, x_in, y_in, series, h_out, x_out, y_out):
    total = arrived[0]
    for n in range(1, SIDE):
        total = total + arrived[n]
    series[...] = total[:, :256]
    ghost = total[:, 256:]
    at_edge = lax.axis_index("rows") == SIDE - 1
    row = lax.broadcasted_iota(jnp.int32, (16, WIDE), 0)
    lane = lax.broadcasted_iota(jnp.int32, (1, 128), 1)
    first = jnp.concatenate(
        [ghost[0:1], ghost[1:2], jnp.where(lane == 0, ghost[5:6], jnp.where(lane == 127, ghost[4:5], 0.0))], axis=1
    )
    second = jnp.concatenate([ghost[2:3], ghost[3:4], jnp.zeros((1, 128), F32)], axis=1)
    beyond = row == 8
    h, x, y, s, c, w = (edge[n] for n in range(6))
    h, s, c, w = (jnp.where(beyond, fill, v) for v, fill in ((h, first), (s, 1.0), (c, 1.0), (w, 1.0)))
    x, y = (jnp.where(beyond, 0.0, v) for v in (x, y))
    h, x, y = advance(h, x, y, s, c, w, 0, 16)
    h, x, y = jnp.where(beyond, second, h), jnp.where(beyond, 0.0, x), jnp.where(beyond, 0.0, y)
    got = advance(h, x, y, s, c, w, 0, 16)
    redo = jnp.logical_and(at_edge, row[:8, :256] >= 6)
    for f, out in enumerate((h_out, x_out, y_out)):
        out[...] = jnp.where(redo, got[f][:8, :256], edge[6 + f, :8, :256])


def last_step(arrived, edge, height, flux_x, flux_y):
    grid_field = like(256, 256)
    row_block = pl.BlockSpec((8, 256), lambda i: (31, 0))
    return pl.pallas_call(
        last_kernel,
        grid=(1,),
        out_shape=(like(8, 256), grid_field, grid_field, grid_field),
        in_specs=[VMEM, VMEM, HBM, HBM, HBM],
        out_specs=(pl.BlockSpec((8, 256), lambda i: (0, 0)), row_block, row_block, row_block),
        input_output_aliases={2: 1, 3: 2, 4: 3},
        compiler_params=params(),
        cost_estimate=cost(1 << 20),
        name="last",
    )(arrived, edge, height, flux_x, flux_y)


def forecast(
    kernel_hat, coefficients, wave_speed_sq, wet_mask, boundary_cell, height, flux_x, flux_y
):
    fields = (height, flux_x, flux_y, wave_speed_sq, wet_mask)
    mine, other = spectrum(kernel_hat, coefficients, boundary_cell)
    got = swap(other, "cols", 1)
    slab = like(2, 72, 128)
    keep, one, two, three = whole(after_core_kernel, (slab,) * 4, 1 << 17, mine, got)
    got = [swap(v, "cols", bits) for v, bits in ((two, 8), (one, 4), (three, 12))]

    message = like(16, 256)
    pair, another = whole(edge_rows_kernel, (message, message), 1 << 14, *fields)
    row_pair = lax.ppermute(pair, "rows", PAIRS)
    row_other = lax.ppermute(another, "rows", ODD_PAIRS)

    slab = like(72, 128)
    mine, other = whole(after_y_kernel, (slab, slab), 1 << 17, keep, got[1], got[0], got[2])
    got = swap(other, "cols", 2)

    message = like(16, WIDE)
    scratch = [pltpu.VMEM((WIDE, 128), F32)]
    pair, another = whole(edge_cols_kernel, (message, message), 1 << 20, *fields, row_pair, row_other, scratch=scratch)
    col_pair = lax.ppermute(pair, "cols", PAIRS)
    col_other = lax.ppermute(another, "cols", ODD_PAIRS)

    sent = whole(after_z_kernel, like(SIDE, 8, WIDE), 1 << 22, mine, got)
    arrived = lax.all_to_all(sent, "rows", 0, 0, tiled=True)

    grid_field = like(256, 256)
    outs = (grid_field, grid_field, grid_field, like(9, 16, WIDE))
    scratch = [pltpu.VMEM((6, TALL, WIDE), F32), pltpu.VMEM((3, TALL, WIDE), F32)]
    halos = (row_pair, row_other, col_pair, col_other)
    *bulk, edge = whole(stencil_kernel, outs, 1 << 24, *fields, *halos, scratch=scratch)
    return last_step(arrived, edge, *bulk)


def solution(mesh):
    return jax.shard_map(
        forecast,
        mesh=mesh,
        in_specs=(
            P(None, "rows", "cols", None),
            P(None, "cols"),
            P("rows", "cols"),
            P("rows", "cols"),
            P(),
            P("rows", "cols"),
            P("rows", "cols"),
            P("rows", "cols"),
        ),
        out_specs=(P("rows", "cols"), P("rows", "cols"), P("rows", "cols"), P("rows", "cols")),
        check_vma=False,
    )
```

time: 174 us -> 62.7 us (0.36)
  the two profiles are of different devices: /device:TPU:8 before, /device:TPU:33 now
where the time goes in v2:
time: 62.7 us; the launch traced here: 62.3 us
  starting transfers between devices  33.5 us (53%)
  waiting for transfers between devices  14.1 us (22%)
  Pallas kernels  12.4 us (20%)
  local copies, waits for them, and re-layouts  1.54 us (2%)
  between operations  0.79 us (1%)
    ppermute x5, starting transfers between devices, swap(): return lax.ppermute(x, axis, [(i, i ^ bits) for i in range(SIDE)])  10.9 us
    ppermute x5, waiting for transfers between devices, swap(): return lax.ppermute(x, axis, [(i, i ^ bits) for i in range(SIDE)])  7.45 us
    all_to_all x1, starting transfers between devices, forecast(): arrived = lax.all_to_all(sent, 'rows', 0, 0, tiled=True)  7.38 us
    pallas_call x6, Pallas kernels, whole(): pl.pallas_call(kernel, out_shape=outs, in_specs=[VMEM] * len(args), out_s...  6.8 us
    ppermute x1, starting transfers between devices, forecast(): col_other = lax.ppermute(another, 'cols', ODD_PAIRS)  6.02 us
    pallas_call x1, Pallas kernels, spectrum(): pl.pallas_call(kernel, out_shape=(like(8, 72, 128), like(8, 72, 128)), in...  4.65 us
    ppermute x1, starting transfers between devices, forecast(): col_pair = lax.ppermute(pair, 'cols', PAIRS)  4.25 us
    ppermute x1, starting transfers between devices, forecast(): row_other = lax.ppermute(another, 'rows', ODD_PAIRS)  3.68 us
  transfers between devices with their start and end apart: 10, of which 6 were waited for; matrix products, arithmetic and copies ran while one was open for 0% of the time, Pallas kernels for 9%

profile of v2, /device:TPU:33, one launch (start us, length us, event | category | flops | bytes accessed | tf_op | source)
XLA Modules:
  0.0 62.3 jit_solution(4206807706950986310)
XLA Ops:
  0.6 0.0 copy-start.2
  0.6 0.0 copy-start.1
  0.7 0.0 copy-start
  0.7 0.0 copy-start.4
  0.7 0.0 copy-start.3
  0.7 0.0 copy-start.5
  0.7 0.8 %copy-done.5 = f32[128,32]{0,1:T(8,128)S(1)} copy-done((f32[128,32]{0,1:T(8,128)S(1)}, f32[128,32]{0,1:T(8,128)}, u32[]{:S(2)}) %copy-start.5) | copy-done | bytes 16408
  1.5 0.0 copy-start.6
  1.5 0.7 %copy-done.6 = s32[4096]{0:T(1024)S(1)} copy-done((s32[4096]{0:T(1024)S(1)}, s32[4096]{0:T(1024)}, u32[]{:S(2)}) %copy-start.6) | copy-done | bytes 16408
  2.2 4.7 %spectrum.1 = (f32[8,72,128]{2,1,0:T(8,128)S(1)}, f32[8,72,128]{2,1,0:T(8,128)S(1)}) custom-call(bf16[2,16,32,4096]{3,2,1,0:T(8,128)(2,1)} %refs_0_.1, f32[32,128]{1,0:T(8,128)S(1)} %bitcast.2, s32[1,4096]{1,0:T(1,128)S(1)} %bitcast.3), custom_call_target="tpu_custom_call" | custom-call | flops 268435456 | bytes 8388608 | tf_op jit(solution)/shard_map/spectrum/pallas_call | solution.py:139
  6.9 0.8 %collective-permute-start = (f32[8,72,128]{2,1,0:T(8,128)S(1)}, f32[8,72,128]{2,1,0:T(8,128)S(1)}, u32[]{:S(2)}, u32[]{:S(2)}) collective-permute-start(f32[8,72,128]{2,1,0:T(8,128)S(1)} %get-tuple-element.21), channel_id=1, source_target_pairs={{0,1},{1,0},{2,3},{3,2},{4,5},{5,4},{6,7},{7,6},{8,9},{9,8},{10,11... | collective-permute-start | bytes 884744 | tf_op jit(solution)/shard_map/ppermute | solution.py:36
  7.6 1.2 %collective-permute-done.got = f32[8,72,128]{2,1,0:T(8,128)S(1)} collective-permute-done((f32[8,72,128]{2,1,0:T(8,128)S(1)}, f32[8,72,128]{2,1,0:T(8,128)S(1)}, u32[]{:S(2)}, u32[]{:S(2)}) %collective-permute-start) | collective-permute-done | bytes 294944 | tf_op jit(solution)/shard_map/ppermute | solution.py:36
  8.9 1.4 %collective-permute-start.1 = (f32[2,72,128]{2,1,0:T(8,128)S(1)}, f32[2,72,128]{2,1,0:T(8,128)S(1)}, u32[]{:S(2)}, u32[]{:S(2)}) collective-permute-start(f32[2,72,128]{2,1,0:T(8,128)S(1)} %get-tuple-element.23), channel_id=1, source_target_pairs={{0,4},{1,5},{2,6},{3,7},{4,0},{5,1},{6,2},{7,3},{8,12},{9,13},{10,... | collective-permute-start | bytes 221192 | tf_op jit(solution)/shard_map/ppermute | solution.py:36
  10.3 2.6 %collective-permute-start.2 = (f32[2,72,128]{2,1,0:T(8,128)S(1)}, f32[2,72,128]{2,1,0:T(8,128)S(1)}, u32[]{:S(2)}, u32[]{:S(2)}) collective-permute-start(f32[2,72,128]{2,1,0:T(8,128)S(1)} %get-tuple-element.24), channel_id=1, source_target_pairs={{0,8},{1,9},{2,10},{3,11},{4,12},{5,13},{6,14},{7,15},{8,0},{9,1},... | collective-permute-start | bytes 221192 | tf_op jit(solution)/shard_map/ppermute | solution.py:36
  12.9 0.0 collective-permute-start.3
  12.9 0.0 collective-permute-done.1.one
  12.9 3.3 %collective-permute-done.2.two = f32[2,72,128]{2,1,0:T(8,128)S(1)} collective-permute-done((f32[2,72,128]{2,1,0:T(8,128)S(1)}, f32[2,72,128]{2,1,0:T(8,128)S(1)}, u32[]{:S(2)}, u32[]{:S(2)}) %collective-permute-start.2) | collective-permute-done | bytes 73760 | tf_op jit(solution)/shard_map/ppermute | solution.py:36
  16.2 1.6 %collective-permute-done.3.three = f32[2,72,128]{2,1,0:T(8,128)S(1)} collective-permute-done((f32[2,72,128]{2,1,0:T(8,128)S(1)}, f32[2,72,128]{2,1,0:T(8,128)S(1)}, u32[]{:S(2)}, u32[]{:S(2)}) %collective-permute-start.3) | collective-permute-done | bytes 73760 | tf_op jit(solution)/shard_map/ppermute | solution.py:36
  17.8 6.1 %collective-permute-start.4 = (f32[72,128]{1,0:T(8,128)S(1)}, f32[72,128]{1,0:T(8,128)S(1)}, u32[]{:S(2)}, u32[]{:S(2)}) collective-permute-start(f32[72,128]{1,0:T(8,128)S(1)} %get-tuple-element.27), channel_id=1, source_target_pairs={{0,2},{1,3},{2,0},{3,1},{4,6},{5,7},{6,4},{7,5},{8,10},{9,11},{10,... | collective-permute-start | bytes 110600 | tf_op jit(solution)/shard_map/ppermute | solution.py:36
  23.9 1.3 %collective-permute-done.4.got = f32[72,128]{1,0:T(8,128)S(1)} collective-permute-done((f32[72,128]{1,0:T(8,128)S(1)}, f32[72,128]{1,0:T(8,128)S(1)}, u32[]{:S(2)}, u32[]{:S(2)}) %collective-permute-start.4) | collective-permute-done | bytes 36896 | tf_op jit(solution)/shard_map/ppermute | solution.py:36
  25.3 1.2 %shard_map.113 = f32[16,8,384]{2,1,0:T(8,128)} custom-call(f32[72,128]{1,0:T(8,128)S(1)} %get-tuple-element.26.mine, f32[72,128]{1,0:T(8,128)S(1)} %collective-permute-done.4.got), custom_call_target="tpu_custom_call" | custom-call | flops 4194304 | bytes 65536 | tf_op jit(solution)/shard_map/pallas_call | solution.py:184
  26.4 7.4 %all-to-all-start = ((f32[16,8,384]{2,1,0:T(8,128)}), f32[16,8,384]{2,1,0:T(8,128)S(1)}, u32[]{:S(2)}, u32[]{:S(2)}) async-start(f32[16,8,384]{2,1,0:T(8,128)} %shard_map.113), calls=%async_computation | async-start | bytes 393216 | tf_op jit(solution)/shard_map/all_to_all | solution.py:388
  33.8 0.0 copy-done.2
  33.8 0.0 copy-done.1
  33.8 0.0 copy-done
  33.8 0.0 copy-done.4
  33.8 0.0 copy-done.3
  33.9 1.3 %collective-permute-start.5 = (f32[16,256]{1,0:T(8,128)S(1)}, f32[16,256]{1,0:T(8,128)S(1)}, u32[]{:S(2)}, u32[]{:S(2)}) collective-permute-start(f32[16,256]{1,0:T(8,128)S(1)} %get-tuple-element.28), channel_id=1, source_target_pairs={{0,16},{16,0},{32,48},{48,32},{64,80},{80,64},{96,112},{112,96},{1... | collective-permute-start | bytes 49160 | tf_op jit(solution)/shard_map/ppermute | solution.py:374
  35.1 3.7 %collective-permute-start.6 = (f32[16,256]{1,0:T(8,128)S(1)}, f32[16,256]{1,0:T(8,128)S(1)}, u32[]{:S(2)}, u32[]{:S(2)}) collective-permute-start(f32[16,256]{1,0:T(8,128)S(1)} %get-tuple-element.29), channel_id=1, source_target_pairs={{16,32},{48,64},{80,96},{112,128},{144,160},{176,192},{208,224},{3... | collective-permute-start | bytes 49160 | tf_op jit(solution)/shard_map/ppermute | solution.py:375
  38.8 0.0 collective-permute-done.5.row_pair
  38.8 3.3 %collective-permute-done.6.row_other = f32[16,256]{1,0:T(8,128)S(1)} collective-permute-done((f32[16,256]{1,0:T(8,128)S(1)}, f32[16,256]{1,0:T(8,128)S(1)}, u32[]{:S(2)}, u32[]{:S(2)}) %collective-permute-start.6) | collective-permute-done | bytes 16416 | tf_op jit(solution)/shard_map/ppermute | solution.py:375
  42.2 0.5 shard_map.115
  42.7 4.3 %collective-permute-start.7 = (f32[16,384]{1,0:T(8,128)S(1)}, f32[16,384]{1,0:T(8,128)S(1)}, u32[]{:S(2)}, u32[]{:S(2)}) collective-permute-start(f32[16,384]{1,0:T(8,128)S(1)} %get-tuple-element.30), channel_id=1, source_target_pairs={{0,1},{1,0},{2,3},{3,2},{4,5},{5,4},{6,7},{7,6},{8,9},{9,8},{10,11... | collective-permute-start | bytes 73736 | tf_op jit(solution)/shard_map/ppermute | solution.py:384
  46.9 6.0 %collective-permute-start.8 = (f32[16,384]{1,0:T(8,128)S(1)}, f32[16,384]{1,0:T(8,128)S(1)}, u32[]{:S(2)}, u32[]{:S(2)}) collective-permute-start(f32[16,384]{1,0:T(8,128)S(1)} %get-tuple-element.31), channel_id=1, source_target_pairs={{1,2},{3,4},{5,6},{7,8},{9,10},{11,12},{13,14},{2,1},{4,3},{6,5},{... | collective-permute-start | bytes 73736 | tf_op jit(solution)/shard_map/ppermute | solution.py:385
  52.9 0.0 collective-permute-done.7.col_pair
  53.0 3.3 %collective-permute-done.8.col_other = f32[16,384]{1,0:T(8,128)S(1)} collective-permute-done((f32[16,384]{1,0:T(8,128)S(1)}, f32[16,384]{1,0:T(8,128)S(1)}, u32[]{:S(2)}, u32[]{:S(2)}) %collective-permute-start.8) | collective-permute-done | bytes 24608 | tf_op jit(solution)/shard_map/ppermute | solution.py:385
  56.3 5.1 %shard_map.116 = (f32[256,256]{1,0:T(8,128)}, f32[256,256]{1,0:T(8,128)}, f32[256,256]{1,0:T(8,128)}, f32[9,16,384]{2,1,0:T(8,128)S(1)}) custom-call(f32[256,256]{1,0:T(8,128)S(1)} %copy-done, f32[256,256]{1,0:T(8,128)S(1)} %copy-done.1, f32[256,256]{1,0:T(8,128)S(1)} %copy-done.2, f32[256,256]{1,0:T(8,128)S(1)} %copy-done.3, s32[256,256]{1,0:T(8,128)S(1)} %copy-done.4, ...), custom_call_target="tpu_custom_call" | custom-call | flops 16777216 | bytes 65536 | tf_op jit(solution)/shard_map/pallas_call | solution.py:184
  61.4 0.0 all-to-all-done.arrived
  61.4 0.9 %last.1 = (f32[8,256]{1,0:T(8,128)}, f32[256,256]{1,0:T(8,128)}, f32[256,256]{1,0:T(8,128)}, f32[256,256]{1,0:T(8,128)}) custom-call(f32[16,8,384]{2,1,0:T(8,128)S(1)} %all-to-all-done.arrived, f32[9,16,384]{2,1,0:T(8,128)S(1)} %get-tuple-element.32.edge, ...), custom_call_target="tpu_custom_call", output_to_operand_aliasing={{1}: (2, {}), {2}: (3, {}), {3}: (4, {})} | custom-call | flops 1048576 | bytes 65536 | tf_op jit(solution)/shard_map/last/pallas_call | solution.py:349
  (3 shorter events, 0.1 us)
Async XLA Ops:
  0.6 33.2 %copy-start.2 = (f32[256,256]{1,0:T(8,128)S(1)}, f32[256,256]{1,0:T(8,128)}, u32[]{:S(2)}) copy-start(f32[256,256]{1,0:T(8,128)} %y.5) | copy-start | bytes 786436
  0.6 33.2 %copy-start.1 = (f32[256,256]{1,0:T(8,128)S(1)}, f32[256,256]{1,0:T(8,128)}, u32[]{:S(2)}) copy-start(f32[256,256]{1,0:T(8,128)} %x.5) | copy-start | bytes 786436
  0.7 33.2 %copy-start = (f32[256,256]{1,0:T(8,128)S(1)}, f32[256,256]{1,0:T(8,128)}, u32[]{:S(2)}) copy-start(f32[256,256]{1,0:T(8,128)} %h.5) | copy-start | bytes 786436
  0.7 33.2 %copy-start.4 = (s32[256,256]{1,0:T(8,128)S(1)}, s32[256,256]{1,0:T(8,128)}, u32[]{:S(2)}) copy-start(s32[256,256]{1,0:T(8,128)} %w.5) | copy-start | bytes 786436
  0.7 33.2 %copy-start.3 = (f32[256,256]{1,0:T(8,128)S(1)}, f32[256,256]{1,0:T(8,128)}, u32[]{:S(2)}) copy-start(f32[256,256]{1,0:T(8,128)} %s.5) | copy-start | bytes 786436
  0.7 0.8 %copy-start.5 = (f32[128,32]{0,1:T(8,128)S(1)}, f32[128,32]{0,1:T(8,128)}, u32[]{:S(2)}) copy-start(f32[128,32]{0,1:T(8,128)} %param.9) | copy-start | bytes 49156
  1.5 0.7 %copy-start.6 = (s32[4096]{0:T(1024)S(1)}, s32[4096]{0:T(1024)}, u32[]{:S(2)}) copy-start(s32[4096]{0:T(1024)} %param.12) | copy-start | bytes 49156
  6.9 2.0 %collective-permute-start = (f32[8,72,128]{2,1,0:T(8,128)S(1)}, f32[8,72,128]{2,1,0:T(8,128)S(1)}, u32[]{:S(2)}, u32[]{:S(2)}) collective-permute-start(f32[8,72,128]{2,1,0:T(8,128)S(1)} %get-tuple-element.21), channel_id=1, source_target_pairs={{0,1},{1,0},{2,3},{3,2},{4,5},{5,4},{6,7},{7,6},{8,9},{9,8},{10,11... | collective-permute-start | bytes 884744 | tf_op jit(solution)/shard_map/ppermute | solution.py:36
  8.9 4.0 %collective-permute-start.1 = (f32[2,72,128]{2,1,0:T(8,128)S(1)}, f32[2,72,128]{2,1,0:T(8,128)S(1)}, u32[]{:S(2)}, u32[]{:S(2)}) collective-permute-start(f32[2,72,128]{2,1,0:T(8,128)S(1)} %get-tuple-element.23), channel_id=1, source_target_pairs={{0,4},{1,5},{2,6},{3,7},{4,0},{5,1},{6,2},{7,3},{8,12},{9,13},{10,... | collective-permute-start | bytes 221192 | tf_op jit(solution)/shard_map/ppermute | solution.py:36
  10.3 5.9 %collective-permute-start.2 = (f32[2,72,128]{2,1,0:T(8,128)S(1)}, f32[2,72,128]{2,1,0:T(8,128)S(1)}, u32[]{:S(2)}, u32[]{:S(2)}) collective-permute-start(f32[2,72,128]{2,1,0:T(8,128)S(1)} %get-tuple-element.24), channel_id=1, source_target_pairs={{0,8},{1,9},{2,10},{3,11},{4,12},{5,13},{6,14},{7,15},{8,0},{9,1},... | collective-permute-start | bytes 221192 | tf_op jit(solution)/shard_map/ppermute | solution.py:36
  12.9 4.9 %collective-permute-start.3 = (f32[2,72,128]{2,1,0:T(8,128)S(1)}, f32[2,72,128]{2,1,0:T(8,128)S(1)}, u32[]{:S(2)}, u32[]{:S(2)}) collective-permute-start(f32[2,72,128]{2,1,0:T(8,128)S(1)} %get-tuple-element.25), channel_id=1, source_target_pairs={{0,12},{1,13},{2,14},{3,15},{4,8},{5,9},{6,10},{7,11},{8,4},{9,5},... | collective-permute-start | bytes 221192 | tf_op jit(solution)/shard_map/ppermute | solution.py:36
  17.8 7.4 %collective-permute-start.4 = (f32[72,128]{1,0:T(8,128)S(1)}, f32[72,128]{1,0:T(8,128)S(1)}, u32[]{:S(2)}, u32[]{:S(2)}) collective-permute-start(f32[72,128]{1,0:T(8,128)S(1)} %get-tuple-element.27), channel_id=1, source_target_pairs={{0,2},{1,3},{2,0},{3,1},{4,6},{5,7},{6,4},{7,5},{8,10},{9,11},{10,... | collective-permute-start | bytes 110600 | tf_op jit(solution)/shard_map/ppermute | solution.py:36
  26.4 35.0 %all-to-all-start = ((f32[16,8,384]{2,1,0:T(8,128)}), f32[16,8,384]{2,1,0:T(8,128)S(1)}, u32[]{:S(2)}, u32[]{:S(2)}) async-start(f32[16,8,384]{2,1,0:T(8,128)} %shard_map.113), calls=%async_computation | async-start | bytes 393216 | tf_op jit(solution)/shard_map/all_to_all | solution.py:388
  33.9 5.0 %collective-permute-start.5 = (f32[16,256]{1,0:T(8,128)S(1)}, f32[16,256]{1,0:T(8,128)S(1)}, u32[]{:S(2)}, u32[]{:S(2)}) collective-permute-start(f32[16,256]{1,0:T(8,128)S(1)} %get-tuple-element.28), channel_id=1, source_target_pairs={{0,16},{16,0},{32,48},{48,32},{64,80},{80,64},{96,112},{112,96},{1... | collective-permute-start | bytes 49160 | tf_op jit(solution)/shard_map/ppermute | solution.py:374
  35.1 7.0 %collective-permute-start.6 = (f32[16,256]{1,0:T(8,128)S(1)}, f32[16,256]{1,0:T(8,128)S(1)}, u32[]{:S(2)}, u32[]{:S(2)}) collective-permute-start(f32[16,256]{1,0:T(8,128)S(1)} %get-tuple-element.29), channel_id=1, source_target_pairs={{16,32},{48,64},{80,96},{112,128},{144,160},{176,192},{208,224},{3... | collective-permute-start | bytes 49160 | tf_op jit(solution)/shard_map/ppermute | solution.py:375
  42.7 10.3 %collective-permute-start.7 = (f32[16,384]{1,0:T(8,128)S(1)}, f32[16,384]{1,0:T(8,128)S(1)}, u32[]{:S(2)}, u32[]{:S(2)}) collective-permute-start(f32[16,384]{1,0:T(8,128)S(1)} %get-tuple-element.30), channel_id=1, source_target_pairs={{0,1},{1,0},{2,3},{3,2},{4,5},{5,4},{6,7},{7,6},{8,9},{9,8},{10,11... | collective-permute-start | bytes 73736 | tf_op jit(solution)/shard_map/ppermute | solution.py:384
  46.9 9.3 %collective-permute-start.8 = (f32[16,384]{1,0:T(8,128)S(1)}, f32[16,384]{1,0:T(8,128)S(1)}, u32[]{:S(2)}, u32[]{:S(2)}) collective-permute-start(f32[16,384]{1,0:T(8,128)S(1)} %get-tuple-element.31), channel_id=1, source_target_pairs={{1,2},{3,4},{5,6},{7,8},{9,10},{11,12},{13,14},{2,1},{4,3},{6,5},{... | collective-permute-start | bytes 73736 | tf_op jit(solution)/shard_map/ppermute | solution.py:385

commit v3 on v2

--- a/solution.py
+++ b/solution.py
@@ -12,6 +12,7 @@
 SIDE = 16
 PAIRS = [(i, i ^ 1) for i in range(SIDE)]
 ODD_PAIRS = [(i, i + 1) for i in range(1, SIDE - 1, 2)] + [(i + 1, i) for i in range(1, SIDE - 1, 2)]
+TIME_OWNERS = [10] + [i for i in range(SIDE) if i != 10]
 PAD = 16
 TALL = 256 + 2 * PAD
 WIDE = 384
@@ -24,8 +25,8 @@
     return jax.ShapeDtypeStruct(shape, dtype)
 
 
-def params(limit=48):
-    return pltpu.CompilerParams(vmem_limit_bytes=limit * 1024 * 1024)
+def params(limit=48 * 1024 * 1024):
+    return pltpu.CompilerParams(vmem_limit_bytes=limit)
 
 
 def cost(flops, nbytes=1 << 16):
@@ -45,9 +46,17 @@
     return jnp.cos(phase.astype(F32) * (2.0 * math.pi / 256))
 
 
-def spectrum_kernel(chunks, kern_hbm, coef_ref, cell_ref, mine_ref, other_ref, data, last, low_hot, sems):
+def spectrum_kernel(
+    chunks, kern_hbm, coef_hbm, cell_hbm, mine_ref, other_ref, data, coef_ref, cell_ref, last, low_hot, sems
+):
     wide = 4096 // chunks
     copies = []
+    small = [
+        pltpu.make_async_copy(coef_hbm, coef_ref, sems.at[chunks]),
+        pltpu.make_async_copy(cell_hbm, cell_ref, sems.at[chunks + 1]),
+    ]
+    for copy in small:
+        copy.start()
     for n in range(chunks):
         part = pl.ds(n * wide, wide)
         copies.append(pltpu.make_async_copy(kern_hbm.at[:, :, :, part], data.at[n], sems.at[n]))
@@ -60,6 +69,8 @@
     part_of = (rows // 4) % 2
     by_re = turn(row_phase(rows, lanes, first, 64 * part_of))
     by_im = turn(row_phase(rows, lanes, first, 64 * part_of - 64))
+    for copy in small:
+        copy.wait()
     coef = jnp.concatenate([coef_ref[...]] * 4, axis=0)
     contract = (((1,), (1,)), ((), ()))
     own = (lanes // 32) == (rows % 4)
@@ -139,18 +150,20 @@
     return pl.pallas_call(
         kernel,
         out_shape=(like(8, 72, 128), like(8, 72, 128)),
-        in_specs=[HBM, VMEM, VMEM],
+        in_specs=[HBM, HBM, HBM],
         out_specs=(VMEM, VMEM),
         scratch_shapes=[
             pltpu.VMEM((chunks, 2, 16, 32, wide), jnp.bfloat16),
+            pltpu.VMEM((32, 128), F32),
+            pltpu.VMEM((1, 4096), jnp.int32),
             pltpu.VMEM((8, 4096), F32),
             pltpu.VMEM((128, 4096), jnp.bfloat16),
-            pltpu.SemaphoreType.DMA((chunks,)),
+            pltpu.SemaphoreType.DMA((chunks + 2,)),
         ],
         compiler_params=params(),
         cost_estimate=cost(1 << 28, 8 << 20),
         name="spectrum",
-    )(kernel_hat, coefficients.T, boundary_cell.reshape(1, -1))
+    )(kernel_hat, *(pltpu.with_memory_space_constraint(v, pltpu.HBM) for v in (coefficients.T, boundary_cell.reshape(1, -1))))
 
 
 def after_core_kernel(mine, got, keep, one, two, three):
@@ -167,16 +180,18 @@
     other[...] = jnp.where(low, total[1], total[0])
 
 
-def after_z_kernel(mine, got, sent):
-    first = lax.axis_index("rows") * 16
-    times = lax.broadcasted_iota(jnp.int32, (128, 32), 0)
-    at_row = lax.broadcasted_iota(jnp.int32, (128, 32), 1)
-    table = turn(row_phase(at_row, times, first, 64 * ((at_row // 4) % 2))) * (1.0 / 256)
+def halves(v):
+    coarse = v.astype(jnp.bfloat16).astype(F32)
+    return coarse, v - coarse
+
+
+def after_z_kernel(mine, got, table, sent):
     block = mine[...] + got[...]
-    spec = jnp.concatenate([block[:32], block[32:64]], axis=1)
-    value = jnp.dot(table, spec, precision=HIGH, preferred_element_type=F32)
-    for n in range(SIDE):
-        sent[n, :, :256] = value[8 * n : 8 * n + 8]
+    coarse, fine = halves(jnp.concatenate([block[:32], block[32:64]], axis=1))
+    spec = jnp.concatenate([coarse, fine, coarse, jnp.zeros_like(fine)], axis=0)
+    value = jnp.dot(table[...], spec.astype(jnp.bfloat16), preferred_element_type=F32)
+    for n, to in enumerate(TIME_OWNERS):
+        sent[n, :, :256] = value[8 * to : 8 * to + 8]
         sent[n, :, 256:] = block[64:]
 
 
@@ -192,49 +207,52 @@
     )(*args)
 
 
-def edge_rows_kernel(h, x, y, s, w, pair, other):
-    even = lax.axis_index("rows") % 2 == 0
-    pair[...] = jnp.zeros_like(pair)
-    other[...] = jnp.zeros_like(other)
-    for f, ref in enumerate((h, x, y, s, w)):
-        head, tail = ref[0:2, :].astype(F32), ref[254:256, :].astype(F32)
-        pair[2 * f : 2 * f + 2, :] = jnp.where(even, tail, head)
-        other[2 * f : 2 * f + 2, :] = jnp.where(even, head, tail)
-
-
-def sides(axis, pair, other):
-    even = lax.axis_index(axis) % 2 == 0
-    return jnp.where(even, other, pair), jnp.where(even, pair, other)
-
-
-def edge_cols_kernel(h, x, y, s, w, row_pair, row_other, pair, other, mat):
-    above, below = sides("rows", row_pair[...], row_other[...])
-    mat[...] = jnp.zeros_like(mat)
-
-    def place(rows, take):
-        left_mix, lane = None, None
-        for f in range(5):
-            value = take(f)
-            left = pltpu.roll(value[:, :128], 2 * f, 1) if f else value[:, :128]
-            right = pltpu.roll(value[:, 128:], 18 + 2 * f, 1)
-            if lane is None:
-                lane = lax.broadcasted_iota(jnp.int32, left.shape, 1)
-                left_mix = jnp.zeros(left.shape, F32)
-            left_mix = jnp.where((lane // 2) == f, left, left_mix)
-            left_mix = jnp.where((lane // 2) == 8 + f, right, left_mix)
-        mat[rows, :] = left_mix
-
+def edge_cols_kernel(h, x, y, s, w, pair, other, mat):
+    lane = lax.broadcasted_iota(jnp.int32, (64, 128), 1) // 2
     for n in range(4):
         part = slice(64 * n, 64 * n + 64)
-        place(slice(PAD + 64 * n, PAD + 64 * n + 64), lambda f: (h, x, y, s, w)[f][part, :].astype(F32))
-    place(slice(PAD - 2, PAD), lambda f: above[2 * f : 2 * f + 2])
-    place(slice(PAD + 256, PAD + 258), lambda f: below[2 * f : 2 * f + 2])
+        mix = jnp.zeros((64, 128), F32)
+        for f, ref in enumerate((h, x, y, s, w)):
+            value = ref[part, :].astype(F32)
+            first = pltpu.roll(value[:, :128], 2 * f, 1) if f else value[:, :128]
+            mix = jnp.where(lane == f, first, mix)
+            mix = jnp.where(lane == 8 + f, pltpu.roll(value[:, 128:], 18 + 2 * f, 1), mix)
+        mat[part, :] = mix
     even = lax.axis_index("cols") % 2 == 0
-    for n in range(3):
+    for n in range(2):
         part = slice(128 * n, 128 * n + 128)
         flat = mat[part, :].T
         pair[:, part] = jnp.where(even, flat[16:32], flat[:16])
         other[:, part] = jnp.where(even, flat[:16], flat[16:32])
+
+
+def sides(axis, pair, other):
+    even = lax.axis_index(axis) % 2 == 0
+    return jnp.where(even, other, pair), jnp.where(even, pair, other)
+
+
+def edge_rows_kernel(h, x, y, s, w, col_pair, col_other, pair, other, table):
+    left, right = sides("cols", col_pair[...], col_other[...])
+    even = lax.axis_index("rows") % 2 == 0
+    lane = lax.broadcasted_iota(jnp.int32, (1, 128), 1)
+    none = jnp.zeros((1, 128), F32)
+    pair[...] = jnp.zeros_like(pair)
+    other[...] = jnp.zeros_like(other)
+    for f, ref in enumerate((h, x, y, s, w)):
+        ends = []
+        for at, row in ((0, 0), (254, 255)):
+            corner = jnp.where(lane == 0, right[2 * f : 2 * f + 1, row : row + 1], 0.0)
+            corner = jnp.where(lane == 127, left[2 * f + 1 : 2 * f + 2, row : row + 1], corner)
+            corner = jnp.concatenate([none, corner] if row else [corner, none], axis=0)
+            ends.append(jnp.concatenate([ref[at : at + 2, :].astype(F32), corner], axis=1))
+        pair[2 * f : 2 * f + 2, :] = jnp.where(even, ends[1], ends[0])
+        other[2 * f : 2 * f + 2, :] = jnp.where(even, ends[0], ends[1])
+    times = lax.broadcasted_iota(jnp.int32, (128, 128), 0)
+    lanes = lax.broadcasted_iota(jnp.int32, (128, 128), 1)
+    at_row = lanes % 32
+    phase = row_phase(at_row, times, lax.axis_index("rows") * 16, 64 * ((at_row // 4) % 2))
+    coarse, fine = halves(turn(phase) * (1.0 / 256))
+    table[...] = jnp.where(lanes < 64, coarse, jnp.where(lanes < 96, fine, 0.0)).astype(jnp.bfloat16)
 
 
 def right_of(v):
@@ -276,26 +294,25 @@
 def stencil_kernel(h, x, y, s, w, row_pair, row_other, col_pair, col_other, h_out, x_out, y_out, edge, fields, state):
     above, below = sides("rows", row_pair[...], row_other[...])
     left, right = sides("cols", col_pair[...], col_other[...])
-    lane = lax.broadcasted_iota(jnp.int32, (WIDE, 128), 1)
+    lane = lax.broadcasted_iota(jnp.int32, (256, 128), 1)
     zeros = jnp.zeros((96, 128), F32)
     turned = jnp.concatenate(
         [
             jnp.concatenate([right[:, part], left[:, part], zeros], axis=0).T
-            for part in (slice(0, 128), slice(128, 256), slice(256, 384))
+            for part in (slice(0, 128), slice(128, 256))
         ],
         axis=0,
     )
-    none = jnp.zeros((PAD, 256), F32)
+    none = jnp.zeros((PAD, WIDE), F32)
     for f, ref in enumerate((h, x, y, s, w)):
         outer = pltpu.roll(turned, (128 - 2 * f) % 128, 1)
         inner = pltpu.roll(turned, 110 - 2 * f, 1)
-        strip = jnp.where(lane < 2, outer, jnp.where(lane >= 126, inner, 0.0))[:TALL]
-        fields[f, :, 256:] = strip
-        fields[f, 0:PAD, :256] = none
-        fields[f, PAD + 256 :, :256] = none
-        fields[f, PAD - 2 : PAD, :256] = above[2 * f : 2 * f + 2]
-        fields[f, PAD + 256 : PAD + 258, :256] = below[2 * f : 2 * f + 2]
+        fields[f, 0:PAD, :] = none
+        fields[f, PAD + 256 :, :] = none
+        fields[f, PAD - 2 : PAD, :] = above[2 * f : 2 * f + 2]
+        fields[f, PAD + 256 : PAD + 258, :] = below[2 * f : 2 * f + 2]
         fields[f, PAD : PAD + 256, :256] = ref[...].astype(F32)
+        fields[f, PAD : PAD + 256, 256:] = jnp.where(lane < 2, outer, jnp.where(lane >= 126, inner, 0.0))
     for n in range(3):
         part = slice(96 * n, 96 * n + 96)
         fields[5, part, :] = jnp.sqrt(fields[3, part, :])
@@ -365,27 +382,29 @@
     fields = (height, flux_x, flux_y, wave_speed_sq, wet_mask)
     mine, other = spectrum(kernel_hat, coefficients, boundary_cell)
     got = swap(other, "cols", 1)
+
+    message = like(16, 256)
+    scratch = [pltpu.VMEM((256, 128), F32)]
+    pair, another = whole(edge_cols_kernel, (message, message), 1 << 20, *fields, scratch=scratch)
+    col_pair = lax.ppermute(pair, "cols", PAIRS)
+    col_other = lax.ppermute(another, "cols", ODD_PAIRS)
+
     slab = like(2, 72, 128)
     keep, one, two, three = whole(after_core_kernel, (slab,) * 4, 1 << 17, mine, got)
     got = [swap(v, "cols", bits) for v, bits in ((two, 8), (one, 4), (three, 12))]
 
-    message = like(16, 256)
-    pair, another = whole(edge_rows_kernel, (message, message), 1 << 14, *fields)
-    row_pair = lax.ppermute(pair, "rows", PAIRS)
-    row_other = lax.ppermute(another, "rows", ODD_PAIRS)
-
     slab = like(72, 128)
     mine, other = whole(after_y_kernel, (slab, slab), 1 << 17, keep, got[1], got[0], got[2])
     got = swap(other, "cols", 2)
 
     message = like(16, WIDE)
-    scratch = [pltpu.VMEM((WIDE, 128), F32)]
-    pair, another = whole(edge_cols_kernel, (message, message), 1 << 20, *fields, row_pair, row_other, scratch=scratch)
-    col_pair = lax.ppermute(pair, "cols", PAIRS)
-    col_other = lax.ppermute(another, "cols", ODD_PAIRS)
-
-    sent = whole(after_z_kernel, like(SIDE, 8, WIDE), 1 << 22, mine, got)
-    arrived = lax.all_to_all(sent, "rows", 0, 0, tiled=True)
+    outs = (message, message, like(128, 128, dtype=jnp.bfloat16))
+    pair, another, table = whole(edge_rows_kernel, outs, 1 << 18, *fields, col_pair, col_other)
+    row_pair = lax.ppermute(pair, "rows", PAIRS)
+    row_other = lax.ppermute(another, "rows", ODD_PAIRS)
+
+    sent = whole(after_z_kernel, like(SIDE, 8, WIDE), 1 << 22, mine, got, table)
+    arrived = lax.all_to_all(sent, "rows", 0, 0, axis_index_groups=[TIME_OWNERS], tiled=True)
 
     grid_field = like(256, 256)
     outs = (grid_field, grid_field, grid_field, like(9, 16, WIDE))

time: 62.7 us -> 54.1 us (0.86)
  starting transfers between devices: 33.5 us -> 24.6 us
  waiting for transfers between devices: 14.1 us -> 16.5 us
  local copies, waits for them, and re-layouts: 1.54 us -> 0.02 us
    ppermute x1, starting transfers between devices: 6.02 us -> 1.91 us  [forecast(): col_other = lax.ppermute(another, 'cols', ODD_PAIRS)]
    ppermute x1, waiting for transfers between devices: 3.31 us -> 7.03 us  [forecast(): col_other = lax.ppermute(another, 'cols', ODD_PAIRS)]
    ppermute x1, starting transfers between devices: 4.25 us -> 1.95 us  [forecast(): col_pair = lax.ppermute(pair, 'cols', PAIRS)]
    unnamed x14 -> x10, local copies, waits for them, and re-layouts: 1.54 us -> 0.02 us
    ppermute x5, waiting for transfers between devices: 7.45 us -> 6.1 us  [swap(): return lax.ppermute(x, axis, [(i, i ^ bits) for i in range(SIDE)])]
    ppermute x1, starting transfers between devices: 1.27 us -> 0.01 us  [forecast(): row_pair = lax.ppermute(pair, 'rows', PAIRS)]
    all_to_all x1, starting transfers between devices: 7.38 us -> 6.53 us  [forecast(): lax.all_to_all(sent, 'rows', 0, 0, axis_index_groups=[TIME_OWNERS], tiled...]
  transfers between devices with their start and end apart: 10 -> 10, of which waited for: 6 -> 5; matrix products, arithmetic and copies ran while one was open for 0% -> 0% of each run, Pallas kernels for 9% -> 11%
where the time goes in v3:
time: 54.1 us; the launch traced here: 53.9 us
  starting transfers between devices  24.6 us (45%)
  waiting for transfers between devices  16.5 us (30%)
  Pallas kernels  12 us (22%)
  between operations  0.76 us (1%)
    ppermute x5, starting transfers between devices, swap(): return lax.ppermute(x, axis, [(i, i ^ bits) for i in range(SIDE)])  10.9 us
    ppermute x1, waiting for transfers between devices, forecast(): col_other = lax.ppermute(another, 'cols', ODD_PAIRS)  7.03 us
    pallas_call x6, Pallas kernels, whole(): pl.pallas_call(kernel, out_shape=outs, in_specs=[VMEM] * len(args), out_s...  6.58 us
    all_to_all x1, starting transfers between devices, forecast(): lax.all_to_all(sent, 'rows', 0, 0, axis_index_groups=[TIME_OWNERS], tiled...  6.53 us
    ppermute x5, waiting for transfers between devices, swap(): return lax.ppermute(x, axis, [(i, i ^ bits) for i in range(SIDE)])  6.1 us
    pallas_call x1, Pallas kernels, spectrum(): pl.pallas_call(kernel, out_shape=(like(8, 72, 128), like(8, 72, 128)), in...  4.52 us
    ppermute x1, starting transfers between devices, forecast(): row_other = lax.ppermute(another, 'rows', ODD_PAIRS)  3.34 us
    ppermute x1, waiting for transfers between devices, forecast(): row_other = lax.ppermute(another, 'rows', ODD_PAIRS)  3.32 us
  transfers between devices with their start and end apart: 10, of which 5 were waited for; matrix products, arithmetic and copies ran while one was open for 0% of the time, Pallas kernels for 11%

profile of v3, /device:TPU:33, one launch (start us, length us, event | category | flops | bytes accessed | tf_op | source)
XLA Modules:
  0.0 53.9 jit_solution(7529058486973789142)
XLA Ops:
  0.6 0.0 copy-start.2
  0.6 0.0 copy-start.1
  0.7 0.0 copy-start
  0.7 0.0 copy-start.4
  0.7 0.0 copy-start.3
  0.7 4.5 %spectrum.1 = (f32[8,72,128]{2,1,0:T(8,128)S(1)}, f32[8,72,128]{2,1,0:T(8,128)S(1)}) custom-call(bf16[2,16,32,4096]{3,2,1,0:T(8,128)(2,1)} %refs_0_.1, f32[32,128]{1,0:T(8,128)} %bitcast.2, s32[1,4096]{1,0:T(1,128)} %bitcast.3), custom_call_target="tpu_custom_call" | custom-call | flops 268435456 | bytes 8388608 | tf_op jit(solution)/shard_map/spectrum/pallas_call | solution.py:150
  5.2 0.8 %collective-permute-start = (f32[8,72,128]{2,1,0:T(8,128)S(1)}, f32[8,72,128]{2,1,0:T(8,128)S(1)}, u32[]{:S(2)}, u32[]{:S(2)}) collective-permute-start(f32[8,72,128]{2,1,0:T(8,128)S(1)} %get-tuple-element.22), channel_id=1, source_target_pairs={{0,1},{1,0},{2,3},{3,2},{4,5},{5,4},{6,7},{7,6},{8,9},{9,8},{10,11... | collective-permute-start | bytes 884744 | tf_op jit(solution)/shard_map/ppermute | solution.py:37
  6.0 1.2 %collective-permute-done.got = f32[8,72,128]{2,1,0:T(8,128)S(1)} collective-permute-done((f32[8,72,128]{2,1,0:T(8,128)S(1)}, f32[8,72,128]{2,1,0:T(8,128)S(1)}, u32[]{:S(2)}, u32[]{:S(2)}) %collective-permute-start) | collective-permute-done | bytes 294944 | tf_op jit(solution)/shard_map/ppermute | solution.py:37
  7.2 1.4 %collective-permute-start.1 = (f32[2,72,128]{2,1,0:T(8,128)S(1)}, f32[2,72,128]{2,1,0:T(8,128)S(1)}, u32[]{:S(2)}, u32[]{:S(2)}) collective-permute-start(f32[2,72,128]{2,1,0:T(8,128)S(1)} %get-tuple-element.24), channel_id=1, source_target_pairs={{0,4},{1,5},{2,6},{3,7},{4,0},{5,1},{6,2},{7,3},{8,12},{9,13},{10,... | collective-permute-start | bytes 221192 | tf_op jit(solution)/shard_map/ppermute | solution.py:37
  8.6 2.6 %collective-permute-start.2 = (f32[2,72,128]{2,1,0:T(8,128)S(1)}, f32[2,72,128]{2,1,0:T(8,128)S(1)}, u32[]{:S(2)}, u32[]{:S(2)}) collective-permute-start(f32[2,72,128]{2,1,0:T(8,128)S(1)} %get-tuple-element.25), channel_id=1, source_target_pairs={{0,8},{1,9},{2,10},{3,11},{4,12},{5,13},{6,14},{7,15},{8,0},{9,1},... | collective-permute-start | bytes 221192 | tf_op jit(solution)/shard_map/ppermute | solution.py:37
  11.2 0.0 collective-permute-start.3
  11.2 0.0 collective-permute-done.1.one
  11.2 3.3 %collective-permute-done.2.two = f32[2,72,128]{2,1,0:T(8,128)S(1)} collective-permute-done((f32[2,72,128]{2,1,0:T(8,128)S(1)}, f32[2,72,128]{2,1,0:T(8,128)S(1)}, u32[]{:S(2)}, u32[]{:S(2)}) %collective-permute-start.2) | collective-permute-done | bytes 73760 | tf_op jit(solution)/shard_map/ppermute | solution.py:37
  14.5 1.6 %collective-permute-done.3.three = f32[2,72,128]{2,1,0:T(8,128)S(1)} collective-permute-done((f32[2,72,128]{2,1,0:T(8,128)S(1)}, f32[2,72,128]{2,1,0:T(8,128)S(1)}, u32[]{:S(2)}, u32[]{:S(2)}) %collective-permute-start.3) | collective-permute-done | bytes 73760 | tf_op jit(solution)/shard_map/ppermute | solution.py:37
  16.1 6.1 %collective-permute-start.4 = (f32[72,128]{1,0:T(8,128)S(1)}, f32[72,128]{1,0:T(8,128)S(1)}, u32[]{:S(2)}, u32[]{:S(2)}) collective-permute-start(f32[72,128]{1,0:T(8,128)S(1)} %get-tuple-element.28), channel_id=1, source_target_pairs={{0,2},{1,3},{2,0},{3,1},{4,6},{5,7},{6,4},{7,5},{8,10},{9,11},{10,... | collective-permute-start | bytes 110600 | tf_op jit(solution)/shard_map/ppermute | solution.py:37
  22.2 0.0 copy-done.2
  22.2 0.0 copy-done.1
  22.2 0.0 copy-done
  22.3 0.0 copy-done.4
  22.3 0.0 copy-done.3
  22.3 0.4 shard_map.113
  22.7 2.0 %collective-permute-start.5 = (f32[16,256]{1,0:T(8,128)S(1)}, f32[16,256]{1,0:T(8,128)S(1)}, u32[]{:S(2)}, u32[]{:S(2)}) collective-permute-start(f32[16,256]{1,0:T(8,128)S(1)} %get-tuple-element.29), channel_id=1, source_target_pairs={{0,1},{1,0},{2,3},{3,2},{4,5},{5,4},{6,7},{7,6},{8,9},{9,8},{10,11... | collective-permute-start | bytes 49160 | tf_op jit(solution)/shard_map/ppermute | solution.py:389
  24.6 1.9 %collective-permute-start.6 = (f32[16,256]{1,0:T(8,128)S(1)}, f32[16,256]{1,0:T(8,128)S(1)}, u32[]{:S(2)}, u32[]{:S(2)}) collective-permute-start(f32[16,256]{1,0:T(8,128)S(1)} %get-tuple-element.30), channel_id=1, source_target_pairs={{1,2},{3,4},{5,6},{7,8},{9,10},{11,12},{13,14},{2,1},{4,3},{6,5},{... | collective-permute-start | bytes 49160 | tf_op jit(solution)/shard_map/ppermute | solution.py:390
  26.5 0.0 collective-permute-done.5.col_pair
  26.5 7.0 %collective-permute-done.6.col_other = f32[16,256]{1,0:T(8,128)S(1)} collective-permute-done((f32[16,256]{1,0:T(8,128)S(1)}, f32[16,256]{1,0:T(8,128)S(1)}, u32[]{:S(2)}, u32[]{:S(2)}) %collective-permute-start.6) | collective-permute-done | bytes 16416 | tf_op jit(solution)/shard_map/ppermute | solution.py:390
  33.6 0.3 shard_map.114
  33.9 0.0 collective-permute-done.4.got
  33.9 0.8 %shard_map.115 = f32[16,8,384]{2,1,0:T(8,128)} custom-call(f32[72,128]{1,0:T(8,128)S(1)} %get-tuple-element.27.mine, f32[72,128]{1,0:T(8,128)S(1)} %collective-permute-done.4.got, bf16[128,128]{1,0:T(8,128)(2,1)S(1)} %get-tuple-element.31.table), custom_call_target="tpu_custom_call" | custom-call | flops 4194304 | bytes 65536 | tf_op jit(solution)/shard_map/pallas_call | solution.py:199
  34.7 6.5 %all-to-all-start = ((f32[16,8,384]{2,1,0:T(8,128)}), f32[16,8,384]{2,1,0:T(8,128)S(1)}, u32[]{:S(2)}, u32[]{:S(2)}) async-start(f32[16,8,384]{2,1,0:T(8,128)} %shard_map.115), calls=%async_computation | async-start | bytes 393216 | tf_op jit(solution)/shard_map/all_to_all | solution.py:407
  41.2 0.0 collective-permute-start.7
  41.2 3.3 %collective-permute-start.8 = (f32[16,384]{1,0:T(8,128)S(1)}, f32[16,384]{1,0:T(8,128)S(1)}, u32[]{:S(2)}, u32[]{:S(2)}) collective-permute-start(f32[16,384]{1,0:T(8,128)S(1)} %get-tuple-element.33), channel_id=1, source_target_pairs={{16,32},{48,64},{80,96},{112,128},{144,160},{176,192},{208,224},{3... | collective-permute-start | bytes 73736 | tf_op jit(solution)/shard_map/ppermute | solution.py:404
  44.6 0.0 collective-permute-done.7.row_pair
  44.6 3.3 %collective-permute-done.8.row_other = f32[16,384]{1,0:T(8,128)S(1)} collective-permute-done((f32[16,384]{1,0:T(8,128)S(1)}, f32[16,384]{1,0:T(8,128)S(1)}, u32[]{:S(2)}, u32[]{:S(2)}) %collective-permute-start.8) | collective-permute-done | bytes 24608 | tf_op jit(solution)/shard_map/ppermute | solution.py:404
  47.9 5.0 %shard_map.116 = (f32[256,256]{1,0:T(8,128)}, f32[256,256]{1,0:T(8,128)}, f32[256,256]{1,0:T(8,128)}, f32[9,16,384]{2,1,0:T(8,128)S(1)}) custom-call(f32[256,256]{1,0:T(8,128)S(1)} %copy-done, f32[256,256]{1,0:T(8,128)S(1)} %copy-done.1, f32[256,256]{1,0:T(8,128)S(1)} %copy-done.2, f32[256,256]{1,0:T(8,128)S(1)} %copy-done.3, s32[256,256]{1,0:T(8,128)S(1)} %copy-done.4, ...), custom_call_target="tpu_custom_call" | custom-call | flops 16777216 | bytes 65536 | tf_op jit(solution)/shard_map/pallas_call | solution.py:199
  52.9 0.0 all-to-all-done.arrived
  52.9 0.9 %last.1 = (f32[8,256]{1,0:T(8,128)}, f32[256,256]{1,0:T(8,128)}, f32[256,256]{1,0:T(8,128)}, f32[256,256]{1,0:T(8,128)}) custom-call(f32[16,8,384]{2,1,0:T(8,128)S(1)} %all-to-all-done.arrived, f32[9,16,384]{2,1,0:T(8,128)S(1)} %get-tuple-element.34.edge, ...), custom_call_target="tpu_custom_call", output_to_operand_aliasing={{1}: (2, {}), {2}: (3, {}), {3}: (4, {})} | custom-call | flops 1048576 | bytes 65536 | tf_op jit(solution)/shard_map/last/pallas_call | solution.py:366
  (2 shorter events, 0.1 us)
Async XLA Ops:
  0.6 21.6 %copy-start.2 = (f32[256,256]{1,0:T(8,128)S(1)}, f32[256,256]{1,0:T(8,128)}, u32[]{:S(2)}) copy-start(f32[256,256]{1,0:T(8,128)} %y.5) | copy-start | bytes 786436
  0.6 21.6 %copy-start.1 = (f32[256,256]{1,0:T(8,128)S(1)}, f32[256,256]{1,0:T(8,128)}, u32[]{:S(2)}) copy-start(f32[256,256]{1,0:T(8,128)} %x.5) | copy-start | bytes 786436
  0.7 21.6 %copy-start = (f32[256,256]{1,0:T(8,128)S(1)}, f32[256,256]{1,0:T(8,128)}, u32[]{:S(2)}) copy-start(f32[256,256]{1,0:T(8,128)} %h.5) | copy-start | bytes 786436
  0.7 21.6 %copy-start.4 = (s32[256,256]{1,0:T(8,128)S(1)}, s32[256,256]{1,0:T(8,128)}, u32[]{:S(2)}) copy-start(s32[256,256]{1,0:T(8,128)} %w.5) | copy-start | bytes 786436
  0.7 21.6 %copy-start.3 = (f32[256,256]{1,0:T(8,128)S(1)}, f32[256,256]{1,0:T(8,128)}, u32[]{:S(2)}) copy-start(f32[256,256]{1,0:T(8,128)} %s.5) | copy-start | bytes 786436
  5.2 2.0 %collective-permute-start = (f32[8,72,128]{2,1,0:T(8,128)S(1)}, f32[8,72,128]{2,1,0:T(8,128)S(1)}, u32[]{:S(2)}, u32[]{:S(2)}) collective-permute-start(f32[8,72,128]{2,1,0:T(8,128)S(1)} %get-tuple-element.22), channel_id=1, source_target_pairs={{0,1},{1,0},{2,3},{3,2},{4,5},{5,4},{6,7},{7,6},{8,9},{9,8},{10,11... | collective-permute-start | bytes 884744 | tf_op jit(solution)/shard_map/ppermute | solution.py:37
  7.2 4.0 %collective-permute-start.1 = (f32[2,72,128]{2,1,0:T(8,128)S(1)}, f32[2,72,128]{2,1,0:T(8,128)S(1)}, u32[]{:S(2)}, u32[]{:S(2)}) collective-permute-start(f32[2,72,128]{2,1,0:T(8,128)S(1)} %get-tuple-element.24), channel_id=1, source_target_pairs={{0,4},{1,5},{2,6},{3,7},{4,0},{5,1},{6,2},{7,3},{8,12},{9,13},{10,... | collective-permute-start | bytes 221192 | tf_op jit(solution)/shard_map/ppermute | solution.py:37
  8.6 5.9 %collective-permute-start.2 = (f32[2,72,128]{2,1,0:T(8,128)S(1)}, f32[2,72,128]{2,1,0:T(8,128)S(1)}, u32[]{:S(2)}, u32[]{:S(2)}) collective-permute-start(f32[2,72,128]{2,1,0:T(8,128)S(1)} %get-tuple-element.25), channel_id=1, source_target_pairs={{0,8},{1,9},{2,10},{3,11},{4,12},{5,13},{6,14},{7,15},{8,0},{9,1},... | collective-permute-start | bytes 221192 | tf_op jit(solution)/shard_map/ppermute | solution.py:37
  11.2 4.9 %collective-permute-start.3 = (f32[2,72,128]{2,1,0:T(8,128)S(1)}, f32[2,72,128]{2,1,0:T(8,128)S(1)}, u32[]{:S(2)}, u32[]{:S(2)}) collective-permute-start(f32[2,72,128]{2,1,0:T(8,128)S(1)} %get-tuple-element.26), channel_id=1, source_target_pairs={{0,12},{1,13},{2,14},{3,15},{4,8},{5,9},{6,10},{7,11},{8,4},{9,5},... | collective-permute-start | bytes 221192 | tf_op jit(solution)/shard_map/ppermute | solution.py:37
  16.1 17.7 %collective-permute-start.4 = (f32[72,128]{1,0:T(8,128)S(1)}, f32[72,128]{1,0:T(8,128)S(1)}, u32[]{:S(2)}, u32[]{:S(2)}) collective-permute-start(f32[72,128]{1,0:T(8,128)S(1)} %get-tuple-element.28), channel_id=1, source_target_pairs={{0,2},{1,3},{2,0},{3,1},{4,6},{5,7},{6,4},{7,5},{8,10},{9,11},{10,... | collective-permute-start | bytes 110600 | tf_op jit(solution)/shard_map/ppermute | solution.py:37
  22.7 3.9 %collective-permute-start.5 = (f32[16,256]{1,0:T(8,128)S(1)}, f32[16,256]{1,0:T(8,128)S(1)}, u32[]{:S(2)}, u32[]{:S(2)}) collective-permute-start(f32[16,256]{1,0:T(8,128)S(1)} %get-tuple-element.29), channel_id=1, source_target_pairs={{0,1},{1,0},{2,3},{3,2},{4,5},{5,4},{6,7},{7,6},{8,9},{9,8},{10,11... | collective-permute-start | bytes 49160 | tf_op jit(solution)/shard_map/ppermute | solution.py:389
  24.6 9.0 %collective-permute-start.6 = (f32[16,256]{1,0:T(8,128)S(1)}, f32[16,256]{1,0:T(8,128)S(1)}, u32[]{:S(2)}, u32[]{:S(2)}) collective-permute-start(f32[16,256]{1,0:T(8,128)S(1)} %get-tuple-element.30), channel_id=1, source_target_pairs={{1,2},{3,4},{5,6},{7,8},{9,10},{11,12},{13,14},{2,1},{4,3},{6,5},{... | collective-permute-start | bytes 49160 | tf_op jit(solution)/shard_map/ppermute | solution.py:390
  34.7 18.2 %all-to-all-start = ((f32[16,8,384]{2,1,0:T(8,128)}), f32[16,8,384]{2,1,0:T(8,128)S(1)}, u32[]{:S(2)}, u32[]{:S(2)}) async-start(f32[16,8,384]{2,1,0:T(8,128)} %shard_map.115), calls=%async_computation | async-start | bytes 393216 | tf_op jit(solution)/shard_map/all_to_all | solution.py:407
  41.2 3.4 %collective-permute-start.7 = (f32[16,384]{1,0:T(8,128)S(1)}, f32[16,384]{1,0:T(8,128)S(1)}, u32[]{:S(2)}, u32[]{:S(2)}) collective-permute-start(f32[16,384]{1,0:T(8,128)S(1)} %get-tuple-element.32), channel_id=1, source_target_pairs={{0,16},{16,0},{32,48},{48,32},{64,80},{80,64},{96,112},{112,96},{1... | collective-permute-start | bytes 73736 | tf_op jit(solution)/shard_map/ppermute | solution.py:403
  41.2 6.7 %collective-permute-start.8 = (f32[16,384]{1,0:T(8,128)S(1)}, f32[16,384]{1,0:T(8,128)S(1)}, u32[]{:S(2)}, u32[]{:S(2)}) collective-permute-start(f32[16,384]{1,0:T(8,128)S(1)} %get-tuple-element.33), channel_id=1, source_target_pairs={{16,32},{48,64},{80,96},{112,128},{144,160},{176,192},{208,224},{3... | collective-permute-start | bytes 73736 | tf_op jit(solution)/shard_map/ppermute | solution.py:404

commit v4 on v3

--- a/solution.py
+++ b/solution.py
@@ -47,7 +47,7 @@
 
 
 def spectrum_kernel(
-    chunks, kern_hbm, coef_hbm, cell_hbm, mine_ref, other_ref, data, coef_ref, cell_ref, last, low_hot, sems
+    chunks, kern_hbm, coef_hbm, cell_hbm, mine_ref, other_ref, data, coef_ref, cell_ref, low_hot, sems
 ):
     wide = 4096 // chunks
     copies = []
@@ -88,6 +88,8 @@
 
     at_row = lax.broadcasted_iota(jnp.int32, (32, 1), 0)
     pair = [turn(row_phase(at_row, t, first, 64 * ((at_row // 4) % 2))) * (1.0 / 256) for t in (126, 127)]
+    high_rows = lax.broadcasted_iota(jnp.int32, (32, wide), 0)
+    placed = jnp.zeros((128, 128), F32)
     for n in range(chunks):
         copies[n].wait()
         got = []
@@ -97,8 +99,15 @@
             )
             got.append(jnp.dot(weights[g], rhs, preferred_element_type=F32))
         value = jnp.concatenate(got, axis=0)
+        part = slice(n * wide, n * wide + wide)
+        here = high_of[:, part] == high_rows
+        spread = []
         for k in range(2):
-            last[k : k + 1, n * wide : n * wide + wide] = jnp.sum(value * pair[k], axis=0, keepdims=True)
+            for piece in halves(jnp.sum(value * pair[k], axis=0, keepdims=True)):
+                spread.append(jnp.where(here, piece, 0.0).astype(jnp.bfloat16))
+        placed = placed + lax.dot_general(
+            jnp.concatenate(spread, axis=0), low_hot[:, part], contract, preferred_element_type=F32
+        )
         for m in range(wide // 512):
             k = n * (wide // 512) + m
             for half in range(2):
@@ -107,20 +116,6 @@
                 mine_ref[k, half * 32 : half * 32 + 32, :] = jnp.where(even, one, two)
                 other_ref[k, half * 32 : half * 32 + 32, :] = jnp.where(even, two, one)
 
-    high_rows = lax.broadcasted_iota(jnp.int32, (32, 512), 0)
-    placed = jnp.zeros((128, 128), F32)
-    for n in range(8):
-        part = slice(n * 512, n * 512 + 512)
-        here = high_of[:, part] == high_rows
-        spread = []
-        for k in range(2):
-            value = last[k : k + 1, part]
-            coarse = value.astype(jnp.bfloat16).astype(F32)
-            for piece in (coarse, value - coarse):
-                spread.append(jnp.where(here, piece, 0.0).astype(jnp.bfloat16))
-        placed = placed + lax.dot_general(
-            jnp.concatenate(spread, axis=0), low_hot[:, part], contract, preferred_element_type=F32
-        )
     early = placed[0:32] + placed[32:64]
     late = placed[64:96] + placed[96:128]
     index = lax.broadcasted_iota(jnp.int32, (32, 128), 0)
@@ -156,7 +151,6 @@
             pltpu.VMEM((chunks, 2, 16, 32, wide), jnp.bfloat16),
             pltpu.VMEM((32, 128), F32),
             pltpu.VMEM((1, 4096), jnp.int32),
-            pltpu.VMEM((8, 4096), F32),
             pltpu.VMEM((128, 4096), jnp.bfloat16),
             pltpu.SemaphoreType.DMA((chunks + 2,)),
         ],
@@ -271,27 +265,30 @@
     return pltpu.roll(v, 1, 0)
 
 
-def fluxes(after, h, q, p, e, c, w):
+def faces(after, c, w):
     opened = 0.5 * (w * after(w))
-    damping = 0.5 * opened * (c + after(c))
+    return opened, 0.5 * opened * (c + after(c))
+
+
+def fluxes(after, opened, damping, h, q, p, e):
     mass = opened * (q + after(q)) - damping * (after(h) - h)
     momentum = opened * (e + after(e)) - damping * (after(q) - q)
-    shear = -damping * (after(p) - p)
+    shear = damping * (p - after(p))
     return mass, momentum, shear
 
 
-def advance(h, x, y, s, c, w, top, rows):
+def advance(h, x, y, s, w, by_x, by_y, top, rows):
     e = s * h
-    mass_y, momentum_y, shear_y = fluxes(below_of, h, y, x, e, c, w)
+    mass_y, momentum_y, shear_y = fluxes(below_of, *by_y, h, y, x, e)
     cut = lambda v: v[top : top + rows]
     rise = lambda v: cut(v - above_of(v))
-    h, x, y, e, c, w = (cut(v) for v in (h, x, y, e, c, w))
-    mass_x, momentum_x, shear_x = fluxes(right_of, h, x, y, e, c, w)
+    h, x, y, e = (cut(v) for v in (h, x, y, e))
+    mass_x, momentum_x, shear_x = fluxes(right_of, *by_x, h, x, y, e)
     step = lambda v, a, b: w * (v - 0.25 * ((a - left_of(a)) + rise(b)))
     return step(h, mass_x, mass_y), step(x, momentum_x, shear_y), step(y, shear_x, momentum_y)
 
 
-def stencil_kernel(h, x, y, s, w, row_pair, row_other, col_pair, col_other, h_out, x_out, y_out, edge, fields, state):
+def stencil_kernel(h, x, y, s, w, row_pair, row_other, col_pair, col_other, h_out, x_out, y_out, edge, fields, state, kept):
     above, below = sides("rows", row_pair[...], row_other[...])
     left, right = sides("cols", col_pair[...], col_other[...])
     lane = lax.broadcasted_iota(jnp.int32, (256, 128), 1)
@@ -317,19 +314,26 @@
         part = slice(96 * n, 96 * n + 96)
         fields[5, part, :] = jnp.sqrt(fields[3, part, :])
 
-    size = 16
+    size = 64
     for at in range(8, TALL - 8, size):
-        part = slice(at - 8, at + size + 8)
-        got = advance(*(fields[f, part, :] for f in (0, 1, 2, 3, 5, 4)), 8, size)
+        rows = min(size, TALL - 8 - at)
+        part, own = slice(at - 8, at + rows + 8), slice(at, at + rows)
+        by_x = faces(right_of, fields[5, own, :], fields[4, own, :])
+        by_y = faces(below_of, fields[5, part, :], fields[4, part, :])
+        got = advance(*(fields[f, part, :] for f in range(4)), fields[4, own, :], by_x, by_y, 8, rows)
         for f in range(3):
-            state[f, at : at + size, :] = got[f]
+            state[f, own, :] = got[f]
+        for f, v in enumerate((*by_x, *(v[8 : 8 + rows] for v in by_y))):
+            kept[f, own, :] = v
     for at in range(PAD, PAD + 256, size):
-        part = slice(at - 8, at + size + 8)
-        got = advance(*(state[f, part, :] for f in range(3)), *(fields[f, part, :] for f in (3, 5, 4)), 8, size)
+        part, own = slice(at - 8, at + size + 8), slice(at, at + size)
+        by_x = (kept[0, own, :], kept[1, own, :])
+        by_y = (kept[2, part, :], kept[3, part, :])
+        got = advance(*(state[f, part, :] for f in range(3)), fields[3, part, :], fields[4, own, :], by_x, by_y, 8, size)
         for f, out in enumerate((h_out, x_out, y_out)):
             out[at - PAD : at - PAD + size, :] = got[f][:, :256]
             if at == PAD + 256 - size:
-                edge[6 + f, 0:8, :] = got[f][8:]
+                edge[6 + f, 0:8, :] = got[f][size - 8 :]
                 edge[6 + f, 8:16, :] = jnp.zeros((8, WIDE), F32)
     for n, f in enumerate((0, 1, 2, 3, 5, 4)):
         edge[n] = fields[f, PAD + 248 : PAD + 264, :]
@@ -352,9 +356,10 @@
     h, x, y, s, c, w = (edge[n] for n in range(6))
     h, s, c, w = (jnp.where(beyond, fill, v) for v, fill in ((h, first), (s, 1.0), (c, 1.0), (w, 1.0)))
     x, y = (jnp.where(beyond, 0.0, v) for v in (x, y))
-    h, x, y = advance(h, x, y, s, c, w, 0, 16)
+    by_x, by_y = faces(right_of, c, w), faces(below_of, c, w)
+    h, x, y = advance(h, x, y, s, w, by_x, by_y, 0, 16)
     h, x, y = jnp.where(beyond, second, h), jnp.where(beyond, 0.0, x), jnp.where(beyond, 0.0, y)
-    got = advance(h, x, y, s, c, w, 0, 16)
+    got = advance(h, x, y, s, w, by_x, by_y, 0, 16)
     redo = jnp.logical_and(at_edge, row[:8, :256] >= 6)
     for f, out in enumerate((h_out, x_out, y_out)):
         out[...] = jnp.where(redo, got[f][:8, :256], edge[6 + f, :8, :256])
@@ -408,7 +413,7 @@
 
     grid_field = like(256, 256)
     outs = (grid_field, grid_field, grid_field, like(9, 16, WIDE))
-    scratch = [pltpu.VMEM((6, TALL, WIDE), F32), pltpu.VMEM((3, TALL, WIDE), F32)]
+    scratch = [pltpu.VMEM((n, TALL, WIDE), F32) for n in (6, 3, 4)]
     halos = (row_pair, row_other, col_pair, col_other)
     *bulk, edge = whole(stencil_kernel, outs, 1 << 24, *fields, *halos, scratch=scratch)
     return last_step(arrived, edge, *bulk)

time: 54.1 us -> 52.6 us (0.972)
  Pallas kernels: 12 us -> 10.5 us
    pallas_call x6, Pallas kernels: 6.58 us -> 5.19 us  [whole(): pl.pallas_call(kernel, out_shape=outs, in_specs=[VMEM] * len(args), out_s...]
  transfers between devices with their start and end apart: 10 -> 10, of which waited for: 5 -> 5; matrix products, arithmetic and copies ran while one was open for 0% -> 0% of each run, Pallas kernels for 11% -> 8%
where the time goes in v4:
time: 52.6 us; the launch traced here: 52.3 us
  starting transfers between devices  24.6 us (47%)
  waiting for transfers between devices  16.5 us (31%)
  Pallas kernels  10.5 us (20%)
  between operations  0.76 us (1%)
    ppermute x5, starting transfers between devices, swap(): return lax.ppermute(x, axis, [(i, i ^ bits) for i in range(SIDE)])  10.9 us
    ppermute x1, waiting for transfers between devices, forecast(): col_other = lax.ppermute(another, 'cols', ODD_PAIRS)  7.03 us
    all_to_all x1, starting transfers between devices, forecast(): lax.all_to_all(sent, 'rows', 0, 0, axis_index_groups=[TIME_OWNERS], tiled...  6.53 us
    ppermute x5, waiting for transfers between devices, swap(): return lax.ppermute(x, axis, [(i, i ^ bits) for i in range(SIDE)])  6.1 us
    pallas_call x6, Pallas kernels, whole(): pl.pallas_call(kernel, out_shape=outs, in_specs=[VMEM] * len(args), out_s...  5.19 us
    pallas_call x1, Pallas kernels, spectrum(): pl.pallas_call(kernel, out_shape=(like(8, 72, 128), like(8, 72, 128)), in...  4.33 us
    ppermute x1, starting transfers between devices, forecast(): row_other = lax.ppermute(another, 'rows', ODD_PAIRS)  3.34 us
    ppermute x1, waiting for transfers between devices, forecast(): row_other = lax.ppermute(another, 'rows', ODD_PAIRS)  3.32 us
  transfers between devices with their start and end apart: 10, of which 5 were waited for; matrix products, arithmetic and copies ran while one was open for 0% of the time, Pallas kernels for 8%

profile of v4, /device:TPU:33, one launch (start us, length us, event | category | flops | bytes accessed | tf_op | source)
XLA Modules:
  0.0 52.3 jit_solution(10168051075328331772)
XLA Ops:
  0.6 0.0 copy-start.2
  0.6 0.0 copy-start.1
  0.7 0.0 copy-start
  0.7 0.0 copy-start.4
  0.7 0.0 copy-start.3
  0.7 4.3 %spectrum.1 = (f32[8,72,128]{2,1,0:T(8,128)S(1)}, f32[8,72,128]{2,1,0:T(8,128)S(1)}) custom-call(bf16[2,16,32,4096]{3,2,1,0:T(8,128)(2,1)} %refs_0_.1, f32[32,128]{1,0:T(8,128)} %bitcast.2, s32[1,4096]{1,0:T(1,128)} %bitcast.3), custom_call_target="tpu_custom_call" | custom-call | flops 268435456 | bytes 8388608 | tf_op jit(solution)/shard_map/spectrum/pallas_call | solution.py:145
  5.0 0.8 %collective-permute-start = (f32[8,72,128]{2,1,0:T(8,128)S(1)}, f32[8,72,128]{2,1,0:T(8,128)S(1)}, u32[]{:S(2)}, u32[]{:S(2)}) collective-permute-start(f32[8,72,128]{2,1,0:T(8,128)S(1)} %get-tuple-element.22), channel_id=1, source_target_pairs={{0,1},{1,0},{2,3},{3,2},{4,5},{5,4},{6,7},{7,6},{8,9},{9,8},{10,11... | collective-permute-start | bytes 884744 | tf_op jit(solution)/shard_map/ppermute | solution.py:37
  5.8 1.2 %collective-permute-done.got = f32[8,72,128]{2,1,0:T(8,128)S(1)} collective-permute-done((f32[8,72,128]{2,1,0:T(8,128)S(1)}, f32[8,72,128]{2,1,0:T(8,128)S(1)}, u32[]{:S(2)}, u32[]{:S(2)}) %collective-permute-start) | collective-permute-done | bytes 294944 | tf_op jit(solution)/shard_map/ppermute | solution.py:37
  7.0 1.4 %collective-permute-start.1 = (f32[2,72,128]{2,1,0:T(8,128)S(1)}, f32[2,72,128]{2,1,0:T(8,128)S(1)}, u32[]{:S(2)}, u32[]{:S(2)}) collective-permute-start(f32[2,72,128]{2,1,0:T(8,128)S(1)} %get-tuple-element.24), channel_id=1, source_target_pairs={{0,4},{1,5},{2,6},{3,7},{4,0},{5,1},{6,2},{7,3},{8,12},{9,13},{10,... | collective-permute-start | bytes 221192 | tf_op jit(solution)/shard_map/ppermute | solution.py:37
  8.4 2.6 %collective-permute-start.2 = (f32[2,72,128]{2,1,0:T(8,128)S(1)}, f32[2,72,128]{2,1,0:T(8,128)S(1)}, u32[]{:S(2)}, u32[]{:S(2)}) collective-permute-start(f32[2,72,128]{2,1,0:T(8,128)S(1)} %get-tuple-element.25), channel_id=1, source_target_pairs={{0,8},{1,9},{2,10},{3,11},{4,12},{5,13},{6,14},{7,15},{8,0},{9,1},... | collective-permute-start | bytes 221192 | tf_op jit(solution)/shard_map/ppermute | solution.py:37
  11.0 0.0 collective-permute-start.3
  11.0 0.0 collective-permute-done.1.one
  11.0 3.3 %collective-permute-done.2.two = f32[2,72,128]{2,1,0:T(8,128)S(1)} collective-permute-done((f32[2,72,128]{2,1,0:T(8,128)S(1)}, f32[2,72,128]{2,1,0:T(8,128)S(1)}, u32[]{:S(2)}, u32[]{:S(2)}) %collective-permute-start.2) | collective-permute-done | bytes 73760 | tf_op jit(solution)/shard_map/ppermute | solution.py:37
  14.3 1.6 %collective-permute-done.3.three = f32[2,72,128]{2,1,0:T(8,128)S(1)} collective-permute-done((f32[2,72,128]{2,1,0:T(8,128)S(1)}, f32[2,72,128]{2,1,0:T(8,128)S(1)}, u32[]{:S(2)}, u32[]{:S(2)}) %collective-permute-start.3) | collective-permute-done | bytes 73760 | tf_op jit(solution)/shard_map/ppermute | solution.py:37
  16.0 6.1 %collective-permute-start.4 = (f32[72,128]{1,0:T(8,128)S(1)}, f32[72,128]{1,0:T(8,128)S(1)}, u32[]{:S(2)}, u32[]{:S(2)}) collective-permute-start(f32[72,128]{1,0:T(8,128)S(1)} %get-tuple-element.28), channel_id=1, source_target_pairs={{0,2},{1,3},{2,0},{3,1},{4,6},{5,7},{6,4},{7,5},{8,10},{9,11},{10,... | collective-permute-start | bytes 110600 | tf_op jit(solution)/shard_map/ppermute | solution.py:37
  22.1 0.0 copy-done.2
  22.1 0.0 copy-done.1
  22.1 0.0 copy-done
  22.1 0.0 copy-done.4
  22.1 0.0 copy-done.3
  22.1 0.4 shard_map.113
  22.5 2.0 %collective-permute-start.5 = (f32[16,256]{1,0:T(8,128)S(1)}, f32[16,256]{1,0:T(8,128)S(1)}, u32[]{:S(2)}, u32[]{:S(2)}) collective-permute-start(f32[16,256]{1,0:T(8,128)S(1)} %get-tuple-element.29), channel_id=1, source_target_pairs={{0,1},{1,0},{2,3},{3,2},{4,5},{5,4},{6,7},{7,6},{8,9},{9,8},{10,11... | collective-permute-start | bytes 49160 | tf_op jit(solution)/shard_map/ppermute | solution.py:394
  24.4 1.9 %collective-permute-start.6 = (f32[16,256]{1,0:T(8,128)S(1)}, f32[16,256]{1,0:T(8,128)S(1)}, u32[]{:S(2)}, u32[]{:S(2)}) collective-permute-start(f32[16,256]{1,0:T(8,128)S(1)} %get-tuple-element.30), channel_id=1, source_target_pairs={{1,2},{3,4},{5,6},{7,8},{9,10},{11,12},{13,14},{2,1},{4,3},{6,5},{... | collective-permute-start | bytes 49160 | tf_op jit(solution)/shard_map/ppermute | solution.py:395
  26.4 0.0 collective-permute-done.5.col_pair
  26.4 7.0 %collective-permute-done.6.col_other = f32[16,256]{1,0:T(8,128)S(1)} collective-permute-done((f32[16,256]{1,0:T(8,128)S(1)}, f32[16,256]{1,0:T(8,128)S(1)}, u32[]{:S(2)}, u32[]{:S(2)}) %collective-permute-start.6) | collective-permute-done | bytes 16416 | tf_op jit(solution)/shard_map/ppermute | solution.py:395
  33.4 0.3 shard_map.114
  33.7 0.0 collective-permute-done.4.got
  33.7 0.8 %shard_map.115 = f32[16,8,384]{2,1,0:T(8,128)} custom-call(f32[72,128]{1,0:T(8,128)S(1)} %get-tuple-element.27.mine, f32[72,128]{1,0:T(8,128)S(1)} %collective-permute-done.4.got, bf16[128,128]{1,0:T(8,128)(2,1)S(1)} %get-tuple-element.31.table), custom_call_target="tpu_custom_call" | custom-call | flops 4194304 | bytes 65536 | tf_op jit(solution)/shard_map/pallas_call | solution.py:193
  34.5 6.5 %all-to-all-start = ((f32[16,8,384]{2,1,0:T(8,128)}), f32[16,8,384]{2,1,0:T(8,128)S(1)}, u32[]{:S(2)}, u32[]{:S(2)}) async-start(f32[16,8,384]{2,1,0:T(8,128)} %shard_map.115), calls=%async_computation | async-start | bytes 393216 | tf_op jit(solution)/shard_map/all_to_all | solution.py:412
  41.0 0.0 collective-permute-start.7
  41.1 3.3 %collective-permute-start.8 = (f32[16,384]{1,0:T(8,128)S(1)}, f32[16,384]{1,0:T(8,128)S(1)}, u32[]{:S(2)}, u32[]{:S(2)}) collective-permute-start(f32[16,384]{1,0:T(8,128)S(1)} %get-tuple-element.33), channel_id=1, source_target_pairs={{16,32},{48,64},{80,96},{112,128},{144,160},{176,192},{208,224},{3... | collective-permute-start | bytes 73736 | tf_op jit(solution)/shard_map/ppermute | solution.py:409
  44.4 0.0 collective-permute-done.7.row_pair
  44.4 3.3 %collective-permute-done.8.row_other = f32[16,384]{1,0:T(8,128)S(1)} collective-permute-done((f32[16,384]{1,0:T(8,128)S(1)}, f32[16,384]{1,0:T(8,128)S(1)}, u32[]{:S(2)}, u32[]{:S(2)}) %collective-permute-start.8) | collective-permute-done | bytes 24608 | tf_op jit(solution)/shard_map/ppermute | solution.py:409
  47.7 3.6 %shard_map.116 = (f32[256,256]{1,0:T(8,128)}, f32[256,256]{1,0:T(8,128)}, f32[256,256]{1,0:T(8,128)}, f32[9,16,384]{2,1,0:T(8,128)S(1)}) custom-call(f32[256,256]{1,0:T(8,128)S(1)} %copy-done, f32[256,256]{1,0:T(8,128)S(1)} %copy-done.1, f32[256,256]{1,0:T(8,128)S(1)} %copy-done.2, f32[256,256]{1,0:T(8,128)S(1)} %copy-done.3, s32[256,256]{1,0:T(8,128)S(1)} %copy-done.4, ...), custom_call_target="tpu_custom_call" | custom-call | flops 16777216 | bytes 65536 | tf_op jit(solution)/shard_map/pallas_call | solution.py:193
  51.4 0.0 all-to-all-done.arrived
  51.4 0.9 %last.1 = (f32[8,256]{1,0:T(8,128)}, f32[256,256]{1,0:T(8,128)}, f32[256,256]{1,0:T(8,128)}, f32[256,256]{1,0:T(8,128)}) custom-call(f32[16,8,384]{2,1,0:T(8,128)S(1)} %all-to-all-done.arrived, f32[9,16,384]{2,1,0:T(8,128)S(1)} %get-tuple-element.34.edge, ...), custom_call_target="tpu_custom_call", output_to_operand_aliasing={{1}: (2, {}), {2}: (3, {}), {3}: (4, {})} | custom-call | flops 1048576 | bytes 65536 | tf_op jit(solution)/shard_map/last/pallas_call | solution.py:371
  (2 shorter events, 0.1 us)
Async XLA Ops:
  0.6 21.4 %copy-start.2 = (f32[256,256]{1,0:T(8,128)S(1)}, f32[256,256]{1,0:T(8,128)}, u32[]{:S(2)}) copy-start(f32[256,256]{1,0:T(8,128)} %y.5) | copy-start | bytes 786436
  0.6 21.4 %copy-start.1 = (f32[256,256]{1,0:T(8,128)S(1)}, f32[256,256]{1,0:T(8,128)}, u32[]{:S(2)}) copy-start(f32[256,256]{1,0:T(8,128)} %x.5) | copy-start | bytes 786436
  0.7 21.4 %copy-start = (f32[256,256]{1,0:T(8,128)S(1)}, f32[256,256]{1,0:T(8,128)}, u32[]{:S(2)}) copy-start(f32[256,256]{1,0:T(8,128)} %h.5) | copy-start | bytes 786436
  0.7 21.4 %copy-start.4 = (s32[256,256]{1,0:T(8,128)S(1)}, s32[256,256]{1,0:T(8,128)}, u32[]{:S(2)}) copy-start(s32[256,256]{1,0:T(8,128)} %w.5) | copy-start | bytes 786436
  0.7 21.4 %copy-start.3 = (f32[256,256]{1,0:T(8,128)S(1)}, f32[256,256]{1,0:T(8,128)}, u32[]{:S(2)}) copy-start(f32[256,256]{1,0:T(8,128)} %s.5) | copy-start | bytes 786436
  5.0 2.0 %collective-permute-start = (f32[8,72,128]{2,1,0:T(8,128)S(1)}, f32[8,72,128]{2,1,0:T(8,128)S(1)}, u32[]{:S(2)}, u32[]{:S(2)}) collective-permute-start(f32[8,72,128]{2,1,0:T(8,128)S(1)} %get-tuple-element.22), channel_id=1, source_target_pairs={{0,1},{1,0},{2,3},{3,2},{4,5},{5,4},{6,7},{7,6},{8,9},{9,8},{10,11... | collective-permute-start | bytes 884744 | tf_op jit(solution)/shard_map/ppermute | solution.py:37
  7.0 4.0 %collective-permute-start.1 = (f32[2,72,128]{2,1,0:T(8,128)S(1)}, f32[2,72,128]{2,1,0:T(8,128)S(1)}, u32[]{:S(2)}, u32[]{:S(2)}) collective-permute-start(f32[2,72,128]{2,1,0:T(8,128)S(1)} %get-tuple-element.24), channel_id=1, source_target_pairs={{0,4},{1,5},{2,6},{3,7},{4,0},{5,1},{6,2},{7,3},{8,12},{9,13},{10,... | collective-permute-start | bytes 221192 | tf_op jit(solution)/shard_map/ppermute | solution.py:37
  8.4 5.9 %collective-permute-start.2 = (f32[2,72,128]{2,1,0:T(8,128)S(1)}, f32[2,72,128]{2,1,0:T(8,128)S(1)}, u32[]{:S(2)}, u32[]{:S(2)}) collective-permute-start(f32[2,72,128]{2,1,0:T(8,128)S(1)} %get-tuple-element.25), channel_id=1, source_target_pairs={{0,8},{1,9},{2,10},{3,11},{4,12},{5,13},{6,14},{7,15},{8,0},{9,1},... | collective-permute-start | bytes 221192 | tf_op jit(solution)/shard_map/ppermute | solution.py:37
  11.0 4.9 %collective-permute-start.3 = (f32[2,72,128]{2,1,0:T(8,128)S(1)}, f32[2,72,128]{2,1,0:T(8,128)S(1)}, u32[]{:S(2)}, u32[]{:S(2)}) collective-permute-start(f32[2,72,128]{2,1,0:T(8,128)S(1)} %get-tuple-element.26), channel_id=1, source_target_pairs={{0,12},{1,13},{2,14},{3,15},{4,8},{5,9},{6,10},{7,11},{8,4},{9,5},... | collective-permute-start | bytes 221192 | tf_op jit(solution)/shard_map/ppermute | solution.py:37
  16.0 17.7 %collective-permute-start.4 = (f32[72,128]{1,0:T(8,128)S(1)}, f32[72,128]{1,0:T(8,128)S(1)}, u32[]{:S(2)}, u32[]{:S(2)}) collective-permute-start(f32[72,128]{1,0:T(8,128)S(1)} %get-tuple-element.28), channel_id=1, source_target_pairs={{0,2},{1,3},{2,0},{3,1},{4,6},{5,7},{6,4},{7,5},{8,10},{9,11},{10,... | collective-permute-start | bytes 110600 | tf_op jit(solution)/shard_map/ppermute | solution.py:37
  22.5 3.9 %collective-permute-start.5 = (f32[16,256]{1,0:T(8,128)S(1)}, f32[16,256]{1,0:T(8,128)S(1)}, u32[]{:S(2)}, u32[]{:S(2)}) collective-permute-start(f32[16,256]{1,0:T(8,128)S(1)} %get-tuple-element.29), channel_id=1, source_target_pairs={{0,1},{1,0},{2,3},{3,2},{4,5},{5,4},{6,7},{7,6},{8,9},{9,8},{10,11... | collective-permute-start | bytes 49160 | tf_op jit(solution)/shard_map/ppermute | solution.py:394
  24.4 9.0 %collective-permute-start.6 = (f32[16,256]{1,0:T(8,128)S(1)}, f32[16,256]{1,0:T(8,128)S(1)}, u32[]{:S(2)}, u32[]{:S(2)}) collective-permute-start(f32[16,256]{1,0:T(8,128)S(1)} %get-tuple-element.30), channel_id=1, source_target_pairs={{1,2},{3,4},{5,6},{7,8},{9,10},{11,12},{13,14},{2,1},{4,3},{6,5},{... | collective-permute-start | bytes 49160 | tf_op jit(solution)/shard_map/ppermute | solution.py:395
  34.5 16.8 %all-to-all-start = ((f32[16,8,384]{2,1,0:T(8,128)}), f32[16,8,384]{2,1,0:T(8,128)S(1)}, u32[]{:S(2)}, u32[]{:S(2)}) async-start(f32[16,8,384]{2,1,0:T(8,128)} %shard_map.115), calls=%async_computation | async-start | bytes 393216 | tf_op jit(solution)/shard_map/all_to_all | solution.py:412
  41.0 3.4 %collective-permute-start.7 = (f32[16,384]{1,0:T(8,128)S(1)}, f32[16,384]{1,0:T(8,128)S(1)}, u32[]{:S(2)}, u32[]{:S(2)}) collective-permute-start(f32[16,384]{1,0:T(8,128)S(1)} %get-tuple-element.32), channel_id=1, source_target_pairs={{0,16},{16,0},{32,48},{48,32},{64,80},{80,64},{96,112},{112,96},{1... | collective-permute-start | bytes 73736 | tf_op jit(solution)/shard_map/ppermute | solution.py:408
  41.1 6.7 %collective-permute-start.8 = (f32[16,384]{1,0:T(8,128)S(1)}, f32[16,384]{1,0:T(8,128)S(1)}, u32[]{:S(2)}, u32[]{:S(2)}) collective-permute-start(f32[16,384]{1,0:T(8,128)S(1)} %get-tuple-element.33), channel_id=1, source_target_pairs={{16,32},{48,64},{80,96},{112,128},{144,160},{176,192},{208,224},{3... | collective-permute-start | bytes 73736 | tf_op jit(solution)/shard_map/ppermute | solution.py:409

commit v5 on v4

--- a/solution.py
+++ b/solution.py
@@ -339,41 +339,47 @@
         edge[n] = fields[f, PAD + 248 : PAD + 264, :]
 
 
-def last_kernel(arrived, edge, h_in, x_in, y_in, series, h_out, x_out, y_out):
+def last_kernel(arrived, edge, h_in, x_in, y_in, series, h_out, x_out, y_out, block, sems):
     total = arrived[0]
     for n in range(1, SIDE):
         total = total + arrived[n]
     series[...] = total[:, :256]
     ghost = total[:, 256:]
-    at_edge = lax.axis_index("rows") == SIDE - 1
-    row = lax.broadcasted_iota(jnp.int32, (16, WIDE), 0)
-    lane = lax.broadcasted_iota(jnp.int32, (1, 128), 1)
-    first = jnp.concatenate(
-        [ghost[0:1], ghost[1:2], jnp.where(lane == 0, ghost[5:6], jnp.where(lane == 127, ghost[4:5], 0.0))], axis=1
-    )
-    second = jnp.concatenate([ghost[2:3], ghost[3:4], jnp.zeros((1, 128), F32)], axis=1)
-    beyond = row == 8
-    h, x, y, s, c, w = (edge[n] for n in range(6))
-    h, s, c, w = (jnp.where(beyond, fill, v) for v, fill in ((h, first), (s, 1.0), (c, 1.0), (w, 1.0)))
-    x, y = (jnp.where(beyond, 0.0, v) for v in (x, y))
-    by_x, by_y = faces(right_of, c, w), faces(below_of, c, w)
-    h, x, y = advance(h, x, y, s, w, by_x, by_y, 0, 16)
-    h, x, y = jnp.where(beyond, second, h), jnp.where(beyond, 0.0, x), jnp.where(beyond, 0.0, y)
-    got = advance(h, x, y, s, w, by_x, by_y, 0, 16)
-    redo = jnp.logical_and(at_edge, row[:8, :256] >= 6)
-    for f, out in enumerate((h_out, x_out, y_out)):
-        out[...] = jnp.where(redo, got[f][:8, :256], edge[6 + f, :8, :256])
+
+    @pl.when(lax.axis_index("rows") == SIDE - 1)
+    def _():
+        row = lax.broadcasted_iota(jnp.int32, (16, WIDE), 0)
+        lane = lax.broadcasted_iota(jnp.int32, (1, 128), 1)
+        first = jnp.concatenate(
+            [ghost[0:1], ghost[1:2], jnp.where(lane == 0, ghost[5:6], jnp.where(lane == 127, ghost[4:5], 0.0))], axis=1
+        )
+        second = jnp.concatenate([ghost[2:3], ghost[3:4], jnp.zeros((1, 128), F32)], axis=1)
+        beyond = row == 8
+        h, x, y, s, c, w = (edge[n] for n in range(6))
+        h, s, c, w = (jnp.where(beyond, fill, v) for v, fill in ((h, first), (s, 1.0), (c, 1.0), (w, 1.0)))
+        x, y = (jnp.where(beyond, 0.0, v) for v in (x, y))
+        by_x, by_y = faces(right_of, c, w), faces(below_of, c, w)
+        h, x, y = advance(h, x, y, s, w, by_x, by_y, 0, 16)
+        h, x, y = jnp.where(beyond, second, h), jnp.where(beyond, 0.0, x), jnp.where(beyond, 0.0, y)
+        got = advance(h, x, y, s, w, by_x, by_y, 0, 16)
+        redo = row[:8, :256] >= 6
+        copies = []
+        for f, out in enumerate((h_out, x_out, y_out)):
+            block[f] = jnp.where(redo, got[f][:8, :256], edge[6 + f, :8, :256])
+            copies.append(pltpu.make_async_copy(block.at[f], out.at[pl.ds(248, 8), :], sems.at[f]))
+            copies[-1].start()
+        for copy in copies:
+            copy.wait()
 
 
 def last_step(arrived, edge, height, flux_x, flux_y):
     grid_field = like(256, 256)
-    row_block = pl.BlockSpec((8, 256), lambda i: (31, 0))
     return pl.pallas_call(
         last_kernel,
-        grid=(1,),
         out_shape=(like(8, 256), grid_field, grid_field, grid_field),
         in_specs=[VMEM, VMEM, HBM, HBM, HBM],
-        out_specs=(pl.BlockSpec((8, 256), lambda i: (0, 0)), row_block, row_block, row_block),
+        out_specs=(VMEM, HBM, HBM, HBM),
+        scratch_shapes=[pltpu.VMEM((3, 8, 256), F32), pltpu.SemaphoreType.DMA((3,))],
         input_output_aliases={2: 1, 3: 2, 4: 3},
         compiler_params=params(),
         cost_estimate=cost(1 << 20),

time: 52.6 us -> 52.3 us (level)
  no operation moved by 1% of the time
where the time goes in v5:
time: 52.3 us; the launch traced here: 52 us
  starting transfers between devices  24.6 us (47%)
  waiting for transfers between devices  16.5 us (32%)
  Pallas kernels  10.2 us (20%)
  between operations  0.76 us (1%)
    ppermute x5, starting transfers between devices, swap(): return lax.ppermute(x, axis, [(i, i ^ bits) for i in range(SIDE)])  10.9 us
    ppermute x1, waiting for transfers between devices, forecast(): col_other = lax.ppermute(another, 'cols', ODD_PAIRS)  7.03 us
    all_to_all x1, starting transfers between devices, forecast(): lax.all_to_all(sent, 'rows', 0, 0, axis_index_groups=[TIME_OWNERS], tiled...  6.53 us
    ppermute x5, waiting for transfers between devices, swap(): return lax.ppermute(x, axis, [(i, i ^ bits) for i in range(SIDE)])  6.1 us
    pallas_call x6, Pallas kernels, whole(): pl.pallas_call(kernel, out_shape=outs, in_specs=[VMEM] * len(args), out_s...  5.19 us
    pallas_call x1, Pallas kernels, spectrum(): pl.pallas_call(kernel, out_shape=(like(8, 72, 128), like(8, 72, 128)), in...  4.33 us
    ppermute x1, starting transfers between devices, forecast(): row_other = lax.ppermute(another, 'rows', ODD_PAIRS)  3.34 us
    ppermute x1, waiting for transfers between devices, forecast(): row_other = lax.ppermute(another, 'rows', ODD_PAIRS)  3.32 us
  transfers between devices with their start and end apart: 10, of which 5 were waited for; matrix products, arithmetic and copies ran while one was open for 0% of the time, Pallas kernels for 8%

profile of v5, /device:TPU:33, one launch (start us, length us, event | category | flops | bytes accessed | tf_op | source)
XLA Modules:
  0.0 52.0 jit_solution(12187905808058542262)
XLA Ops:
  0.6 0.0 copy-start.2
  0.6 0.0 copy-start.1
  0.7 0.0 copy-start
  0.7 0.0 copy-start.4
  0.7 0.0 copy-start.3
  0.7 4.3 %spectrum.1 = (f32[8,72,128]{2,1,0:T(8,128)S(1)}, f32[8,72,128]{2,1,0:T(8,128)S(1)}) custom-call(bf16[2,16,32,4096]{3,2,1,0:T(8,128)(2,1)} %refs_0_.1, f32[32,128]{1,0:T(8,128)} %bitcast.2, s32[1,4096]{1,0:T(1,128)} %bitcast.3), custom_call_target="tpu_custom_call" | custom-call | flops 268435456 | bytes 8388608 | tf_op jit(solution)/shard_map/spectrum/pallas_call | solution.py:145
  5.0 0.8 %collective-permute-start = (f32[8,72,128]{2,1,0:T(8,128)S(1)}, f32[8,72,128]{2,1,0:T(8,128)S(1)}, u32[]{:S(2)}, u32[]{:S(2)}) collective-permute-start(f32[8,72,128]{2,1,0:T(8,128)S(1)} %get-tuple-element.22), channel_id=1, source_target_pairs={{0,1},{1,0},{2,3},{3,2},{4,5},{5,4},{6,7},{7,6},{8,9},{9,8},{10,11... | collective-permute-start | bytes 884744 | tf_op jit(solution)/shard_map/ppermute | solution.py:37
  5.8 1.2 %collective-permute-done.got = f32[8,72,128]{2,1,0:T(8,128)S(1)} collective-permute-done((f32[8,72,128]{2,1,0:T(8,128)S(1)}, f32[8,72,128]{2,1,0:T(8,128)S(1)}, u32[]{:S(2)}, u32[]{:S(2)}) %collective-permute-start) | collective-permute-done | bytes 294944 | tf_op jit(solution)/shard_map/ppermute | solution.py:37
  7.0 1.4 %collective-permute-start.1 = (f32[2,72,128]{2,1,0:T(8,128)S(1)}, f32[2,72,128]{2,1,0:T(8,128)S(1)}, u32[]{:S(2)}, u32[]{:S(2)}) collective-permute-start(f32[2,72,128]{2,1,0:T(8,128)S(1)} %get-tuple-element.24), channel_id=1, source_target_pairs={{0,4},{1,5},{2,6},{3,7},{4,0},{5,1},{6,2},{7,3},{8,12},{9,13},{10,... | collective-permute-start | bytes 221192 | tf_op jit(solution)/shard_map/ppermute | solution.py:37
  8.4 2.6 %collective-permute-start.2 = (f32[2,72,128]{2,1,0:T(8,128)S(1)}, f32[2,72,128]{2,1,0:T(8,128)S(1)}, u32[]{:S(2)}, u32[]{:S(2)}) collective-permute-start(f32[2,72,128]{2,1,0:T(8,128)S(1)} %get-tuple-element.25), channel_id=1, source_target_pairs={{0,8},{1,9},{2,10},{3,11},{4,12},{5,13},{6,14},{7,15},{8,0},{9,1},... | collective-permute-start | bytes 221192 | tf_op jit(solution)/shard_map/ppermute | solution.py:37
  11.0 0.0 collective-permute-start.3
  11.0 0.0 collective-permute-done.1.one
  11.0 3.3 %collective-permute-done.2.two = f32[2,72,128]{2,1,0:T(8,128)S(1)} collective-permute-done((f32[2,72,128]{2,1,0:T(8,128)S(1)}, f32[2,72,128]{2,1,0:T(8,128)S(1)}, u32[]{:S(2)}, u32[]{:S(2)}) %collective-permute-start.2) | collective-permute-done | bytes 73760 | tf_op jit(solution)/shard_map/ppermute | solution.py:37
  14.3 1.6 %collective-permute-done.3.three = f32[2,72,128]{2,1,0:T(8,128)S(1)} collective-permute-done((f32[2,72,128]{2,1,0:T(8,128)S(1)}, f32[2,72,128]{2,1,0:T(8,128)S(1)}, u32[]{:S(2)}, u32[]{:S(2)}) %collective-permute-start.3) | collective-permute-done | bytes 73760 | tf_op jit(solution)/shard_map/ppermute | solution.py:37
  16.0 6.1 %collective-permute-start.4 = (f32[72,128]{1,0:T(8,128)S(1)}, f32[72,128]{1,0:T(8,128)S(1)}, u32[]{:S(2)}, u32[]{:S(2)}) collective-permute-start(f32[72,128]{1,0:T(8,128)S(1)} %get-tuple-element.28), channel_id=1, source_target_pairs={{0,2},{1,3},{2,0},{3,1},{4,6},{5,7},{6,4},{7,5},{8,10},{9,11},{10,... | collective-permute-start | bytes 110600 | tf_op jit(solution)/shard_map/ppermute | solution.py:37
  22.1 0.0 copy-done.2
  22.1 0.0 copy-done.1
  22.1 0.0 copy-done
  22.1 0.0 copy-done.4
  22.1 0.0 copy-done.3
  22.1 0.4 shard_map.113
  22.5 2.0 %collective-permute-start.5 = (f32[16,256]{1,0:T(8,128)S(1)}, f32[16,256]{1,0:T(8,128)S(1)}, u32[]{:S(2)}, u32[]{:S(2)}) collective-permute-start(f32[16,256]{1,0:T(8,128)S(1)} %get-tuple-element.29), channel_id=1, source_target_pairs={{0,1},{1,0},{2,3},{3,2},{4,5},{5,4},{6,7},{7,6},{8,9},{9,8},{10,11... | collective-permute-start | bytes 49160 | tf_op jit(solution)/shard_map/ppermute | solution.py:400
  24.4 1.9 %collective-permute-start.6 = (f32[16,256]{1,0:T(8,128)S(1)}, f32[16,256]{1,0:T(8,128)S(1)}, u32[]{:S(2)}, u32[]{:S(2)}) collective-permute-start(f32[16,256]{1,0:T(8,128)S(1)} %get-tuple-element.30), channel_id=1, source_target_pairs={{1,2},{3,4},{5,6},{7,8},{9,10},{11,12},{13,14},{2,1},{4,3},{6,5},{... | collective-permute-start | bytes 49160 | tf_op jit(solution)/shard_map/ppermute | solution.py:401
  26.4 0.0 collective-permute-done.5.col_pair
  26.4 7.0 %collective-permute-done.6.col_other = f32[16,256]{1,0:T(8,128)S(1)} collective-permute-done((f32[16,256]{1,0:T(8,128)S(1)}, f32[16,256]{1,0:T(8,128)S(1)}, u32[]{:S(2)}, u32[]{:S(2)}) %collective-permute-start.6) | collective-permute-done | bytes 16416 | tf_op jit(solution)/shard_map/ppermute | solution.py:401
  33.4 0.3 shard_map.114
  33.7 0.0 collective-permute-done.4.got
  33.7 0.8 %shard_map.115 = f32[16,8,384]{2,1,0:T(8,128)} custom-call(f32[72,128]{1,0:T(8,128)S(1)} %get-tuple-element.27.mine, f32[72,128]{1,0:T(8,128)S(1)} %collective-permute-done.4.got, bf16[128,128]{1,0:T(8,128)(2,1)S(1)} %get-tuple-element.31.table), custom_call_target="tpu_custom_call" | custom-call | flops 4194304 | bytes 65536 | tf_op jit(solution)/shard_map/pallas_call | solution.py:193
  34.5 6.5 %all-to-all-start = ((f32[16,8,384]{2,1,0:T(8,128)}), f32[16,8,384]{2,1,0:T(8,128)S(1)}, u32[]{:S(2)}, u32[]{:S(2)}) async-start(f32[16,8,384]{2,1,0:T(8,128)} %shard_map.115), calls=%async_computation | async-start | bytes 393216 | tf_op jit(solution)/shard_map/all_to_all | solution.py:418
  41.0 0.0 collective-permute-start.7
  41.1 3.3 %collective-permute-start.8 = (f32[16,384]{1,0:T(8,128)S(1)}, f32[16,384]{1,0:T(8,128)S(1)}, u32[]{:S(2)}, u32[]{:S(2)}) collective-permute-start(f32[16,384]{1,0:T(8,128)S(1)} %get-tuple-element.33), channel_id=1, source_target_pairs={{16,32},{48,64},{80,96},{112,128},{144,160},{176,192},{208,224},{3... | collective-permute-start | bytes 73736 | tf_op jit(solution)/shard_map/ppermute | solution.py:415
  44.4 0.0 collective-permute-done.7.row_pair
  44.4 3.3 %collective-permute-done.8.row_other = f32[16,384]{1,0:T(8,128)S(1)} collective-permute-done((f32[16,384]{1,0:T(8,128)S(1)}, f32[16,384]{1,0:T(8,128)S(1)}, u32[]{:S(2)}, u32[]{:S(2)}) %collective-permute-start.8) | collective-permute-done | bytes 24608 | tf_op jit(solution)/shard_map/ppermute | solution.py:415
  47.7 3.6 %shard_map.116 = (f32[256,256]{1,0:T(8,128)}, f32[256,256]{1,0:T(8,128)}, f32[256,256]{1,0:T(8,128)}, f32[9,16,384]{2,1,0:T(8,128)S(1)}) custom-call(f32[256,256]{1,0:T(8,128)S(1)} %copy-done, f32[256,256]{1,0:T(8,128)S(1)} %copy-done.1, f32[256,256]{1,0:T(8,128)S(1)} %copy-done.2, f32[256,256]{1,0:T(8,128)S(1)} %copy-done.3, s32[256,256]{1,0:T(8,128)S(1)} %copy-done.4, ...), custom_call_target="tpu_custom_call" | custom-call | flops 16777216 | bytes 65536 | tf_op jit(solution)/shard_map/pallas_call | solution.py:193
  51.4 0.0 all-to-all-done.arrived
  51.4 0.6 %last.1 = (f32[8,256]{1,0:T(8,128)}, f32[256,256]{1,0:T(8,128)}, f32[256,256]{1,0:T(8,128)}, f32[256,256]{1,0:T(8,128)}) custom-call(f32[16,8,384]{2,1,0:T(8,128)S(1)} %all-to-all-done.arrived, f32[9,16,384]{2,1,0:T(8,128)S(1)} %get-tuple-element.34.edge, ...), custom_call_target="tpu_custom_call", output_to_operand_aliasing={{1}: (2, {}), {2}: (3, {}), {3}: (4, {})} | custom-call | flops 1048576 | bytes 65536 | tf_op jit(solution)/shard_map/last/pallas_call | solution.py:377
  (2 shorter events, 0.1 us)
Async XLA Ops:
  0.6 21.4 %copy-start.2 = (f32[256,256]{1,0:T(8,128)S(1)}, f32[256,256]{1,0:T(8,128)}, u32[]{:S(2)}) copy-start(f32[256,256]{1,0:T(8,128)} %y.5) | copy-start | bytes 786436
  0.6 21.4 %copy-start.1 = (f32[256,256]{1,0:T(8,128)S(1)}, f32[256,256]{1,0:T(8,128)}, u32[]{:S(2)}) copy-start(f32[256,256]{1,0:T(8,128)} %x.5) | copy-start | bytes 786436
  0.7 21.4 %copy-start = (f32[256,256]{1,0:T(8,128)S(1)}, f32[256,256]{1,0:T(8,128)}, u32[]{:S(2)}) copy-start(f32[256,256]{1,0:T(8,128)} %h.5) | copy-start | bytes 786436
  0.7 21.4 %copy-start.4 = (s32[256,256]{1,0:T(8,128)S(1)}, s32[256,256]{1,0:T(8,128)}, u32[]{:S(2)}) copy-start(s32[256,256]{1,0:T(8,128)} %w.5) | copy-start | bytes 786436
  0.7 21.4 %copy-start.3 = (f32[256,256]{1,0:T(8,128)S(1)}, f32[256,256]{1,0:T(8,128)}, u32[]{:S(2)}) copy-start(f32[256,256]{1,0:T(8,128)} %s.5) | copy-start | bytes 786436
  5.0 2.0 %collective-permute-start = (f32[8,72,128]{2,1,0:T(8,128)S(1)}, f32[8,72,128]{2,1,0:T(8,128)S(1)}, u32[]{:S(2)}, u32[]{:S(2)}) collective-permute-start(f32[8,72,128]{2,1,0:T(8,128)S(1)} %get-tuple-element.22), channel_id=1, source_target_pairs={{0,1},{1,0},{2,3},{3,2},{4,5},{5,4},{6,7},{7,6},{8,9},{9,8},{10,11... | collective-permute-start | bytes 884744 | tf_op jit(solution)/shard_map/ppermute | solution.py:37
  7.0 4.0 %collective-permute-start.1 = (f32[2,72,128]{2,1,0:T(8,128)S(1)}, f32[2,72,128]{2,1,0:T(8,128)S(1)}, u32[]{:S(2)}, u32[]{:S(2)}) collective-permute-start(f32[2,72,128]{2,1,0:T(8,128)S(1)} %get-tuple-element.24), channel_id=1, source_target_pairs={{0,4},{1,5},{2,6},{3,7},{4,0},{5,1},{6,2},{7,3},{8,12},{9,13},{10,... | collective-permute-start | bytes 221192 | tf_op jit(solution)/shard_map/ppermute | solution.py:37
  8.4 5.9 %collective-permute-start.2 = (f32[2,72,128]{2,1,0:T(8,128)S(1)}, f32[2,72,128]{2,1,0:T(8,128)S(1)}, u32[]{:S(2)}, u32[]{:S(2)}) collective-permute-start(f32[2,72,128]{2,1,0:T(8,128)S(1)} %get-tuple-element.25), channel_id=1, source_target_pairs={{0,8},{1,9},{2,10},{3,11},{4,12},{5,13},{6,14},{7,15},{8,0},{9,1},... | collective-permute-start | bytes 221192 | tf_op jit(solution)/shard_map/ppermute | solution.py:37
  11.0 4.9 %collective-permute-start.3 = (f32[2,72,128]{2,1,0:T(8,128)S(1)}, f32[2,72,128]{2,1,0:T(8,128)S(1)}, u32[]{:S(2)}, u32[]{:S(2)}) collective-permute-start(f32[2,72,128]{2,1,0:T(8,128)S(1)} %get-tuple-element.26), channel_id=1, source_target_pairs={{0,12},{1,13},{2,14},{3,15},{4,8},{5,9},{6,10},{7,11},{8,4},{9,5},... | collective-permute-start | bytes 221192 | tf_op jit(solution)/shard_map/ppermute | solution.py:37
  16.0 17.7 %collective-permute-start.4 = (f32[72,128]{1,0:T(8,128)S(1)}, f32[72,128]{1,0:T(8,128)S(1)}, u32[]{:S(2)}, u32[]{:S(2)}) collective-permute-start(f32[72,128]{1,0:T(8,128)S(1)} %get-tuple-element.28), channel_id=1, source_target_pairs={{0,2},{1,3},{2,0},{3,1},{4,6},{5,7},{6,4},{7,5},{8,10},{9,11},{10,... | collective-permute-start | bytes 110600 | tf_op jit(solution)/shard_map/ppermute | solution.py:37
  22.5 3.9 %collective-permute-start.5 = (f32[16,256]{1,0:T(8,128)S(1)}, f32[16,256]{1,0:T(8,128)S(1)}, u32[]{:S(2)}, u32[]{:S(2)}) collective-permute-start(f32[16,256]{1,0:T(8,128)S(1)} %get-tuple-element.29), channel_id=1, source_target_pairs={{0,1},{1,0},{2,3},{3,2},{4,5},{5,4},{6,7},{7,6},{8,9},{9,8},{10,11... | collective-permute-start | bytes 49160 | tf_op jit(solution)/shard_map/ppermute | solution.py:400
  24.4 9.0 %collective-permute-start.6 = (f32[16,256]{1,0:T(8,128)S(1)}, f32[16,256]{1,0:T(8,128)S(1)}, u32[]{:S(2)}, u32[]{:S(2)}) collective-permute-start(f32[16,256]{1,0:T(8,128)S(1)} %get-tuple-element.30), channel_id=1, source_target_pairs={{1,2},{3,4},{5,6},{7,8},{9,10},{11,12},{13,14},{2,1},{4,3},{6,5},{... | collective-permute-start | bytes 49160 | tf_op jit(solution)/shard_map/ppermute | solution.py:401
  34.5 16.8 %all-to-all-start = ((f32[16,8,384]{2,1,0:T(8,128)}), f32[16,8,384]{2,1,0:T(8,128)S(1)}, u32[]{:S(2)}, u32[]{:S(2)}) async-start(f32[16,8,384]{2,1,0:T(8,128)} %shard_map.115), calls=%async_computation | async-start | bytes 393216 | tf_op jit(solution)/shard_map/all_to_all | solution.py:418
  41.0 3.4 %collective-permute-start.7 = (f32[16,384]{1,0:T(8,128)S(1)}, f32[16,384]{1,0:T(8,128)S(1)}, u32[]{:S(2)}, u32[]{:S(2)}) collective-permute-start(f32[16,384]{1,0:T(8,128)S(1)} %get-tuple-element.32), channel_id=1, source_target_pairs={{0,16},{16,0},{32,48},{48,32},{64,80},{80,64},{96,112},{112,96},{1... | collective-permute-start | bytes 73736 | tf_op jit(solution)/shard_map/ppermute | solution.py:414
  41.1 6.7 %collective-permute-start.8 = (f32[16,384]{1,0:T(8,128)S(1)}, f32[16,384]{1,0:T(8,128)S(1)}, u32[]{:S(2)}, u32[]{:S(2)}) collective-permute-start(f32[16,384]{1,0:T(8,128)S(1)} %get-tuple-element.33), channel_id=1, source_target_pairs={{16,32},{48,64},{80,96},{112,128},{144,160},{176,192},{208,224},{3... | collective-permute-start | bytes 73736 | tf_op jit(solution)/shard_map/ppermute | solution.py:415
